TPU v7x, 32 devices: a whole 2x2x4 slice. The times are simulated.
32 devices in a mesh: dp: 8 (over z, y), tensor: 4 (over x, core).
Axes of the slice: x: 2, y: 2, z: 4, core: 2. Of those that a mesh axis runs over, the one named last changes fastest.
Arguments:
- block_input: float32 [16384, 1152], P(('dp', 'tensor'))
- conditioning: float32 [16, 1152], P('dp'), may hold values from -6 to 6
- patch_counts: int32 [16], P('dp'), may hold values from 480 to 1024, as said below
- positions: int32 [16384, 2], P('dp'), may hold values from 0 to 63, as said below
- w_mod: float32 [1152, 6, 1152], P('dp', None, 'tensor'), may hold values from -0.1875 to 0.1875
- b_mod: float32 [6, 1152], P(None, 'tensor'), may hold values from -3 to 3
- w_qkv: float32 [1152, 3, 1152], P('dp', None, 'tensor'), may hold values from -0.1875 to 0.1875
- b_qkv: float32 [3, 1152], P(None, 'tensor'), may hold values from -3 to 3
- w_out: float32 [1152, 1152], P('tensor', 'dp'), may hold values from -3 to 3
- b_out: float32 [1152], replicated, may hold values from -3 to 3
- w_up: float32 [1152, 4608], P('dp', 'tensor'), may hold values from -0.1875 to 0.1875
- b_up: float32 [4608], P('tensor'), may hold values from -3 to 3
- w_down: float32 [4608, 1152], P('tensor', 'dp'), may hold values from -0.09375 to 0.09375
- b_down: float32 [1152], replicated, may hold values from -3 to 3
- cotangent: float32 [16384, 1152], P(('dp', 'tensor')), may hold values from -6 to 6
Outputs:
- block_output: float32 [16384, 1152], P(('dp', 'tensor'))
- grad_input: float32 [16384, 1152], P(('dp', 'tensor'))
- grad_cond: float32 [16, 1152], P('dp')
- grad_wmod: float32 [1152, 6, 1152], P('dp', None, 'tensor')
- grad_bmod: float32 [6, 1152], P(None, 'tensor')
- grad_wqkv: float32 [1152, 3, 1152], P('dp', None, 'tensor')
- grad_bqkv: float32 [3, 1152], P(None, 'tensor')
- grad_wout: float32 [1152, 1152], P('tensor', 'dp')
- grad_bout: float32 [1152], replicated
- grad_wup: float32 [1152, 4608], P('dp', 'tensor')
- grad_bup: float32 [4608], P('tensor')
- grad_wdown: float32 [4608, 1152], P('tensor', 'dp')
- grad_bdown: float32 [1152], replicated
Inputs may be any that keep to these rules, and one draw needn't show every extreme that they name: Image i's patches form a grid of h rows and w columns with h w = patch_counts[i]; one image in every draw fills all 1024 slots. `positions`: slot s of image i holds the patch at (s // w, s % w) of its grid of width w for s < patch_counts[i], and (0, 0) past it.
All inputs are finite; a program needn't handle non-finite values.
Results may differ from a plain program's by a relative error of at most 0.017.
The roundings to bfloat16 on the way count: a program that leaves them out, or rounds other values in their place, can miss the bound.
Values may be sent and summed in bfloat16 or wider, within the bound.
A program may use at most 320 MiB of HBM per device.

v0:
```python
from functools import partial
import math

import jax
import jax.numpy as jnp
from jax import lax
from jax.sharding import PartitionSpec as P

HEAD = 72


epsilon = 1e-06
rope_base = 10000.0
gelu_coeff = 0.044715
root_two_pi = math.sqrt(2.0 / math.pi)


def gelu_tanh(values):
    return (
        0.5
        * values
        * (1.0 + jnp.tanh(root_two_pi * (values + gelu_coeff * values * values * values)))
    )


def rotate(values, positions, direction):
    quarter = values.shape[-1] // 4
    frequency = rope_base ** (-jnp.arange(quarter, dtype=jnp.float32) / quarter)
    pieces = []
    for column in range(2):
        angles = positions[:, column].astype(jnp.float32)[:, None, None] * frequency
        cosine = jnp.cos(angles)
        sine_term = direction * jnp.sin(angles)
        leading = values[..., 2 * column * quarter : (2 * column + 1) * quarter]
        trailing = values[..., (2 * column + 1) * quarter : (2 * column + 2) * quarter]
        pieces.append(leading * cosine - trailing * sine_term)
        pieces.append(leading * sine_term + trailing * cosine)
    return jnp.concatenate(pieces, -1)


def contract(left, right, left_dim, right_dim):
    return lax.dot_general(
        left, right, (((left_dim,), (right_dim,)), ((), ())), preferred_element_type=jnp.float32
    )


def exact_dot(left, right):
    return jnp.dot(left, right, precision=lax.Precision.HIGHEST, preferred_element_type=jnp.float32)


def row_norm(rows):
    average = jnp.mean(rows, 1)
    inverse = lax.rsqrt(jnp.mean(rows * rows, 1) - average * average + epsilon)
    return ((rows - average[:, None]) * inverse[:, None], inverse)


def masked_scores(query_rows, key_rows, patch_count, factor):
    raw_scores = (
        jnp.einsum("qhd,khd->hqk", query_rows, key_rows, preferred_element_type=jnp.float32)
        * factor
    )
    visible = jnp.arange(key_rows.shape[0]) < patch_count
    return jnp.where(visible[None, None, :], raw_scores, -1e30)


def attend_forward(factor, inputs):
    query_rows, key_rows, value_rows, patch_count = inputs
    scores = masked_scores(query_rows, key_rows, patch_count, factor)
    highest = jnp.max(scores, -1, keepdims=True)
    exponent = jnp.exp(scores - highest)
    denominator = jnp.sum(exponent, -1, keepdims=True)
    softmax_rows = (exponent / denominator).astype(jnp.bfloat16)
    attended = jnp.einsum(
        "hqk,khd->qhd", softmax_rows, value_rows, preferred_element_type=jnp.float32
    )
    return (attended, (highest + jnp.log(denominator))[..., 0])


def attend_backward(factor, inputs):
    query_rows, key_rows, value_rows, patch_count, logsum, grad_rows = inputs
    scores = masked_scores(query_rows, key_rows, patch_count, factor)
    softmax_rows = jnp.exp(scores - logsum[..., None])
    grad_soft = jnp.einsum(
        "qhd,khd->hqk", grad_rows, value_rows, preferred_element_type=jnp.float32
    )
    grad_values = jnp.einsum(
        "hqk,qhd->khd",
        softmax_rows.astype(jnp.bfloat16),
        grad_rows,
        preferred_element_type=jnp.float32,
    )
    inner_sum = jnp.sum(softmax_rows * grad_soft, -1, keepdims=True)
    grad_scores = (softmax_rows * (grad_soft - inner_sum) * factor).astype(jnp.bfloat16)
    grad_query = jnp.einsum(
        "hqk,khd->qhd", grad_scores, key_rows, preferred_element_type=jnp.float32
    )
    grad_keys = jnp.einsum(
        "hqk,qhd->khd", grad_scores, query_rows, preferred_element_type=jnp.float32
    )
    return (grad_query, grad_keys, grad_values)


def per_device(
    block_input,
    conditioning,
    patch_counts,
    positions,
    w_mod,
    b_mod,
    w_qkv,
    b_qkv,
    w_out,
    b_out,
    w_up,
    b_up,
    w_down,
    b_down,
    cotangent,
):
    own_rows, model_width = block_input.shape
    group_rows = positions.shape[0]
    images_local = conditioning.shape[0]
    slot_count = group_rows // images_local
    feat_local = w_qkv.shape[2]
    heads_local = feat_local // HEAD
    row_start = lax.axis_index("tensor") * own_rows
    factor = 1.0 / math.sqrt(HEAD)
    image_of = (row_start + jnp.arange(own_rows)) // slot_count
    one_hot = (image_of[:, None] == jnp.arange(images_local)[None, :]).astype(jnp.float32)

    def to_rows(vectors):
        return exact_dot(one_hot, vectors)

    def to_images(values):
        return exact_dot(one_hot.T, values)

    def per_image(stacked):
        return stacked.reshape((images_local, slot_count) + stacked.shape[1:])

    def modulate_group(values, shift, scale):
        shaped = values.reshape(images_local, slot_count, values.shape[1])
        return (shaped * (1.0 + scale[:, None, :]) + shift[:, None, :]).reshape(values.shape)

    mod_full, qkv_full, out_full, up_full, down_full = (
        lax.all_gather(w_mod.astype(jnp.bfloat16), "dp", axis=0, tiled=True),
        lax.all_gather(w_qkv.astype(jnp.bfloat16), "dp", axis=0, tiled=True),
        lax.all_gather(w_out.astype(jnp.bfloat16), "dp", axis=1, tiled=True),
        lax.all_gather(w_up.astype(jnp.bfloat16), "dp", axis=0, tiled=True),
        lax.all_gather(w_down.astype(jnp.bfloat16), "dp", axis=1, tiled=True),
    )
    silu_cond = jax.nn.silu(conditioning).astype(jnp.bfloat16)
    mod_cols = jnp.dot(
        silu_cond, mod_full.reshape(model_width, 6 * feat_local), preferred_element_type=jnp.float32
    )
    mod_cols = mod_cols.reshape(images_local, 6, feat_local) + b_mod
    mod_all = lax.all_gather(mod_cols, "tensor", axis=2, tiled=True)

    def norm_gather(rows_local, shift, scale):
        rows_group = lax.all_gather(rows_local, "tensor", axis=0, tiled=True)
        normal_group, inverse_group = row_norm(rows_group)
        hidden = modulate_group(normal_group, shift, scale).astype(jnp.bfloat16)
        normal = lax.dynamic_slice_in_dim(normal_group, row_start, own_rows, 0)
        inverse = lax.dynamic_slice_in_dim(inverse_group, row_start, own_rows, 0)
        return (hidden, normal, inverse)

    hidden_one, normal_one, inverse_one = norm_gather(block_input, mod_all[:, 0], mod_all[:, 1])
    projected = jnp.dot(
        hidden_one,
        qkv_full.reshape(model_width, 3 * feat_local),
        preferred_element_type=jnp.float32,
    ) + b_qkv.reshape(-1)
    projected = projected.reshape(group_rows, 3, heads_local, HEAD)
    query_rows = rotate(projected[:, 0], positions, 1.0).astype(jnp.bfloat16)
    key_rows = rotate(projected[:, 1], positions, 1.0).astype(jnp.bfloat16)
    value_rows = projected[:, 2].astype(jnp.bfloat16)
    attended, logsum = lax.map(
        partial(attend_forward, factor),
        (per_image(query_rows), per_image(key_rows), per_image(value_rows), patch_counts),
    )
    attended = attended.reshape(group_rows, feat_local).astype(jnp.bfloat16)

    def branch_sum(partial_terms, offset):
        return lax.psum_scatter(partial_terms, "tensor", scatter_dimension=0, tiled=True) + offset

    gate_one_rows = to_rows(mod_all[:, 2])
    gate_two_rows = to_rows(mod_all[:, 5])
    branch_one = branch_sum(jnp.dot(attended, out_full, preferred_element_type=jnp.float32), b_out)
    middle = block_input + gate_one_rows * branch_one
    hidden_two, normal_two, inverse_two = norm_gather(middle, mod_all[:, 3], mod_all[:, 4])
    up_pre = jnp.dot(hidden_two, up_full, preferred_element_type=jnp.float32) + b_up
    activated = gelu_tanh(up_pre).astype(jnp.bfloat16)
    branch_two = branch_sum(
        jnp.dot(activated, down_full, preferred_element_type=jnp.float32), b_down
    )
    block_output = middle + gate_two_rows * branch_two
    mod_back, qkv_back, out_back, up_back, down_back = (
        lax.all_gather(w_mod.astype(jnp.bfloat16), "dp", axis=0, tiled=True),
        lax.all_gather(w_qkv.astype(jnp.bfloat16), "dp", axis=0, tiled=True),
        lax.all_gather(w_out.astype(jnp.bfloat16), "dp", axis=1, tiled=True),
        lax.all_gather(w_up.astype(jnp.bfloat16), "dp", axis=0, tiled=True),
        lax.all_gather(w_down.astype(jnp.bfloat16), "dp", axis=1, tiled=True),
    )

    def spread_grad(grad_branch):
        return lax.all_gather(grad_branch, "tensor", axis=0, tiled=True)

    def input_sum(partial_terms):
        return lax.psum_scatter(partial_terms, "tensor", scatter_dimension=0, tiled=True)

    def norm_backward(grad_hidden, normal, inverse, scale):
        grad_normal = grad_hidden * (1.0 + to_rows(scale))
        mean_plain = jnp.mean(grad_normal, 1, keepdims=True)
        mean_cross = jnp.mean(grad_normal * normal, 1, keepdims=True)
        return inverse[:, None] * (grad_normal - mean_plain - normal * mean_cross)

    grad_gate_two = to_images(cotangent * branch_two)
    grad_branch_two = (cotangent * gate_two_rows).astype(jnp.bfloat16)
    grad_rows_two = spread_grad(grad_branch_two)
    grad_bdown_local = jnp.sum(grad_rows_two.astype(jnp.float32), 0)
    grad_wdown_local = contract(activated, grad_rows_two, 0, 0)
    grad_activated = contract(grad_rows_two, down_back, 1, 1)
    gelu_pull = jax.vjp(gelu_tanh, up_pre)[1]
    grad_up = gelu_pull(grad_activated)[0].astype(jnp.bfloat16)
    grad_bup_local = jnp.sum(grad_up.astype(jnp.float32), 0)
    grad_wup_local = contract(hidden_two, grad_up, 0, 0)
    grad_hidden_two = input_sum(contract(grad_up, up_back, 1, 1))
    grad_shift_two = to_images(grad_hidden_two)
    grad_scale_two = to_images(grad_hidden_two * normal_two)
    grad_middle = cotangent + norm_backward(grad_hidden_two, normal_two, inverse_two, mod_all[:, 4])
    grad_gate_one = to_images(grad_middle * branch_one)
    grad_branch_one = (grad_middle * gate_one_rows).astype(jnp.bfloat16)
    grad_rows_one = spread_grad(grad_branch_one)
    grad_bout_local = jnp.sum(grad_rows_one.astype(jnp.float32), 0)
    grad_wout_local = contract(attended, grad_rows_one, 0, 0)
    grad_attended = contract(grad_rows_one, out_back, 1, 1).astype(jnp.bfloat16)
    grad_attended = grad_attended.reshape(group_rows, heads_local, HEAD)
    grad_query, grad_keys, grad_values = lax.map(
        partial(attend_backward, factor),
        (
            per_image(query_rows),
            per_image(key_rows),
            per_image(value_rows),
            patch_counts,
            logsum,
            per_image(grad_attended),
        ),
    )
    head_shape = (group_rows, heads_local, HEAD)
    grad_projected = jnp.stack(
        [
            rotate(grad_query.reshape(head_shape), positions, -1.0),
            rotate(grad_keys.reshape(head_shape), positions, -1.0),
            grad_values.reshape(head_shape),
        ],
        1,
    )
    grad_projected = grad_projected.astype(jnp.bfloat16).reshape(group_rows, 3 * feat_local)
    grad_bqkv_local = jnp.sum(grad_projected.astype(jnp.float32), 0).reshape(3, feat_local)
    grad_wqkv_local = contract(hidden_one, grad_projected, 0, 0).reshape(model_width, 3, feat_local)
    grad_hidden_one = input_sum(
        contract(grad_projected, qkv_back.reshape(model_width, 3 * feat_local), 1, 1)
    )
    grad_shift_one = to_images(grad_hidden_one)
    grad_scale_one = to_images(grad_hidden_one * normal_one)
    grad_input = grad_middle + norm_backward(
        grad_hidden_one, normal_one, inverse_one, mod_all[:, 1]
    )
    grad_mod_part = jnp.stack(
        [
            grad_shift_one,
            grad_scale_one,
            grad_gate_one,
            grad_shift_two,
            grad_scale_two,
            grad_gate_two,
        ],
        1,
    )
    grad_mod = lax.psum_scatter(grad_mod_part, "tensor", scatter_dimension=2, tiled=True).astype(
        jnp.bfloat16
    )
    grad_bmod_local = jnp.sum(grad_mod.astype(jnp.float32), 0)
    grad_mod_flat = grad_mod.reshape(images_local, 6 * feat_local)
    grad_wmod_local = contract(silu_cond, grad_mod_flat, 0, 0).reshape(model_width, 6, feat_local)
    grad_silu = lax.psum(
        contract(grad_mod_flat, mod_back.reshape(model_width, 6 * feat_local), 1, 1), "tensor"
    )
    silu_pull = jax.vjp(jax.nn.silu, conditioning)[1]
    grad_cond = silu_pull(grad_silu)[0]
    grad_wmod, grad_wqkv, grad_wout, grad_wup, grad_wdown = (
        lax.psum_scatter(
            grad_wmod_local.astype(jnp.bfloat16), "dp", scatter_dimension=0, tiled=True
        ).astype(jnp.float32),
        lax.psum_scatter(
            grad_wqkv_local.astype(jnp.bfloat16), "dp", scatter_dimension=0, tiled=True
        ).astype(jnp.float32),
        lax.psum_scatter(
            grad_wout_local.astype(jnp.bfloat16), "dp", scatter_dimension=1, tiled=True
        ).astype(jnp.float32),
        lax.psum_scatter(
            grad_wup_local.astype(jnp.bfloat16), "dp", scatter_dimension=0, tiled=True
        ).astype(jnp.float32),
        lax.psum_scatter(
            grad_wdown_local.astype(jnp.bfloat16), "dp", scatter_dimension=1, tiled=True
        ).astype(jnp.float32),
    )
    grad_bmod, grad_bqkv, grad_bout, grad_bup, grad_bdown = lax.psum(
        (grad_bmod_local, grad_bqkv_local, grad_bout_local, grad_bup_local, grad_bdown_local), "dp"
    )
    return (
        block_output,
        grad_input,
        grad_cond,
        grad_wmod,
        grad_bmod,
        grad_wqkv,
        grad_bqkv,
        grad_wout,
        grad_bout,
        grad_wup,
        grad_bup,
        grad_wdown,
        grad_bdown,
    )


def solution(mesh):
    placed = (
        P(("dp", "tensor"), None),
        P("dp", None),
        P("dp"),
        P("dp", None),
        P("dp", None, "tensor"),
        P(None, "tensor"),
        P("dp", None, "tensor"),
        P(None, "tensor"),
        P("tensor", "dp"),
        P(),
        P("dp", "tensor"),
        P("tensor"),
        P("tensor", "dp"),
        P(),
        P(("dp", "tensor"), None),
    )
    return jax.shard_map(
        per_device,
        mesh=mesh,
        in_specs=placed,
        out_specs=(
            P(("dp", "tensor"), None),
            P(("dp", "tensor"), None),
            P("dp", None),
            P("dp", None, "tensor"),
            P(None, "tensor"),
            P("dp", None, "tensor"),
            P(None, "tensor"),
            P("tensor", "dp"),
            P(),
            P("dp", "tensor"),
            P("tensor"),
            P("tensor", "dp"),
            P(),
        ),
        check_vma=False,
    )
```

profile of v0, /device:TPU:0, one launch (start us, length us, event | category | flops | bytes accessed | tf_op | source)
XLA Modules:
  0.0 1679.5 jit_solution(13129470823882768155)
XLA Ops:
  12.4 37.9 %all_gather.39 = bf16[288,1152]{0,1:T(8,128)(2,1)} all-gather(bf16[288,144]{0,1:T(8,128)(2,1)S(1)} %convert_element_type.170), channel_id=1, replica_groups=mesh['dp'=8,'tensor'=4] {'dp'}, dimensions={1}, use_global_device_ids=true | all-gather | bytes 746496 | tf_op jit(solution)/shard_map/all_gather | solution.py:147
  76.5 84.8 %all-gather.9.cloned.1.call-done = bf16[1152,6,288]{2,0,1:T(8,128)(2,1)} async-done(((bf16[144,6,288]{2,0,1:T(8,128)(2,1)}), bf16[1152,6,288]{2,0,1:T(8,128)(2,1)}) %all-gather.9.cloned.1.call-update) | async-done | bytes 3981328 | tf_op jit(solution)/shard_map/all_gather | solution.py:145
  199.6 32.1 %all-gather.11.cloned.1.call-done = f32[2048,1152]{1,0:T(8,128)} async-done(((f32[512,1152]{1,0:T(8,128)}), f32[2048,1152]{1,0:T(8,128)}) %all-gather.11.cloned.1.call-update) | async-done | bytes 9437200 | tf_op jit(solution)/shard_map/all_gather | solution.py:159
  269.7 31.5 %while.26 = (s32[]{:T(128)}, bf16[2,1024,4,72]{1,3,2,0:T(8,128)(2,1)}, f32[2,4,1024]{2,1,0:T(4,128)}, bf16[2,1024,4,72]{1,3,2,0:T(8,128)(2,1)S(1)}, s32[2]{0:T(1...) while((s32[]{:T(128)}, ...), condition=%wide.region_5.6_spmd, body=%wide.region_2.5_spmd.sunk | while | flops 1258288128 | bytes 63117536 | solution.py:176
  311.6 76.3 %reduce-scatter.13.cloned.1.call-done = f32[512,1152]{1,0:T(8,128)} async-done(((f32[2048,1152]{1,0:T(8,128)}), f32[512,1152]{1,0:T(8,128)}) %reduce-scatter.13.cloned.1.call-update) | async-done | bytes 2359312 | tf_op jit(solution)/shard_map/reduce_scatter | solution.py:183
  399.2 58.3 %all-gather.15.cloned.1.call-done = f32[2048,1152]{1,0:T(8,128)} async-done(((f32[512,1152]{1,0:T(8,128)}), f32[2048,1152]{1,0:T(8,128)}) %all-gather.15.cloned.1.call-update) | async-done | bytes 9437200 | tf_op jit(solution)/shard_map/all_gather | solution.py:159
  469.8 45.2 %all-gather.17.cloned.1.call-done = bf16[1152,1152]{1,0:T(8,128)(2,1)} async-done(((bf16[144,1152]{1,0:T(8,128)(2,1)}), bf16[1152,1152]{1,0:T(8,128)(2,1)}) %all-gather.17.cloned.1.call-update) | async-done | bytes 2654224 | tf_op jit(solution)/shard_map/all_gather | solution.py:148
  526.6 44.8 %all-gather.19.cloned.1.call-done = bf16[1152,1152]{0,1:T(8,128)(2,1)} async-done(((bf16[1152,144]{0,1:T(8,128)(2,1)}), bf16[1152,1152]{0,1:T(8,128)(2,1)}) %all-gather.19.cloned.1.call-update) | async-done | bytes 2654224 | tf_op jit(solution)/shard_map/all_gather | solution.py:149
  587.5 74.3 %reduce-scatter.15.cloned.1.call-done = f32[512,1152]{1,0:T(8,128)} async-done(((f32[2048,1152]{1,0:T(8,128)}), f32[512,1152]{1,0:T(8,128)}) %reduce-scatter.15.cloned.1.call-update) | async-done | bytes 2359312 | tf_op jit(solution)/shard_map/reduce_scatter | solution.py:183
  667.5 37.5 %all-gather.21.cloned.1.call-done = bf16[2048,1152]{1,0:T(8,128)(2,1)} async-done(((bf16[512,1152]{1,0:T(8,128)(2,1)}), bf16[2048,1152]{1,0:T(8,128)(2,1)}) %all-gather.21.cloned.1.call-update) | async-done | bytes 4718608 | tf_op jit(solution)/shard_map/all_gather | solution.py:205
  735.6 76.7 %reduce-scatter.17.cloned.1.call-done = f32[512,1152]{1,0:T(8,128)} async-done(((f32[2048,1152]{1,0:T(8,128)}), f32[512,1152]{1,0:T(8,128)}) %reduce-scatter.17.cloned.1.call-update) | async-done | bytes 2359312 | tf_op jit(solution)/shard_map/reduce_scatter | solution.py:208
  820.8 37.5 %all-gather.23.cloned.1.call-done = bf16[2048,1152]{1,0:T(8,128)(2,1)} async-done(((bf16[512,1152]{1,0:T(8,128)(2,1)}), bf16[2048,1152]{1,0:T(8,128)(2,1)}) %all-gather.23.cloned.1.call-update) | async-done | bytes 4718608 | tf_op jit(solution)/shard_map/all_gather | solution.py:205
  864.9 264.6 %while.27 = (s32[]{:T(128)}, f32[2,1024,4,72]{1,0,3,2:T(2,128)}, f32[2,1024,4,72]{1,0,3,2:T(2,128)}, bf16[2,1024,4,72]{1,0,3,2:T(2,128)(2,1)}, bf16[2,1024,4,72]...) while((s32[]{:T(128)}, f32[2,1024,4,72]{1,0,3,2:T(2,128)}, ...), condition=%wide.region_15.16_spmd, body=%wide.region_13.15_spmd.sunk | while | flops 3078630400 | bytes 284741888 | solution.py:237
  908.1 22.7 %fusion.217 = f32[1,1024,4,72]{1,3,2,0:T(8,128)S(1)} fusion(f32[4,1024,1024]{1,2,0:T(8,128)} %copy-done, f32[4,1024,1024]{1,2,0:T(8,128)} %fusion.215, bf16[2,1024,4,72]{1,3,2,0:T(8,128)(2,1)} %get-tuple-element.464, s32[]{:T(128)S(6)} %copy.237), kind=kOutput, calls=%fused_computation.31.clone.1 | convolution fusion | flops 624956416 | bytes 68878336 | tf_op jit(solution)/shard_map/while/body/eval_jaxpr/hqk,qhd->khd/dot_general | solution.py:97
  930.8 22.0 %fusion.216 = f32[1,1024,4,72]{1,3,2,0:T(8,128)S(1)} fusion(f32[4,1024,1024]{1,2,0:T(8,128)} %copy-done, f32[4,1024,1024]{1,2,0:T(8,128)} %fusion.215, bf16[2,1024,4,72]{1,3,2,0:T(8,128)(2,1)} %copy-done.11, s32[]{:T(128)S(6)} %copy.237), kind=kOutput, calls=%fused_computation.30.clone.1 | convolution fusion | flops 624956416 | bytes 68878336 | tf_op jit(solution)/shard_map/while/body/eval_jaxpr/hqk,khd->qhd/dot_general | solution.py:94
  1040.2 22.7 %fusion.217 = f32[1,1024,4,72]{1,3,2,0:T(8,128)S(1)} fusion(f32[4,1024,1024]{1,2,0:T(8,128)} %copy-done, f32[4,1024,1024]{1,2,0:T(8,128)} %fusion.215, bf16[2,1024,4,72]{1,3,2,0:T(8,128)(2,1)} %get-tuple-element.464, s32[]{:T(128)S(6)} %copy.237), kind=kOutput, calls=%fused_computation.31.clone.1 | convolution fusion | flops 624956416 | bytes 68878336 | tf_op jit(solution)/shard_map/while/body/eval_jaxpr/hqk,qhd->khd/dot_general | solution.py:97
  1062.9 22.0 %fusion.216 = f32[1,1024,4,72]{1,3,2,0:T(8,128)S(1)} fusion(f32[4,1024,1024]{1,2,0:T(8,128)} %copy-done, f32[4,1024,1024]{1,2,0:T(8,128)} %fusion.215, bf16[2,1024,4,72]{1,3,2,0:T(8,128)(2,1)} %copy-done.11, s32[]{:T(128)S(6)} %copy.237), kind=kOutput, calls=%fused_computation.30.clone.1 | convolution fusion | flops 624956416 | bytes 68878336 | tf_op jit(solution)/shard_map/while/body/eval_jaxpr/hqk,khd->qhd/dot_general | solution.py:94
  1155.7 77.6 %reduce-scatter.19.cloned.1.call-done = f32[512,1152]{1,0:T(8,128)} async-done(((f32[2048,1152]{1,0:T(8,128)}), f32[512,1152]{1,0:T(8,128)}) %reduce-scatter.19.cloned.1.call-update) | async-done | bytes 2359312 | tf_op jit(solution)/shard_map/reduce_scatter | solution.py:208
  1306.8 42.9 %reduce-scatter.29.cloned.1.call-done = bf16[1152,144]{0,1:T(8,128)(2,1)} async-done(((bf16[1152,1152]{0,1:T(8,128)(2,1)}), bf16[1152,144]{0,1:T(8,128)(2,1)}) %reduce-scatter.29.cloned.1.call-update) | async-done | bytes 331792 | tf_op jit(solution)/shard_map/reduce_scatter | solution.py:303
  1351.6 72.4 %reduce-scatter.27.cloned.1.call-done = bf16[144,1152]{1,0:T(8,128)(2,1)} async-done(((bf16[1152,1152]{1,0:T(8,128)(2,1)}), bf16[144,1152]{1,0:T(8,128)(2,1)}) %reduce-scatter.27.cloned.1.call-update) | async-done | bytes 331792 | tf_op jit(solution)/shard_map/reduce_scatter | solution.py:300
  1429.0 60.2 %reduce-scatter.25.cloned.1.call-done = bf16[288,144]{0,1:T(8,128)(2,1)} async-done(((bf16[288,1152]{0,1:T(8,128)(2,1)}), bf16[288,144]{0,1:T(8,128)(2,1)}) %reduce-scatter.25.cloned.1.call-update) | async-done | bytes 82960 | tf_op jit(solution)/shard_map/reduce_scatter | solution.py:297
  1490.7 71.7 %reduce-scatter.23.cloned.1.call-done = bf16[144,3,288]{2,0,1:T(8,128)(2,1)} async-done(((bf16[1152,3,288]{2,0,1:T(8,128)(2,1)}), bf16[144,3,288]{2,0,1:T(8,128)(2,1)}) %reduce-scatter.23.cloned.1.call-update) | async-done | bytes 248848 | tf_op jit(solution)/shard_map/reduce_scatter | solution.py:294
  1571.5 38.3 %all-reduce = (f32[6,288]{1,0:T(8,128)}, f32[3,288]{1,0:T(4,128)}, f32[1152]{0:T(1024)}, f32[1152]{0:T(1024)}, f32[1152]{0:T(1024)}) all-reduce(f32[6,288]{1,0:T(8,128)S(1)} %convert_reduce_fusion.4, f32[3,288]{1,0:T(4,128)S(1)} %reshape.391, f32[1152]{0:T(1024)S(1)} %convert_reduce_fusion.2, ...), channel_id=1, replica_groups=mesh['dp'=8,'tensor'=4] {'dp'}, use_global_device_ids=true, to_apply=%region_23.24 | all-reduce | flops 6048 | bytes 48384 | tf_op jit(solution)/shard_map/psum | solution.py:307
  1620.8 49.4 %reduce-scatter.21.cloned.1.call-done = bf16[144,6,288]{2,0,1:T(8,128)(2,1)} async-done(((bf16[1152,6,288]{2,0,1:T(8,128)(2,1)}), bf16[144,6,288]{2,0,1:T(8,128)(2,1)}) %reduce-scatter.21.cloned.1.call-update) | async-done | bytes 497680 | tf_op jit(solution)/shard_map/reduce_scatter | solution.py:291
  (324 shorter events, 556.2 us)
Async XLA Ops:
  7.2 65.1 %all-gather.13.cloned.1.call-start = ((), (), s32[]{:S(2)}) async-start(), calls=%async_computation.12 | async-start | bytes 2985984 | tf_op jit(solution)/shard_map/all_gather | solution.py:146
  9.1 152.3 %all-gather.9.cloned.1.call-start = ((), (), s32[]{:S(2)}) async-start(), calls=%async_computation.10 | async-start | bytes 5971968 | tf_op jit(solution)/shard_map/all_gather | solution.py:145
  11.5 220.3 %all-gather.11.cloned.1.call-start = ((), (), s32[]{:S(2)}) async-start(), calls=%async_computation.11 | async-start | bytes 11796480 | tf_op jit(solution)/shard_map/all_gather | solution.py:159
  12.2 375.7 %reduce-scatter.13.cloned.1.call-start = ((), (), s32[]{:S(2)}) async-start(), calls=%async_computation.13 | async-start | bytes 11796480 | tf_op jit(solution)/shard_map/reduce_scatter | solution.py:183
  52.5 197.0 %copy-start.19 = (f32[2048,18]{0,1:T(8,128)}, f32[2048,18]{0,1:T(8,128)S(1)}, u32[]{:S(2)}) copy-start(f32[2048,18]{0,1:T(8,128)S(1)} %get-tuple-element.285) | copy-start | bytes 442372
  52.6 197.0 %copy-start.21 = (f32[2048,18]{0,1:T(8,128)}, f32[2048,18]{0,1:T(8,128)S(1)}, u32[]{:S(2)}) copy-start(f32[2048,18]{0,1:T(8,128)S(1)} %get-tuple-element.294) | copy-start | bytes 442372
  76.5 91.4 %copy-start.44 = (f32[2,1152]{1,0:T(2,128)S(1)}, f32[2,1152]{1,0:T(2,128)}, u32[]{:S(2)}) copy-start(f32[2,1152]{1,0:T(2,128)} %param.20) | copy-start | bytes 27652
  76.5 91.4 %copy-start.51 = (f32[6,288]{1,0:T(8,128)S(1)}, f32[6,288]{1,0:T(8,128)}, u32[]{:S(2)}) copy-start(f32[6,288]{1,0:T(8,128)} %param.24) | copy-start | bytes 20740
  309.8 147.6 %all-gather.15.cloned.1.call-start = ((), (), s32[]{:S(2)}) async-start(), calls=%async_computation.14 | async-start | bytes 11796480 | tf_op jit(solution)/shard_map/all_gather | solution.py:159
  309.9 502.4 %copy-start.37 = (s32[512]{0:T(512)}, s32[512]{0:T(512)S(1)}, u32[]{:S(2)}) copy-start(s32[512]{0:T(512)S(1)} %add_select_fusion) | copy-start | bytes 6148
  393.1 122.0 %all-gather.17.cloned.1.call-start = ((), (), s32[]{:S(2)}) async-start(), calls=%async_computation.15 | async-start | bytes 2985984 | tf_op jit(solution)/shard_map/all_gather | solution.py:148
  395.2 176.2 %all-gather.19.cloned.1.call-start = ((), (), s32[]{:S(2)}) async-start(), calls=%async_computation.16 | async-start | bytes 2985984 | tf_op jit(solution)/shard_map/all_gather | solution.py:149
  397.1 264.7 %reduce-scatter.15.cloned.1.call-start = ((), (), s32[]{:S(2)}) async-start(), calls=%async_computation.17 | async-start | bytes 11796480 | tf_op jit(solution)/shard_map/reduce_scatter | solution.py:183
  585.2 119.9 %all-gather.21.cloned.1.call-start = ((), (), s32[]{:S(2)}) async-start(), calls=%async_computation.18 | async-start | bytes 5898240 | tf_op jit(solution)/shard_map/all_gather | solution.py:205
  667.5 144.8 %reduce-scatter.17.cloned.1.call-start = ((), (), s32[]{:S(2)}) async-start(), calls=%async_computation.19 | async-start | bytes 11796480 | tf_op jit(solution)/shard_map/reduce_scatter | solution.py:208
  734.2 124.1 %all-gather.23.cloned.1.call-start = ((), (), s32[]{:S(2)}) async-start(), calls=%async_computation.20 | async-start | bytes 5898240 | tf_op jit(solution)/shard_map/all_gather | solution.py:205
  820.7 412.6 %reduce-scatter.19.cloned.1.call-start = ((), (), s32[]{:S(2)}) async-start(), calls=%async_computation.21 | async-start | bytes 11796480 | tf_op jit(solution)/shard_map/reduce_scatter | solution.py:208
  1155.2 141.9 %reduce-scatter.31.cloned.1.call-start = ((), (), s32[]{:S(2)}) async-start(), calls=%async_computation.27 | async-start | bytes 737280
  1252.9 96.8 %reduce-scatter.29.cloned.1.call-start = ((), (), s32[]{:S(2)}) async-start(), calls=%async_computation.26 | async-start | bytes 2985984 | tf_op jit(solution)/shard_map/reduce_scatter | solution.py:303
  1266.4 157.5 %reduce-scatter.27.cloned.1.call-start = ((), (), s32[]{:S(2)}) async-start(), calls=%async_computation.25 | async-start | bytes 2985984 | tf_op jit(solution)/shard_map/reduce_scatter | solution.py:300
  1278.5 210.7 %reduce-scatter.25.cloned.1.call-start = ((), (), s32[]{:S(2)}) async-start(), calls=%async_computation.24 | async-start | bytes 995328 | tf_op jit(solution)/shard_map/reduce_scatter | solution.py:297
  1285.7 276.8 %reduce-scatter.23.cloned.1.call-start = ((), (), s32[]{:S(2)}) async-start(), calls=%async_computation.23 | async-start | bytes 2985984 | tf_op jit(solution)/shard_map/reduce_scatter | solution.py:294
  1297.1 373.1 %reduce-scatter.21.cloned.1.call-start = ((), (), s32[]{:S(2)}) async-start(), calls=%async_computation.22 | async-start | bytes 5971968 | tf_op jit(solution)/shard_map/reduce_scatter | solution.py:291
  1425.9 138.4 %copy-start.43 = (f32[2,1,1152]{2,0,1:T(2,128)S(1)}, f32[2,1,1152]{2,0,1:T(2,128)}, u32[]{:S(2)}) copy-start(f32[2,1,1152]{2,0,1:T(2,128)} %copy-done.42) | copy-start | bytes 27652
  (62 other events, 679.3 us)
Sparse Core Ops, SparseCore 0:
  10.8 61.4 all-gather.12
  75.1 86.1 all-gather.8
  162.9 68.7 all-gather.10
  309.9 77.8 reduce-scatter.12
  393.2 64.1 all-gather.14
  460.0 54.9 all-gather.16
  517.8 53.5 all-gather.18
  585.3 76.4 reduce-scatter.14
  667.6 37.4 all-gather.20
  734.3 77.8 reduce-scatter.16
  820.9 37.4 all-gather.22
  1155.3 77.9 reduce-scatter.18
  1253.0 22.0 reduce-scatter.30
  1278.6 71.0 reduce-scatter.28
  1353.2 70.7 reduce-scatter.26
  1427.8 61.2 reduce-scatter.24
  1492.6 69.7 reduce-scatter.22
  1566.0 104.0 reduce-scatter.20
where the time goes:
time: 1690 us; the launch traced here: 1680 us
  waiting for transfers between devices  962 us (57%)
  matrix products  303 us (18%)
  local copies, waits for them, and re-layouts  217 us (13%)
  blocking collectives  100 us (6%)
  other arithmetic  79.3 us (5%)
    reduce_scatter x2, waiting for transfers between devices, input_sum(): lax.psum_scatter(partial_terms, 'tensor', scatter_dimension=0, tiled=True)  154 us
    reduce_scatter x2, waiting for transfers between devices, branch_sum(): lax.psum_scatter(partial_terms, 'tensor', scatter_dimension=0, tiled=True)  151 us
    dynamic_update_slice x12, local copies, waits for them, and re-layouts, per_device(): lax.map(partial(attend_forward, factor), (per_image(query_rows), per_imag...  130 us
    all_gather x2, waiting for transfers between devices, norm_gather(): rows_group = lax.all_gather(rows_local, 'tensor', axis=0, tiled=True)  90.4 us
    dot_general x10, matrix products, contract(): lax.dot_general(left, right, (((left_dim,), (right_dim,)), ((), ())), pre...  89.3 us
    all_gather x1, waiting for transfers between devices, per_device(): lax.all_gather(w_mod.astype(jnp.bfloat16), 'dp', axis=0, tiled=True)  84.8 us
    all_gather x2, waiting for transfers between devices, spread_grad(): return lax.all_gather(grad_branch, 'tensor', axis=0, tiled=True)  75.1 us
    reduce_scatter x1, waiting for transfers between devices, per_device(): lax.psum_scatter(grad_wup_local.astype(jnp.bfloat16), 'dp', scatter_dimen...  72.4 us
  transfers between devices with their start and end apart: 18, of which 17 were waited for; matrix products, arithmetic and copies ran while one was open for 8% of the time, Pallas kernels for 0%

commit v1 on v0

--- a/solution.py
+++ b/solution.py
@@ -4,6 +4,8 @@
 import jax
 import jax.numpy as jnp
 from jax import lax
+from jax.experimental import pallas as pl
+from jax.experimental.pallas import tpu as pltpu
 from jax.sharding import PartitionSpec as P
 
 HEAD = 72
@@ -324,7 +326,782 @@
     )
 
 
+LANES = 128
+ZS, YS, XS, CORES = 4, 2, 2, 2
+MESH_ID = pl.DeviceIdType.MESH
+CORE_SWAP = [(0, 1), (1, 0), (2, 3), (3, 2)]
+X_SWAP = [(0, 2), (2, 0), (1, 3), (3, 1)]
+LOG2E = 1.0 / math.log(2.0)
+PAIRS = (
+    (0, 0, 32, 32),
+    (0, 64, 48, 32),
+    (1, 0, 32, 32),
+    (1, 64, 32, 48),
+    (2, 0, 32, 32),
+    (2, 64, 48, 32),
+)
+HBM = pl.BlockSpec(memory_space=pl.ANY)
+VMEM = pl.BlockSpec(memory_space=pltpu.VMEM)
+
+
+def image_per_chip(mesh):
+    return dict(mesh.shape) == {"dp": ZS * YS, "tensor": XS * CORES}
+
+
+def place():
+    data, tensor = lax.axis_index("dp"), lax.axis_index("tensor")
+    return data // YS, data % YS, tensor // CORES, tensor % CORES
+
+
+def flip_z(z, step):
+    high, low = z // 2, z % 2
+    if step & 2:
+        high = 1 - high
+    if step & 1:
+        low = 1 - low
+    return high * 2 + low
+
+
+def device(z, y, x, core):
+    return (z * YS + y, x * CORES + core)
+
+
+def greet(targets):
+    barrier = pltpu.get_barrier_semaphore()
+    for target in targets:
+        pl.semaphore_signal(barrier, inc=1, device_id=target, device_id_type=MESH_ID)
+    pl.semaphore_wait(barrier, len(targets))
+
+
+def grid_peers():
+    z, y, x, core = place()
+    peers = [device(z, y, 1 - x, core), device(z, 1 - y, x, core)]
+    return peers + [device(flip_z(z, step), y, x, core) for step in (1, 2, 3)]
+
+
+def chunk_list():
+    chunks = []
+    for matrix, row, first, second in PAIRS:
+        chunks.append(((matrix, row, first, 0), (matrix, row + first, second, 1)))
+    return chunks
+
+
+def remote(source, target_ref, sems, index, where):
+    return pltpu.make_async_remote_copy(
+        src_ref=source,
+        dst_ref=target_ref,
+        send_sem=sems[0].at[index],
+        recv_sem=sems[1].at[index],
+        device_id=where,
+        device_id_type=MESH_ID,
+    )
+
+
+def gather_kernel(*refs):
+    shards, wholes = refs[:3], refs[3:6]
+    sends, recvs, local = refs[6:]
+    sems = (sends, recvs)
+    z, y, x, core = place()
+    peers = grid_peers()
+    width = shards[0].shape[1]
+    greet(peers)
+    mine = pl.ds(pl.multiple_of(x * width, LANES), width)
+    keeps = []
+    for matrix in range(3):
+        keep = pltpu.make_async_copy(
+            shards[matrix], wholes[matrix].at[z, y, :, mine], local.at[matrix]
+        )
+        keep.start()
+        keeps.append(keep)
+    chunks = chunk_list()
+    copies = {}
+
+    def launch(number, stage, chunk):
+        matrix, row, rows, route = chunk
+        whole, span = wholes[matrix], pl.ds(row, rows)
+        base = number * 5
+        if stage == 0:
+            made = [
+                remote(
+                    shards[matrix].at[span, :],
+                    whole.at[z, y, span, mine],
+                    sems,
+                    base + step,
+                    peers[2 + step],
+                )
+                for step in range(3)
+            ]
+        elif (stage == 1) == (route == 0):
+            part = whole.at[:, y, span, mine] if stage == 1 else whole.at[:, :, span, mine]
+            made = [remote(part, part, sems, base + 2 + stage, peers[0])]
+        else:
+            part = whole.at[:, y, span, mine] if stage == 1 else whole.at[:, y, span, :]
+            made = [remote(part, part, sems, base + 2 + stage, peers[1])]
+        for copy in made:
+            copy.start()
+        copies[number, stage] = made
+
+    def settle(number, stage):
+        for copy in copies[number, stage]:
+            copy.wait_recv()
+
+    total = len(chunks)
+    for tick in range(total + 3):
+        for stage in (2, 1, 0):
+            pair = tick - stage
+            if not 0 <= pair < total:
+                continue
+            for route in range(2):
+                number = pair * 2 + route
+                if stage > 0:
+                    settle(number, stage - 1)
+                if stage == 1 and route == 0 and chunks[pair][0][1] == 0:
+                    keeps[chunks[pair][0][0]].wait()
+                launch(number, stage, chunks[pair][route])
+        pair = tick - 3
+        if 0 <= pair < total:
+            for route in range(2):
+                settle(pair * 2 + route, 2)
+    for made in copies.values():
+        for copy in made:
+            copy.wait_send()
+
+
+def gather_weights(shards, ident):
+    rows, width = shards[0].shape
+    shape = jax.ShapeDtypeStruct((ZS, YS, rows, XS * width), jnp.bfloat16)
+    count = len(PAIRS) * 2 * 5
+    wholes = pl.pallas_call(
+        gather_kernel,
+        out_shape=[shape] * 3,
+        in_specs=[VMEM] * 3,
+        out_specs=[HBM] * 3,
+        scratch_shapes=[
+            pltpu.SemaphoreType.DMA((count,)),
+            pltpu.SemaphoreType.DMA((count,)),
+            pltpu.SemaphoreType.DMA((3,)),
+        ],
+        compiler_params=pltpu.CompilerParams(collective_id=ident, has_side_effects=True),
+        name="gather_weights",
+    )(*shards)
+    return [whole.reshape(ZS * YS * rows, XS * width) for whole in wholes]
+
+
+def scatter_kernel(*refs):
+    parts, sums = refs[:3], refs[3:6]
+    own, first_in, second_in, third_in, sends, recvs, local = refs[6:]
+    sems = (sends, recvs)
+    z, y, x, core = place()
+    peers = grid_peers()
+    width = sums[0].shape[1]
+    greet(peers)
+    mine = pl.ds(pl.multiple_of(x * width, LANES), width)
+    theirs = pl.ds(pl.multiple_of((1 - x) * width, LANES), width)
+    chunks = chunk_list()
+    copies = {}
+    loads = {}
+
+    def launch(number, stage, chunk):
+        matrix, row, rows, route = chunk
+        part, span = parts[matrix], pl.ds(row, rows)
+        base = number * 3
+        if stage == 0:
+            made = []
+            for slot in range(2):
+                if route == 0:
+                    column = mine if slot == 0 else theirs
+                    source = part.at[:, 1 - y, span, column]
+                    kept = part.at[:, y, span, column]
+                    where = peers[1]
+                else:
+                    line = y if slot == 0 else 1 - y
+                    source = part.at[:, line, span, theirs]
+                    kept = part.at[:, line, span, mine]
+                    where = peers[0]
+                copy = remote(source, first_in.at[matrix, slot, :, span, :], sems, base + slot, where)
+                made.append(copy)
+                load = pltpu.make_async_copy(
+                    kept, own.at[matrix, slot, :, span, :], local.at[number * 2 + slot]
+                )
+                load.start()
+                loads[number, slot] = load
+        elif stage == 1:
+            where = peers[0] if route == 0 else peers[1]
+            made = [
+                remote(
+                    own.at[matrix, 1, :, span, :],
+                    second_in.at[matrix, :, span, :],
+                    sems,
+                    base + 2,
+                    where,
+                )
+            ]
+        else:
+            made = [
+                remote(
+                    own.at[matrix, 0, flip_z(z, step), span, :],
+                    third_in.at[matrix, step - 1, span, :],
+                    sems,
+                    third[number] + step - 1,
+                    peers[1 + step],
+                )
+                for step in (1, 2, 3)
+            ]
+        for copy in made:
+            copy.start()
+        copies[number, stage] = made
+
+    third = {n: len(chunks) * 2 * 3 + n * 3 for n in range(len(chunks) * 2)}
+
+    def add_into(target, arrived, rows):
+        def step(i, carry):
+            at = pl.ds(pl.multiple_of(i * 16, 16), 16)
+            target[at, :] = (
+                target[at, :].astype(jnp.float32) + arrived[at, :].astype(jnp.float32)
+            ).astype(jnp.bfloat16)
+            return carry
+
+        lax.fori_loop(0, rows // 16, step, 0)
+
+    def merge(number, stage, chunk):
+        matrix, row, rows, route = chunk
+        span = pl.ds(row, rows)
+        for copy in copies[number, stage]:
+            copy.wait_recv()
+        if stage == 0:
+            for slot in range(2):
+                loads[number, slot].wait()
+
+                def one(i, carry, slot=slot):
+                    add_into(
+                        own.at[matrix, slot, i, span, :],
+                        first_in.at[matrix, slot, i, span, :],
+                        rows,
+                    )
+                    return carry
+
+                lax.fori_loop(0, ZS, one, 0)
+        elif stage == 1:
+
+            def two(i, carry):
+                add_into(own.at[matrix, 0, i, span, :], second_in.at[matrix, i, span, :], rows)
+                return carry
+
+            lax.fori_loop(0, ZS, two, 0)
+        else:
+
+            def step(i, carry):
+                at = pl.ds(pl.multiple_of(row + i * 16, 16), 16)
+                total = own[matrix, 0, z, at, :].astype(jnp.float32)
+                for k in range(3):
+                    total = total + third_in[matrix, k, at, :].astype(jnp.float32)
+                sums[matrix][at, :] = total
+                return carry
+
+            lax.fori_loop(0, rows // 16, step, 0)
+
+    total = len(chunks)
+    for tick in range(total + 3):
+        for stage in (2, 1, 0):
+            pair = tick - stage
+            if not 0 <= pair < total:
+                continue
+            for route in range(2):
+                number = pair * 2 + route
+                if stage > 0:
+                    merge(number, stage - 1, chunks[pair][route])
+                launch(number, stage, chunks[pair][route])
+        pair = tick - 3
+        if 0 <= pair < total:
+            for route in range(2):
+                merge(pair * 2 + route, 2, chunks[pair][route])
+    for made in copies.values():
+        for copy in made:
+            copy.wait_send()
+
+
+def scatter_grads(parts, ident):
+    rows, width = parts[0].shape[0] // (ZS * YS), parts[0].shape[1] // XS
+    parts = [part.reshape(ZS, YS, rows, XS * width) for part in parts]
+    pairs = len(PAIRS) * 2
+    return pl.pallas_call(
+        scatter_kernel,
+        out_shape=[jax.ShapeDtypeStruct((rows, width), jnp.float32)] * 3,
+        in_specs=[HBM] * 3,
+        out_specs=[VMEM] * 3,
+        scratch_shapes=[
+            pltpu.VMEM((3, 2, ZS, rows, width), jnp.bfloat16),
+            pltpu.VMEM((3, 2, ZS, rows, width), jnp.bfloat16),
+            pltpu.VMEM((3, ZS, rows, width), jnp.bfloat16),
+            pltpu.VMEM((3, 3, rows, width), jnp.bfloat16),
+            pltpu.SemaphoreType.DMA((pairs * 6,)),
+            pltpu.SemaphoreType.DMA((pairs * 6,)),
+            pltpu.SemaphoreType.DMA((pairs * 2,)),
+        ],
+        compiler_params=pltpu.CompilerParams(
+            collective_id=ident, has_side_effects=True, vmem_limit_bytes=60 * 2**20
+        ),
+        name="scatter_grads",
+    )(*parts)
+
+
+def group_of(kind):
+    z, y, x, core = place()
+    data, tensor = z * YS + y, x * CORES + core
+    if kind == "dp":
+        return ZS * YS, data, lambda i: (i, tensor)
+    if kind == "same_core":
+        return ZS * YS * XS, data * XS + x, lambda i: (i // XS, (i % XS) * CORES + core)
+    return (
+        ZS * YS * XS * CORES,
+        data * XS * CORES + tensor,
+        lambda i: (i // (XS * CORES), i % (XS * CORES)),
+    )
+
+
+def exchange_kernel(kind, gather, blocks, arrived, sends, recvs):
+    count, me, device_of = group_of(kind)
+    targets = [(me + step) % count for step in range(1, count)]
+    greet([device_of(target) for target in targets])
+    copies = []
+    for step, target in enumerate(targets):
+        copy = pltpu.make_async_remote_copy(
+            src_ref=blocks if gather else blocks.at[target],
+            dst_ref=arrived.at[me],
+            send_sem=sends.at[step],
+            recv_sem=recvs.at[step],
+            device_id=device_of(target),
+            device_id_type=MESH_ID,
+        )
+        copy.start()
+        copies.append(copy)
+    arrived[me] = blocks[...] if gather else blocks[me]
+    for copy in copies:
+        copy.wait_send()
+    for copy in copies:
+        copy.wait_recv()
+
+
+def exchange(blocks, kind, ident, gather=False):
+    count = {"dp": ZS * YS, "same_core": ZS * YS * XS, "all": ZS * YS * XS * CORES}[kind]
+    shape = blocks.shape if gather else blocks.shape[1:]
+    return pl.pallas_call(
+        partial(exchange_kernel, kind, gather),
+        out_shape=jax.ShapeDtypeStruct((count,) + shape, blocks.dtype),
+        in_specs=[VMEM],
+        out_specs=VMEM,
+        scratch_shapes=[
+            pltpu.SemaphoreType.DMA((count - 1,)),
+            pltpu.SemaphoreType.DMA((count - 1,)),
+        ],
+        compiler_params=pltpu.CompilerParams(collective_id=ident, has_side_effects=True),
+        name="exchange_" + kind,
+    )(blocks)
+
+
+QUARTER = HEAD // 4
+BLOCK = 256
+
+
+def turn(values, tables, back):
+    cosine, to_left, to_right = tables
+    swapped = (
+        pltpu.roll(values, LANES - QUARTER, axis=1) * to_left
+        + pltpu.roll(values, QUARTER, axis=1) * to_right
+    )
+    return values * cosine - swapped if back else values * cosine + swapped
+
+
+def attend_kernel(heads, scale, *refs):
+    projected, (cos_ref, left_ref, right_ref, hide_ref) = refs[:2], refs[2:6]
+    out_refs = refs[6:8]
+    query_ref, key_ref, value_ref, logsum_ref, held = refs[8:]
+    slots = cos_ref.shape[0]
+    per = heads // 2
+    blocks = slots // BLOCK
+
+    def prepare(i, carry):
+        at = pl.ds(pl.multiple_of(i * BLOCK, BLOCK), BLOCK)
+        tables = cos_ref[at, :], left_ref[at, :], right_ref[at, :]
+        hide = hide_ref[at, :]
+        lane = lax.broadcasted_iota(jnp.int32, (BLOCK, LANES), 1)
+        for head in range(heads):
+            source, local = projected[head // per], head % per
+            for part, target in enumerate((query_ref, key_ref, value_ref)):
+                start = (part * per + local) * HEAD
+                values = source[at, start : start + LANES]
+                if part == 2:
+                    values = jnp.where(lane < HEAD, values, 0.0)
+                else:
+                    values = turn(values, tables, False)
+                    values = values + (jnp.where(lane == HEAD, 1.0, 0.0) if part == 0 else hide)
+                target[head, at, :] = values.astype(jnp.bfloat16)
+        return carry
+
+    lax.fori_loop(0, blocks, prepare, 0)
+
+    def attend(i, carry):
+        head, block = i // blocks, i % blocks
+        at = pl.ds(pl.multiple_of(block * BLOCK, BLOCK), BLOCK)
+        scores = contract(query_ref[head, at, :], key_ref[head], 1, 1)
+        highest = jnp.max(scores, 1, keepdims=True)
+        exponent = jnp.exp2((scores - highest) * (scale * LOG2E))
+        denominator = jnp.sum(exponent, 1, keepdims=True)
+        result = jnp.dot(
+            exponent.astype(jnp.bfloat16), value_ref[head], preferred_element_type=jnp.float32
+        )
+        held[head, at, :] = result / denominator
+        logsum_ref[head, at, :] = jnp.broadcast_to(
+            (highest * scale + jnp.log(denominator)) * LOG2E, (BLOCK, LANES)
+        )
+        return carry
+
+    lax.fori_loop(0, heads * blocks, attend, 0)
+
+    def finish(i, carry):
+        at = pl.ds(pl.multiple_of(i * BLOCK, BLOCK), BLOCK)
+        for half in range(2):
+            row = jnp.concatenate(
+                [held[half * per + local, at, :][:, :HEAD] for local in range(per)], 1
+            )
+            out_refs[half][at, :] = row.astype(jnp.bfloat16)
+        return carry
+
+    lax.fori_loop(0, blocks, finish, 0)
+
+
+def attend(projected, tables, heads, scale):
+    slots = projected[0].shape[0]
+    packed = jax.ShapeDtypeStruct((heads, slots, LANES), jnp.bfloat16)
+    half = jax.ShapeDtypeStruct((slots, heads // 2 * HEAD), jnp.bfloat16)
+    results = pl.pallas_call(
+        partial(attend_kernel, heads, scale),
+        out_shape=[
+            half,
+            half,
+            packed,
+            packed,
+            packed,
+            jax.ShapeDtypeStruct((heads, slots, LANES), jnp.float32),
+        ],
+        in_specs=[VMEM] * 6,
+        out_specs=[VMEM] * 6,
+        scratch_shapes=[pltpu.VMEM((heads, slots, LANES), jnp.float32)],
+        compiler_params=pltpu.CompilerParams(vmem_limit_bytes=60 * 2**20),
+        name="attend",
+    )(*projected, *tables)
+    return results[:2], results[2:]
+
+
+def attend_back_kernel(heads, scale, *refs):
+    query_ref, key_ref, value_ref, logsum_ref = refs[:4]
+    grads, (cos_ref, left_ref, right_ref) = refs[4:6], refs[6:9]
+    out_refs = refs[9:11]
+    held, grad_q, grad_k, grad_v = refs[11:]
+    slots = cos_ref.shape[0]
+    per = heads // 2
+    blocks = slots // BLOCK
+
+    def prepare(i, carry):
+        at = pl.ds(pl.multiple_of(i * BLOCK, BLOCK), BLOCK)
+        for head in range(heads):
+            local = head % per
+            piece = grads[head // per][at, local * HEAD : (local + 1) * HEAD]
+            padding = jnp.zeros((BLOCK, LANES - HEAD), piece.dtype)
+            held[head, at, :] = jnp.concatenate([piece, padding], 1)
+        return carry
+
+    lax.fori_loop(0, blocks, prepare, 0)
+
+    def attend(i, carry):
+        head, block = i // blocks, i % blocks
+        at = pl.ds(pl.multiple_of(block * BLOCK, BLOCK), BLOCK)
+        query, grad = query_ref[head, at, :], held[head, at, :]
+        key = key_ref[head]
+        scores = contract(query, key, 1, 1)
+        soft = jnp.exp2(scores * (scale * LOG2E) - logsum_ref[head, at, :1])
+        grad_soft = contract(grad, value_ref[head], 1, 1)
+        value_part = contract(soft.astype(jnp.bfloat16), grad, 0, 0)
+        product = soft * grad_soft
+        inner = jnp.sum(product, 1, keepdims=True)
+        grad_scores = ((product - soft * inner) * scale).astype(jnp.bfloat16)
+        grad_q[head, at, :] = jnp.dot(grad_scores, key, preferred_element_type=jnp.float32)
+        key_part = contract(grad_scores, query, 0, 0)
+
+        @pl.when(block == 0)
+        def _():
+            grad_v[head] = value_part
+            grad_k[head] = key_part
+
+        @pl.when(block > 0)
+        def _():
+            grad_v[head] += value_part
+            grad_k[head] += key_part
+
+        return carry
+
+    lax.fori_loop(0, heads * blocks, attend, 0)
+
+    def finish(i, carry):
+        at = pl.ds(pl.multiple_of(i * BLOCK, BLOCK), BLOCK)
+        tables = cos_ref[at, :], left_ref[at, :], right_ref[at, :]
+        for half in range(2):
+            pieces = []
+            for part, source in enumerate((grad_q, grad_k, grad_v)):
+                for local in range(per):
+                    values = source[half * per + local, at, :]
+                    if part < 2:
+                        values = turn(values, tables, True)
+                    pieces.append(values[:, :HEAD])
+            out_refs[half][at, :] = jnp.concatenate(pieces, 1).astype(jnp.bfloat16)
+        return carry
+
+    lax.fori_loop(0, blocks, finish, 0)
+
+
+def attend_back(saved, grads, tables, heads, scale):
+    slots = grads[0].shape[0]
+    half = jax.ShapeDtypeStruct((slots, 3 * (heads // 2) * HEAD), jnp.bfloat16)
+    wide = pltpu.VMEM((heads, slots, LANES), jnp.float32)
+    return pl.pallas_call(
+        partial(attend_back_kernel, heads, scale),
+        out_shape=[half, half],
+        in_specs=[VMEM] * 9,
+        out_specs=[VMEM] * 2,
+        scratch_shapes=[pltpu.VMEM((heads, slots, LANES), jnp.bfloat16), wide, wide, wide],
+        compiler_params=pltpu.CompilerParams(vmem_limit_bytes=60 * 2**20),
+        name="attend_back",
+    )(*saved, *grads, *tables[:3])
+
+
+def turn_tables(positions, visible):
+    lane = jnp.arange(LANES)
+    inside = lane < HEAD
+    frequency = rope_base ** (-(lane % QUARTER).astype(jnp.float32) / QUARTER)
+    by_row = positions[:, :1].astype(jnp.float32) * frequency
+    by_column = positions[:, 1:].astype(jnp.float32) * frequency
+    angles = jnp.where(lane < HEAD // 2, by_row, by_column)
+    cosine = jnp.where(inside, jnp.cos(angles), 0.0)
+    sine = jnp.where(inside, jnp.sin(angles), 0.0)
+    leads = lane // QUARTER % 2 == 0
+    hide = jnp.where((lane == HEAD) & ~visible[:, None], -1e30, 0.0)
+    return cosine, jnp.where(leads, -sine, 0.0), jnp.where(leads, 0.0, sine), hide
+
+
+def image_device(
+    block_input,
+    conditioning,
+    patch_counts,
+    positions,
+    w_mod,
+    b_mod,
+    w_qkv,
+    b_qkv,
+    w_out,
+    b_out,
+    w_up,
+    b_up,
+    w_down,
+    b_down,
+    cotangent,
+):
+    own_rows, model_width = block_input.shape
+    slot_count = own_rows * CORES
+    shard_rows, _, feat = w_qkv.shape
+    units = w_up.shape[1]
+    heads = CORES * feat // HEAD
+    scale = 1.0 / math.sqrt(HEAD)
+    images = ZS * YS * XS
+    z, y, x, core = place()
+    data = z * YS + y
+    bf16 = jnp.bfloat16
+
+    def swap(values):
+        return lax.ppermute(values, "tensor", CORE_SWAP)
+
+    def both(values):
+        return jnp.concatenate([values, swap(values)], 0)
+
+    def own_sum(terms):
+        return terms[:own_rows] + swap(terms[own_rows:].astype(bf16)).astype(jnp.float32)
+
+    silu_cond = jax.nn.silu(conditioning).astype(bf16)
+    every = exchange(
+        silu_cond.astype(jnp.float32).reshape(-1, LANES), "dp", 0, gather=True
+    ).reshape(images, model_width)
+    silu_rows = lax.dynamic_slice_in_dim(every, data * shard_rows, shard_rows, 1).astype(bf16)
+    mod_matrix = w_mod.astype(bf16).reshape(shard_rows, 6 * feat)
+    mod_part = jnp.dot(silu_rows, mod_matrix, preferred_element_type=jnp.float32)
+    mod_part = mod_part + jnp.where(data == 0, b_mod.reshape(-1), 0.0)
+    mod_part = jnp.broadcast_to(
+        mod_part.reshape(images, 1, 8, -1), (images, CORES, 8, 6 * feat // 8)
+    ).reshape(images * CORES, 8, -1)
+    mod_parts = exchange(mod_part, "all", 1).reshape(ZS * YS, XS * CORES, 6, feat)
+    mod = mod_parts.sum(0).transpose(1, 0, 2).reshape(6, model_width)
+    shift_one, scale_one, gate_one, shift_two, scale_two, gate_two = (mod[i] for i in range(6))
+
+    shards = [
+        jnp.concatenate([w_qkv.reshape(shard_rows, 3 * feat), w_out.T], 1).astype(bf16),
+        w_up.astype(bf16),
+        w_down.T.astype(bf16),
+    ]
+    first, up_full, down_full = gather_weights(shards, 2)
+    biases = jnp.concatenate([b_qkv.reshape(-1), b_up])
+    other_biases = lax.ppermute(biases, "tensor", X_SWAP)
+    low_biases = jnp.where(x == 0, biases, other_biases)
+    high_biases = jnp.where(x == 0, other_biases, biases)
+    qkv_width = 3 * feat
+    joined = first.shape[1] // XS
+
+    own_slots = core * own_rows + jnp.arange(own_rows)
+    other_slots = (1 - core) * own_rows + jnp.arange(own_rows)
+    slots = jnp.concatenate([own_slots, other_slots])
+    visible = slots < lax.dynamic_index_in_dim(patch_counts, x, 0, False)
+    image_start = x * slot_count
+    places = jnp.concatenate(
+        [
+            lax.dynamic_slice_in_dim(positions, image_start + core * own_rows, own_rows, 0),
+            lax.dynamic_slice_in_dim(positions, image_start + (1 - core) * own_rows, own_rows, 0),
+        ]
+    )
+    tables = turn_tables(places, visible)
+
+    normal_one, inverse_one = row_norm(block_input)
+    hidden_one = both((normal_one * (1.0 + scale_one) + shift_one).astype(bf16))
+    projected = []
+    for half, bias in enumerate((low_biases, high_biases)):
+        matrix = first[:, half * joined : half * joined + 8 * LANES]
+        row = jnp.pad(bias[:qkv_width], (0, 8 * LANES - qkv_width))
+        projected.append(jnp.dot(hidden_one, matrix, preferred_element_type=jnp.float32) + row)
+    attended, saved = attend(projected, tables, heads, scale)
+    out_parts = [first[:, half * joined + qkv_width : (half + 1) * joined] for half in range(2)]
+    branch_one = (
+        own_sum(contract(attended[0], out_parts[0], 1, 1) + contract(attended[1], out_parts[1], 1, 1))
+        + b_out
+    )
+    middle = block_input + gate_one * branch_one
+    normal_two, inverse_two = row_norm(middle)
+    hidden_two = both((normal_two * (1.0 + scale_two) + shift_two).astype(bf16))
+    bias_up = jnp.concatenate([low_biases[qkv_width:], high_biases[qkv_width:]])
+    up_pre = jnp.dot(hidden_two, up_full, preferred_element_type=jnp.float32) + bias_up
+    activated = gelu_tanh(up_pre).astype(bf16)
+    branch_two = own_sum(contract(activated, down_full, 1, 1)) + b_down
+    block_output = middle + gate_two * branch_two
+
+    def norm_back(grad_hidden, normal, inverse, factor):
+        grad_normal = grad_hidden * (1.0 + factor)
+        mean_plain = jnp.mean(grad_normal, 1, keepdims=True)
+        mean_cross = jnp.mean(grad_normal * normal, 1, keepdims=True)
+        return inverse[:, None] * (grad_normal - mean_plain - normal * mean_cross)
+
+    def column_sum(values):
+        return jnp.sum(values.astype(jnp.float32), 0)
+
+    grad_gate_two = jnp.sum(cotangent * branch_two, 0)
+    grad_rows_two = both((cotangent * gate_two).astype(bf16))
+    grad_bdown = column_sum(grad_rows_two)
+    grad_down = contract(grad_rows_two, activated, 0, 0).astype(bf16)
+    grad_activated = jnp.dot(grad_rows_two, down_full, preferred_element_type=jnp.float32)
+    grad_up = jax.vjp(gelu_tanh, up_pre)[1](grad_activated)[0].astype(bf16)
+    grad_bup = column_sum(grad_up)
+    grad_wup = contract(hidden_two, grad_up, 0, 0).astype(bf16)
+    grad_hidden_two = own_sum(contract(grad_up, up_full, 1, 1))
+    grad_shift_two = jnp.sum(grad_hidden_two, 0)
+    grad_scale_two = jnp.sum(grad_hidden_two * normal_two, 0)
+    grad_middle = cotangent + norm_back(grad_hidden_two, normal_two, inverse_two, scale_two)
+    grad_gate_one = jnp.sum(grad_middle * branch_one, 0)
+    grad_rows_one = both((grad_middle * gate_one).astype(bf16))
+    grad_bout = column_sum(grad_rows_one)
+    grad_attended = [
+        jnp.dot(grad_rows_one, part, preferred_element_type=jnp.float32).astype(bf16)
+        for part in out_parts
+    ]
+    grad_projected = attend_back(saved, grad_attended, tables, heads, scale)
+    first_parts, hidden_terms, bias_terms = [], 0.0, []
+    for half in range(2):
+        first_parts.append(contract(hidden_one, grad_projected[half], 0, 0).astype(bf16))
+        first_parts.append(contract(grad_rows_one, attended[half], 0, 0).astype(bf16))
+        matrix = first[:, half * joined : half * joined + qkv_width]
+        hidden_terms = hidden_terms + contract(grad_projected[half], matrix, 1, 1)
+        bias_terms.append(column_sum(grad_projected[half]))
+    grad_first = jnp.concatenate(first_parts, 1)
+    grad_hidden_one = own_sum(hidden_terms)
+    grad_shift_one = jnp.sum(grad_hidden_one, 0)
+    grad_scale_one = jnp.sum(grad_hidden_one * normal_one, 0)
+    grad_input = grad_middle + norm_back(grad_hidden_one, normal_one, inverse_one, scale_one)
+
+    sum_down, sum_up, sum_first = scatter_grads([grad_down, grad_wup, grad_first], 3)
+    grad_wqkv = sum_first[:, :qkv_width].reshape(shard_rows, 3, feat)
+    grad_wout = sum_first[:, qkv_width:].T
+    grad_wdown = sum_down.T
+
+    grad_mod = jnp.stack(
+        [
+            grad_shift_one,
+            grad_scale_one,
+            grad_gate_one,
+            grad_shift_two,
+            grad_scale_two,
+            grad_gate_two,
+        ]
+    )
+    grad_mod = (grad_mod + swap(grad_mod)).astype(bf16).astype(jnp.float32)
+    grad_mod = grad_mod.reshape(6, XS, CORES, feat)
+    grad_mod = lax.dynamic_index_in_dim(grad_mod, core, 2, False)
+    small = 6 * feat + qkv_width + units + 2 * model_width
+    lines = -(-small // LANES)
+    sends = []
+    for half in range(2):
+        flat = jnp.concatenate(
+            [
+                grad_mod[:, half].reshape(-1),
+                bias_terms[half],
+                grad_bup[half * units : (half + 1) * units],
+                grad_bout,
+                grad_bdown,
+            ]
+        )
+        sends.append(jnp.pad(flat, (0, lines * LANES - small)).reshape(1, lines, LANES))
+    blocks = jnp.broadcast_to(jnp.stack(sends, 1), (ZS * YS, 2, lines, LANES))
+    small_all = exchange(blocks.reshape(images, lines, LANES), "same_core", 4).reshape(images, -1)
+    mod_all = small_all[:, : 6 * feat]
+    summed = jnp.sum(small_all, 0)
+    grad_bmod = summed[: 6 * feat].reshape(6, feat)
+    offset = 6 * feat
+    grad_bqkv = summed[offset : offset + qkv_width].reshape(3, feat)
+    offset += qkv_width
+    grad_bup = summed[offset : offset + units]
+    offset += units
+    grad_bout = summed[offset : offset + model_width]
+    grad_bdown = summed[offset + model_width : offset + 2 * model_width]
+    mod_all = mod_all.astype(bf16)
+    grad_wmod = contract(silu_rows, mod_all, 0, 0).reshape(shard_rows, 6, feat)
+    silu_part = contract(mod_all, mod_matrix, 1, 1).reshape(ZS * YS, 1, -1)
+    silu_part = jnp.pad(silu_part, ((0, 0), (0, 0), (0, 8 * LANES - XS * shard_rows)))
+    silu_part = jnp.broadcast_to(silu_part, (ZS * YS, XS * CORES, 8 * LANES))
+    silu_all = exchange(silu_part.reshape(-1, 8, LANES), "all", 5)
+    silu_all = silu_all.reshape(ZS * YS, XS * CORES, -1)[:, :, : XS * shard_rows].sum(1)
+    grad_silu = silu_all.reshape(ZS * YS, XS, shard_rows).transpose(1, 0, 2).reshape(XS, model_width)
+    grad_cond = jax.vjp(jax.nn.silu, conditioning)[1](grad_silu)[0]
+    return (
+        block_output,
+        grad_input,
+        grad_cond,
+        grad_wmod,
+        grad_bmod,
+        grad_wqkv,
+        grad_bqkv,
+        grad_wout,
+        grad_bout,
+        sum_up,
+        grad_bup,
+        grad_wdown,
+        grad_bdown,
+    )
+
+
 def solution(mesh):
+    body = image_device if image_per_chip(mesh) else per_device
     placed = (
         P(("dp", "tensor"), None),
         P("dp", None),
@@ -343,7 +1120,7 @@
         P(("dp", "tensor"), None),
     )
     return jax.shard_map(
-        per_device,
+        body,
         mesh=mesh,
         in_specs=placed,
         out_specs=(

time: 1690 us -> 723 us (0.43)
  waiting for transfers between devices: 962 us -> 0.03 us
  Pallas kernels: 0 us -> 473 us
  matrix products: 303 us -> 122 us
  local copies, waits for them, and re-layouts: 217 us -> 58.6 us
  blocking collectives: 100 us -> 0 us
  other arithmetic: 79.3 us -> 54.1 us
    reduce_scatter x9 -> x0, waiting for transfers between devices: 601 us -> none  [the longest x2 154 us: input_sum(): lax.psum_scatter(partial_terms, 'tensor', scatter_dimension=0, tiled=True)]
    pallas_call x0 -> x8, Pallas kernels: none -> 473 us  [the longest x1 168 us: scatter_grads(): pl.pallas_call(scatter_kernel, out_shape=[jax.ShapeDtypeStruct((rows, wid...]
    all_gather x8 -> x0, waiting for transfers between devices: 360 us -> none  [the longest x2 90.4 us: norm_gather(): rows_group = lax.all_gather(rows_local, 'tensor', axis=0, tiled=True)]
    dot_general x29 -> x7, matrix products: 214 us -> 51.2 us  [the longest x1 17.2 us: image_device(): jnp.dot(grad_rows_two, down_full, preferred_element_type=jnp.float32)]
    dynamic_update_slice x12 -> x0, local copies, waits for them, and re-layouts: 130 us -> none  [per_device(): lax.map(partial(attend_forward, factor), (per_image(query_rows), per_imag...]
    all_gather x2 -> x0, blocking collectives: 55.6 us -> none  [the longest x1 37.9 us: per_device(): lax.all_gather(w_out.astype(jnp.bfloat16), 'dp', axis=1, tiled=True)]
    psum x2 -> x0, blocking collectives: 44.6 us -> none  [the longest x1 38.3 us: per_device(): lax.psum((grad_bmod_local, grad_bqkv_local, grad_bout_local, grad_bup_loc...]
    convert_element_type x14 -> x8, other arithmetic: 32.1 us -> 7.24 us  [the longest x1 2.16 us: image_device(): hidden_one = both((normal_one * (1.0 + scale_one) + shift_one).astype(bf16))]
  transfers between devices with their start and end apart: 18 -> 10, of which waited for: 17 -> 0; matrix products, arithmetic and copies ran while one was open for 8% -> 15% of each run, Pallas kernels for 0% -> 49%
where the time goes in v1:
time: 723 us; the launch traced here: 714 us
  Pallas kernels  473 us (65%)
  matrix products  122 us (17%)
  local copies, waits for them, and re-layouts  58.6 us (8%)
  other arithmetic  54.1 us (7%)
    pallas_call x1, Pallas kernels, scatter_grads(): pl.pallas_call(scatter_kernel, out_shape=[jax.ShapeDtypeStruct((rows, wid...  168 us
    pallas_call x1, Pallas kernels, gather_weights(): pl.pallas_call(gather_kernel, out_shape=[shape] * 3, in_specs=[VMEM] * 3,...  159 us
    dot_general x14, matrix products, contract(): lax.dot_general(left, right, (((left_dim,), (right_dim,)), ((), ())), pre...  70.4 us
    pallas_call x1, Pallas kernels, attend(): pl.pallas_call(partial(attend_kernel, heads, scale), out_shape=[half, hal...  50.2 us
    pallas_call x1, Pallas kernels, attend_back(): pl.pallas_call(partial(attend_back_kernel, heads, scale), out_shape=[half...  49.6 us
    pallas_call x4, Pallas kernels, exchange(): pl.pallas_call(partial(exchange_kernel, kind, gather), out_shape=jax.Shap...  45.9 us
    dot_general x1, matrix products, image_device(): jnp.dot(grad_rows_two, down_full, preferred_element_type=jnp.float32)  17.2 us
  transfers between devices with their start and end apart: 10, of which 0 were waited for; matrix products, arithmetic and copies ran while one was open for 15% of the time, Pallas kernels for 49%

profile of v1, /device:TPU:0, one launch (start us, length us, event | category | flops | bytes accessed | tf_op | source)
XLA Modules:
  0.0 714.3 jit_solution(2405543356696624161)
XLA Ops:
  9.3 8.6 %exchange_dp.1 = f32[8,18,128]{2,1,0:T(8,128)} custom-call(f32[18,128]{1,0:T(8,128)} %reshape.252.blocks), custom_call_target="tpu_custom_call" | custom-call | tf_op jit(solution)/shard_map/exchange_dp/pallas_call | solution.py:688
  23.1 11.8 %exchange_all.2 = f32[32,8,216]{2,1,0:T(8,128)} custom-call(f32[32,8,216]{2,1,0:T(8,128)} %bitcast.58), custom_call_target="tpu_custom_call" | custom-call | tf_op jit(solution)/shard_map/exchange_all/pallas_call | solution.py:688
  54.4 4.0 fusion.26
  60.9 159.1 %gather_weights.1 = (bf16[4,2,144,2304]{3,2,1,0:T(8,128)(2,1)}, bf16[4,2,144,2304]{3,2,1,0:T(8,128)(2,1)}, bf16[4,2,144,2304]{3,2,1,0:T(8,128)(2,1)}) custom-call(bf16[144,1152]{1,0:T(8,128)(2,1)} %pad_maximum_fusion.11.refs_0_, bf16[144,1152]{1,0:T(8,128)(2,1)} %convert_element_type.124.refs_1_, bf16[144,1152]{1,0:T(8,128)(2,1)} %convert_bitcast_fusion.refs_2_), custom_call_target="tpu_custom_call" | custom-call | tf_op jit(solution)/shard_map/gather_weights/pallas_call | solution.py:474
  221.4 7.2 %broadcast_add_fusion.refs_1_ = f32[1024,1024]{1,0:T(8,128)} fusion(f32[1024]{0:T(1024)S(1)} %get-tuple-element.140, bf16[1152,2304]{1,0:T(8,128)(2,1)} %bitcast.61, bf16[512,1152]{1,0:T(8,128)(2,1)} %collective-permute-done, bf16[512,1152]{1,0:T(8,128)(2,1)} %add_convert_fusion.1), kind=kOutput, calls=%fused_computation.62 | convolution fusion | flops 2421686272 | bytes 8916992 | tf_op jit(solution)/shard_map/dot_general | solution.py:975
  228.6 7.2 %broadcast_add_fusion.1.refs_0_ = f32[1024,1024]{1,0:T(8,128)} fusion(f32[1024]{0:T(1024)S(1)} %get-tuple-element.141, bf16[1152,2304]{1,0:T(8,128)(2,1)} %bitcast.62, bf16[512,1152]{1,0:T(8,128)(2,1)} %collective-permute-done, bf16[512,1152]{1,0:T(8,128)(2,1)} %add_convert_fusion.1), kind=kOutput, calls=%fused_computation.63 | convolution fusion | flops 2421686272 | bytes 8916992 | tf_op jit(solution)/shard_map/dot_general | solution.py:975
  235.9 50.2 %attend.1 = (bf16[1024,288]{1,0:T(8,128)(2,1)}, bf16[1024,288]{1,0:T(8,128)(2,1)}, bf16[8,1024,128]{2,1,0:T(8,128)(2,1)}, bf16[8,1024,128]{2,1,0:T(8,128)(2,1)},...) custom-call(f32[1024,1024]{1,0:T(8,128)} %broadcast_add_fusion.1.refs_0_, ...), custom_call_target="tpu_custom_call" | custom-call | tf_op jit(solution)/shard_map/attend/pallas_call | solution.py:777
  309.7 12.3 %fusion.19 = f32[1024,2304]{1,0:T(8,128)} fusion(bf16[1152,2304]{1,0:T(8,128)(2,1)} %bitcast.79, bf16[512,1152]{1,0:T(8,128)(2,1)} %collective-permute-done.3, bf16[512,1152]{1,0:T(8,128)(2,1)} %add_convert_fusion), kind=kOutput, calls=%fused_computation.69 | convolution fusion | flops 5440536576 | bytes 17104896 | tf_op jit(solution)/shard_map/dot_general | solution.py:986
  322.0 10.8 %fusion.55 = f32[1024,1152]{1,0:T(8,128)S(1)} fusion(bf16[1152,2304]{1,0:T(8,128)(2,1)S(1)} %bitcast.83, f32[1024,2304]{1,0:T(8,128)} %fusion.19, f32[2304]{0:T(1024)S(1)} %pad_maximum_fusion.12), kind=kOutput, calls=%fused_computation.171 | convolution fusion | flops 5459410944 | bytes 19473408 | tf_op jit(solution)/shard_map/dot_general | solution.py:44
  332.9 17.2 %convert_reduce_fusion = (f32[2304]{0:T(1024)S(1)}, bf16[1024,2304]{1,0:T(8,128)(2,1)}) fusion(bf16[1152,2304]{1,0:T(8,128)(2,1)S(1)} %bitcast.84, bf16[512,1152]{1,0:T(8,128)(2,1)} %collective-permute-done.5, bf16[512,1152]{1,0:T(8,128)(2,1)S(1)} %multiply_convert_fusion.2, f32[1024,2304]{1,0:T(8,128)} %fusion.19, f32[2304]{0:T(1024)S(1)} %pad_maximum_fusion.12), kind=kOutput, calls=%fused_computation.12 | convolution fusion | flops 5504235520 | bytes 21841920 | tf_op jit(solution)/shard_map/dot_general | solution.py:1004
  350.1 9.9 %fusion.61 = f32[1024,1152]{1,0:T(8,128)S(1)} fusion(bf16[1024,2304]{1,0:T(8,128)(2,1)} %get-tuple-element.143, bf16[1152,2304]{1,0:T(8,128)(2,1)} %bitcast.80), kind=kOutput, calls=%fused_computation.177 | convolution fusion | flops 5435817984 | bytes 14745600 | tf_op jit(solution)/shard_map/dot_general | solution.py:44
  361.0 11.6 %convolution_convert_fusion.1 = bf16[1152,2304]{1,0:T(8,128)(2,1)} fusion(bf16[512,1152]{1,0:T(8,128)(2,1)} %collective-permute-done.5, bf16[512,1152]{1,0:T(8,128)(2,1)S(1)} %multiply_convert_fusion.2, f32[1024,2304]{1,0:T(8,128)} %fusion.19, f32[2304]{0:T(1024)S(1)} %pad_maximum_fusion.12), kind=kOutput, calls=%fused_computation.5 | convolution fusion | flops 5466783744 | bytes 17114112 | tf_op jit(solution)/shard_map/dot_general | solution.py:44
  374.8 4.5 multiply_reduce_fusion
  380.0 10.6 %convolution_convert_fusion = bf16[1152,2304]{1,0:T(8,128)(2,1)} fusion(bf16[1024,2304]{1,0:T(8,128)(2,1)} %get-tuple-element.143, bf16[512,1152]{1,0:T(8,128)(2,1)} %collective-permute-done.3, bf16[512,1152]{1,0:T(8,128)(2,1)} %add_convert_fusion), kind=kOutput, calls=%fused_computation.4 | convolution fusion | flops 5443190784 | bytes 12386304 | tf_op jit(solution)/shard_map/dot_general | solution.py:44
  405.0 49.6 %attend_back.1 = (bf16[1024,864]{1,0:T(8,128)(2,1)}, bf16[1024,864]{1,0:T(8,128)(2,1)}) custom-call(bf16[8,1024,128]{2,1,0:T(8,128)(2,1)} %get-tuple-element.32.refs_0_, bf16[8,1024,128]{2,1,0:T(8,128)(2,1)} %get-tuple-element.33.refs_1_, bf16[8,1024,128]{2,1,0:T(8,128)(2,1)} %get-tuple-element.34.refs_2_, f32[8,1024,128]{2,1,0:T(8,128)} %get-tuple-element.35.refs_3_, ...), custom_call_target="tpu_custom_call" | custom-call | tf_op jit(solution)/shard_map/attend_back/pallas_call | solution.py:866
  454.5 5.1 fusion.13
  459.7 4.7 convolution_add_fusion.1
  469.0 4.2 convolution_convert_fusion.3
  473.1 4.2 convolution_convert_fusion.2
  480.4 8.6 %copy.54 = bf16[1152,2304]{1,0:T(8,128)(2,1)} copy(bf16[1152,2304]{0,1:T(8,128)(2,1)} %pad_maximum_fusion) | data formatting | bytes 10616832 | tf_op jit(solution)/shard_map/concatenate | solution.py:1027
  489.0 168.1 %scatter_grads.1 = (f32[144,1152]{1,0:T(8,128)}, f32[144,1152]{1,0:T(8,128)}, f32[144,1152]{1,0:T(8,128)}) custom-call(bf16[4,2,144,2304]{3,2,1,0:T(8,128)(2,1)} %bitcast.55, bf16[4,2,144,2304]{3,2,1,0:T(8,128)(2,1)} %bitcast.56, bf16[4,2,144,2304]{3,2,1,0:T(8,128)(2,1)} %bitcast.54), custom_call_target="tpu_custom_call" | custom-call | tf_op jit(solution)/shard_map/scatter_grads/pallas_call | solution.py:627
  671.2 5.0 multiply_add_fusion.2
  677.6 13.2 %exchange_same_core.1 = f32[16,48,128]{2,1,0:T(8,128)} custom-call(f32[16,48,128]{2,1,0:T(8,128)} %bitcast.57), custom_call_target="tpu_custom_call" | custom-call | tf_op jit(solution)/shard_map/exchange_same_core/pallas_call | solution.py:688
  696.3 12.3 %exchange_all.3 = f32[32,8,128]{2,1,0:T(8,128)} custom-call(f32[32,8,128]{2,1,0:T(8,128)} %reshape.240.blocks), custom_call_target="tpu_custom_call" | custom-call | tf_op jit(solution)/shard_map/exchange_all/pallas_call | solution.py:688
  (265 shorter events, 112.5 us)
Async XLA Ops:
  0.7 18.2 %copy-start.13 = (f32[144,6,288]{2,0,1:T(8,128)S(1)}, f32[144,6,288]{2,0,1:T(8,128)}, u32[]{:S(2)}) copy-start(f32[144,6,288]{2,0,1:T(8,128)} %param.19) | copy-start | bytes 2985988
  2.9 217.1 %collective-permute-start.1 = (f32[2016]{0:T(1024)}, f32[2016]{0:T(1024)}, u32[]{:S(2)}, u32[]{:S(2)}) collective-permute-start(f32[2016]{0:T(1024)} %pad_maximum_fusion.13), channel_id=1, source_target_pairs={{0,2},{2,0},{1,3},{3,1},{4,6},{6,4},{5,7},{7,5},{8,10},{10,8},{9,1... | collective-permute-start | bytes 24200 | tf_op jit(solution)/shard_map/ppermute | solution.py:950
  20.1 22.0 %copy-start = (f32[512,1152]{1,0:T(8,128)S(1)}, f32[512,1152]{1,0:T(8,128)}, u32[]{:S(2)}) copy-start(f32[512,1152]{1,0:T(8,128)} %param.15) | copy-start | bytes 7077892
  22.0 22.2 %copy-start.7 = (bf16[144,1728]{1,0:T(8,128)(2,1)}, bf16[144,1728]{1,0:T(8,128)(2,1)S(1)}, u32[]{:S(2)}) copy-start(bf16[144,1728]{1,0:T(8,128)(2,1)S(1)} %reshape.227) | copy-start | bytes 1492996
  44.2 177.2 %collective-permute-start = (bf16[512,1152]{1,0:T(8,128)(2,1)}, bf16[512,1152]{1,0:T(8,128)(2,1)}, u32[]{:S(2)}, u32[]{:S(2)}) collective-permute-start(bf16[512,1152]{1,0:T(8,128)(2,1)} %add_convert_fusion.1), channel_id=1, source_target_pairs={{0,1},{1,0},{2,3},{3,2},{4,5},{5,4},{6,7},{7,6},{8,9},{9,8},{10,11... | collective-permute-start | bytes 3538952 | tf_op jit(solution)/shard_map/ppermute | solution.py:920
  54.4 165.7 %copy-start.38 = (f32[1152]{0:T(1024)S(1)}, f32[1152]{0:T(1024)}, u32[]{:S(2)}) copy-start(f32[1152]{0:T(1024)} %param.26) | copy-start | bytes 13828
  54.4 167.0 %copy-start.54 = (pred[1024]{0:T(1024)(128)(4,1)S(1)}, pred[1024]{0:T(1024)(128)(4,1)}, u32[]{:S(2)}) copy-start(pred[1024]{0:T(1024)(128)(4,1)} %constant.116.clone.1) | copy-start | bytes 3076
  295.4 4.7 collective-permute-start.2
  297.3 10.0 %collective-permute-start.5 = (bf16[512,1152]{1,0:T(8,128)(2,1)S(1)}, bf16[512,1152]{1,0:T(8,128)(2,1)}, u32[]{:S(2)}, u32[]{:S(2)}) collective-permute-start(bf16[512,1152]{1,0:T(8,128)(2,1)S(1)} %multiply_convert_fusion.2), channel_id=1, source_target_pairs={{0,1},{1,0},{2,3},{3,2},{4,5},{5,4},{6,7},{7,6},{8,9},{9,8},{10,11... | collective-permute-start | bytes 3538952 | tf_op jit(solution)/shard_map/ppermute | solution.py:920
  305.7 4.0 collective-permute-start.3
  307.3 14.7 %slice-start.2 = ((s8[5308416]{0:T(1024)(128)(4,1)}), s8[4194304]{0:T(1024)(128)(4,1)S(1)}, s32[]{:S(2)}) async-start(s8[5308416]{0:T(1024)(128)(4,1)} %bitcast.81), calls=%async_computation.2 | async-start | bytes 8388608
  309.7 12.3 %slice-start.3 = ((s8[5308416]{0:T(1024)(128)(4,1)}), s8[1114112]{0:T(1024)(128)(4,1)S(1)}, s32[]{:S(2)}) async-start(s8[5308416]{0:T(1024)(128)(4,1)} %bitcast.81), calls=%async_computation.3 | async-start | bytes 2228224
  360.0 14.4 %slice-start = ((s8[4718592]{0:T(1024)(128)(4,1)}), s8[4194304]{0:T(1024)(128)(4,1)S(1)}, s32[]{:S(2)}) async-start(s8[4718592]{0:T(1024)(128)(4,1)} %bitcast.52), calls=%async_computation | async-start | bytes 8388608
  360.3 12.9 %copy-start.2 = (f32[512,1152]{1,0:T(8,128)S(1)}, f32[512,1152]{1,0:T(8,128)}, u32[]{:S(2)}) copy-start(f32[512,1152]{1,0:T(8,128)} %copy-done.1) | copy-start | bytes 7077892
  360.3 12.9 %copy-start.44 = (f32[512]{0:T(512)S(1)}, f32[512]{0:T(512)}, u32[]{:S(2)}) copy-start(f32[512]{0:T(512)} %copy-done.43) | copy-start | bytes 6148
  360.3 12.9 %copy-start.46 = (f32[512]{0:T(512)S(1)}, f32[512]{0:T(512)}, u32[]{:S(2)}) copy-start(f32[512]{0:T(512)} %copy-done.45) | copy-start | bytes 6148
  360.3 14.1 %slice-start.1 = ((s8[4718592]{0:T(1024)(128)(4,1)}), s8[524288]{0:T(1024)(128)(4,1)S(1)}, s32[]{:S(2)}) async-start(s8[4718592]{0:T(1024)(128)(4,1)} %bitcast.52), calls=%async_computation.1 | async-start | bytes 1048576
  360.3 14.0 %collective-permute-start.4 = (bf16[512,1152]{1,0:T(8,128)(2,1)S(1)}, bf16[512,1152]{1,0:T(8,128)(2,1)S(1)}, u32[]{:S(2)}, u32[]{:S(2)}) collective-permute-start(bf16[512,1152]{1,0:T(8,128)(2,1)S(1)} %slice.298), channel_id=1, source_target_pairs={{0,1},{1,0},{2,3},{3,2},{4,5},{5,4},{6,7},{7,6},{8,9},{9,8},{10,11... | collective-permute-start | bytes 3538952 | tf_op jit(solution)/shard_map/ppermute | solution.py:920
  360.9 12.3 %collective-permute-start.6 = (bf16[512,1152]{1,0:T(8,128)(2,1)S(1)}, bf16[512,1152]{1,0:T(8,128)(2,1)S(1)}, u32[]{:S(2)}, u32[]{:S(2)}) collective-permute-start(bf16[512,1152]{1,0:T(8,128)(2,1)S(1)} %slice.297), channel_id=1, source_target_pairs={{0,1},{1,0},{2,3},{3,2},{4,5},{5,4},{6,7},{7,6},{8,9},{9,8},{10,11... | collective-permute-start | bytes 3538952 | tf_op jit(solution)/shard_map/ppermute | solution.py:920
  379.5 12.9 %collective-permute-start.7 = (bf16[512,1152]{1,0:T(8,128)(2,1)S(1)}, bf16[512,1152]{1,0:T(8,128)(2,1)S(1)}, u32[]{:S(2)}, u32[]{:S(2)}) collective-permute-start(bf16[512,1152]{1,0:T(8,128)(2,1)S(1)} %multiply_convert_fusion.1), channel_id=1, source_target_pairs={{0,1},{1,0},{2,3},{3,2},{4,5},{5,4},{6,7},{7,6},{8,9},{9,8},{10,11... | collective-permute-start | bytes 3538952 | tf_op jit(solution)/shard_map/ppermute | solution.py:920
  465.7 202.0 %collective-permute-start.8 = (bf16[512,1152]{1,0:T(8,128)(2,1)}, bf16[512,1152]{1,0:T(8,128)(2,1)}, u32[]{:S(2)}, u32[]{:S(2)}) collective-permute-start(bf16[512,1152]{1,0:T(8,128)(2,1)} %slice.296), channel_id=1, source_target_pairs={{0,1},{1,0},{2,3},{3,2},{4,5},{5,4},{6,7},{7,6},{8,9},{9,8},{10,11... | collective-permute-start | bytes 3538952 | tf_op jit(solution)/shard_map/ppermute | solution.py:920
  671.1 5.1 collective-permute-start.9
  676.2 16.6 %copy-start.8 = (bf16[144,1728]{1,0:T(8,128)(2,1)S(1)}, bf16[144,1728]{1,0:T(8,128)(2,1)}, u32[]{:S(2)}) copy-start(bf16[144,1728]{1,0:T(8,128)(2,1)} %copy-done.7) | copy-start | bytes 1492996
  677.6 32.2 %copy-start.33 = (f32[2,1152]{1,0:T(2,128)S(1)}, f32[2,1152]{1,0:T(2,128)}, u32[]{:S(2)}) copy-start(f32[2,1152]{1,0:T(2,128)} %param.16) | copy-start | bytes 27652
  (46 other events, 181.0 us)

commit v2 on v1

--- a/solution.py
+++ b/solution.py
@@ -332,14 +332,6 @@
 CORE_SWAP = [(0, 1), (1, 0), (2, 3), (3, 2)]
 X_SWAP = [(0, 2), (2, 0), (1, 3), (3, 1)]
 LOG2E = 1.0 / math.log(2.0)
-PAIRS = (
-    (0, 0, 32, 32),
-    (0, 64, 48, 32),
-    (1, 0, 32, 32),
-    (1, 64, 32, 48),
-    (2, 0, 32, 32),
-    (2, 64, 48, 32),
-)
 HBM = pl.BlockSpec(memory_space=pl.ANY)
 VMEM = pl.BlockSpec(memory_space=pltpu.VMEM)
 
@@ -373,271 +365,454 @@
     pl.semaphore_wait(barrier, len(targets))
 
 
-def grid_peers():
+GATHER_STEPS, SCATTER_STEPS = 5, 6
+
+
+def grouped(matrices, rows, unit):
+    groups = []
+    for matrix in matrices:
+        for row in range(0, rows, 3 * unit):
+            short = len(groups) % 2
+            groups.append(
+                [
+                    (matrix, row, unit, 2),
+                    (matrix, row + unit, unit, 3),
+                    (matrix, row + 2 * unit, unit, short),
+                ]
+            )
+    return groups
+
+
+def numbered(groups):
+    chunks, members = [], []
+    for group in groups:
+        members.append(range(len(chunks), len(chunks) + len(group)))
+        chunks.extend(group)
+    return chunks, members
+
+
+def ticks_of(members, steps, act):
+    def tick(time):
+        for group, numbers in enumerate(members):
+            step = time - group
+            if 0 <= step < steps:
+                for number in numbers:
+                    act(number, step)
+
+    return [partial(tick, time) for time in range(len(members) + steps - 1)]
+
+
+def gather_plan(groups, shards, wholes, sends, recvs, local):
+    chunks, members = numbered(groups)
     z, y, x, core = place()
-    peers = [device(z, y, 1 - x, core), device(z, 1 - y, x, core)]
-    return peers + [device(flip_z(z, step), y, x, core) for step in (1, 2, 3)]
-
-
-def chunk_list():
-    chunks = []
-    for matrix, row, first, second in PAIRS:
-        chunks.append(((matrix, row, first, 0), (matrix, row + first, second, 1)))
-    return chunks
-
-
-def remote(source, target_ref, sems, index, where):
-    return pltpu.make_async_remote_copy(
-        src_ref=source,
-        dst_ref=target_ref,
-        send_sem=sems[0].at[index],
-        recv_sem=sems[1].at[index],
-        device_id=where,
-        device_id_type=MESH_ID,
-    )
-
-
-def gather_kernel(*refs):
-    shards, wholes = refs[:3], refs[3:6]
-    sends, recvs, local = refs[6:]
-    sems = (sends, recvs)
-    z, y, x, core = place()
-    peers = grid_peers()
+    inner = jnp.logical_or(z == 1, z == 2)
     width = shards[0].shape[1]
-    greet(peers)
     mine = pl.ds(pl.multiple_of(x * width, LANES), width)
-    keeps = []
-    for matrix in range(3):
-        keep = pltpu.make_async_copy(
+    every = slice(None)
+    at_x, at_y = device(z, y, 1 - x, core), device(z, 1 - y, x, core)
+    beside, mirror = device(flip_z(z, 1), y, x, core), device(3 - z, y, x, core)
+    pair = pl.ds(z // 2 * 2, 2)
+    far = pl.ds(2 - z // 2 * 2, 2)
+
+    def copy(number, send, recv, source, target, where):
+        return pltpu.make_async_remote_copy(
+            src_ref=source,
+            dst_ref=target,
+            send_sem=sends.at[number * 5 + send],
+            recv_sem=recvs.at[number * 4 + recv],
+            device_id=where,
+            device_id_type=MESH_ID,
+        )
+
+    def moves(number):
+        matrix, row, rows, route = chunks[number]
+        whole, span = wholes[matrix], pl.ds(row, rows)
+        own, shard = whole.at[z, y, span, mine], shards[matrix].at[span, :]
+        lines, columns = (every if route == 3 else y), (every if route == 2 else mine)
+        made = {}
+        near = shard if route < 2 else whole.at[z, lines, span, columns]
+        near_to = own if route < 2 else near
+        made["near"] = partial(copy, number, 0, 0, near, near_to, beside)
+        both = whole.at[pair, lines, span, columns]
+        made["mirror"] = partial(copy, number, 1, 1, both, both, mirror)
+        there = whole.at[far, lines, span, columns]
+        made["forward"] = partial(copy, number, 2, 1, there, there, beside)
+        if route < 2:
+            column = whole.at[:, y, span, mine]
+            made["second"] = partial(copy, number, 3, 2, column, column, at_x if route == 0 else at_y)
+        else:
+            made["first"] = partial(copy, number, 3, 2, shard, own, at_x if route == 2 else at_y)
+        if route in (0, 2):
+            last = whole.at[:, y, span, :]
+        else:
+            last = whole.at[:, :, span, mine]
+        made["third"] = partial(copy, number, 4, 3, last, last, at_y if route in (0, 2) else at_x)
+        return made
+
+    def keep(matrix):
+        return pltpu.make_async_copy(
             shards[matrix], wholes[matrix].at[z, y, :, mine], local.at[matrix]
         )
-        keep.start()
-        keeps.append(keep)
-    chunks = chunk_list()
-    copies = {}
-
-    def launch(number, stage, chunk):
-        matrix, row, rows, route = chunk
-        whole, span = wholes[matrix], pl.ds(row, rows)
-        base = number * 5
-        if stage == 0:
-            made = [
-                remote(
-                    shards[matrix].at[span, :],
-                    whole.at[z, y, span, mine],
-                    sems,
-                    base + step,
-                    peers[2 + step],
+
+    kept = []
+
+    def ready(number):
+        matrix = chunks[number][0]
+        if matrix not in kept:
+            kept.append(matrix)
+            keep(matrix).wait()
+
+    def act(number, step):
+        made = moves(number)
+        straight = chunks[number][3] < 2
+        if step == 0:
+            made["near" if straight else "first"]().start()
+        elif step == 1:
+            ready(number)
+            if straight:
+                made["near"]().wait_recv()
+                pl.when(inner)(lambda: made["mirror"]().start())
+            else:
+                made["first"]().wait_recv()
+                made["near"]().start()
+        elif step == 2:
+            if straight:
+                made["mirror"]().wait_recv()
+                pl.when(inner)(lambda: made["forward"]().start())
+                made["second"]().start()
+            else:
+                made["near"]().wait_recv()
+                pl.when(inner)(lambda: made["mirror"]().start())
+        elif step == 3:
+            if straight:
+                made["second"]().wait_recv()
+            else:
+                made["mirror"]().wait_recv()
+                pl.when(inner)(lambda: made["forward"]().start())
+            made["third"]().start()
+        else:
+            made["third"]().wait_recv()
+
+    def start():
+        for matrix in sorted({chunk[0] for chunk in chunks}):
+            keep(matrix).start()
+
+    def finish():
+        for number in range(len(chunks)):
+            made = moves(number)
+            for name in made:
+                if name not in ("mirror", "forward"):
+                    made[name]().wait_send()
+
+            def rest(made=made):
+                made["mirror"]().wait_send()
+                made["forward"]().wait_send()
+
+            pl.when(inner)(rest)
+
+    return start, ticks_of(members, GATHER_STEPS, act), finish
+
+
+def gather_scratch(groups, matrices):
+    count = sum(len(group) for group in groups)
+    return [
+        pltpu.SemaphoreType.DMA((count * 5,)),
+        pltpu.SemaphoreType.DMA((count * 4,)),
+        pltpu.SemaphoreType.DMA((matrices,)),
+    ]
+
+
+def scatter_plan(groups, parts, sums, buffers, sends, recvs, local):
+    chunks, members = numbered(groups)
+    own, first_in, second_in, outer_in, mirror_in, near_in, last_in = buffers
+    z, y, x, core = place()
+    inner = jnp.logical_or(z == 1, z == 2)
+    outer = jnp.logical_or(z == 0, z == 3)
+    width = sums[0].shape[1]
+    mine = pl.ds(pl.multiple_of(x * width, LANES), width)
+    theirs = pl.ds(pl.multiple_of((1 - x) * width, LANES), width)
+    at_x, at_y = device(z, y, 1 - x, core), device(z, 1 - y, x, core)
+    z_near = flip_z(z, 1)
+    beside, mirror = device(z_near, y, x, core), device(3 - z, y, x, core)
+    pair_at, far_at = z // 2 * 2, 2 - z // 2 * 2
+    pair, far = pl.ds(pair_at, 2), pl.ds(far_at, 2)
+
+    def copy(number, index, source, target, where):
+        return pltpu.make_async_remote_copy(
+            src_ref=source,
+            dst_ref=target,
+            send_sem=sends.at[number * 6 + index],
+            recv_sem=recvs.at[number * 6 + index],
+            device_id=where,
+            device_id_type=MESH_ID,
+        )
+
+    def moves(number):
+        matrix, row, rows, route = chunks[number]
+        part, span = parts[matrix], pl.ds(row, rows)
+        by_y = route in (0, 2)
+        made = {}
+        for slot in range(2):
+            if by_y:
+                column = mine if slot == 0 else theirs
+                source, kept = part.at[:, 1 - y, span, column], part.at[:, y, span, column]
+            else:
+                line = y if slot == 0 else 1 - y
+                source, kept = part.at[:, line, span, theirs], part.at[:, line, span, mine]
+            made["first", slot] = partial(
+                copy,
+                number,
+                slot,
+                source,
+                first_in.at[matrix, slot, :, span, :],
+                at_y if by_y else at_x,
+            )
+            made["load", slot] = partial(
+                pltpu.make_async_copy,
+                kept, own.at[matrix, slot, :, span, :], local.at[number * 2 + slot]
+            )
+        if route < 2:
+            made["second"] = partial(
+                copy,
+                number,
+                2,
+                own.at[matrix, 1, :, span, :],
+                second_in.at[matrix, :, span, :],
+                at_x if by_y else at_y,
+            )
+            slots = 0
+        else:
+            made["last"] = partial(
+                copy,
+                number,
+                2,
+                own.at[matrix, 1, z, span, :],
+                last_in.at[matrix, span, :],
+                at_x if by_y else at_y,
+            )
+            slots = slice(None)
+        made["outer"] = partial(
+                copy,
+            number,
+            3,
+            own.at[matrix, slots, far, span, :],
+            outer_in.at[matrix, slots, :, span, :],
+            beside,
+        )
+        made["mirror"] = partial(
+                copy,
+            number,
+            4,
+            own.at[matrix, slots, far, span, :],
+            mirror_in.at[matrix, slots, :, span, :],
+            mirror,
+        )
+        made["near"] = partial(
+                copy,
+            number,
+            5,
+            own.at[matrix, slots, z_near, span, :],
+            near_in.at[matrix, slots, span, :],
+            beside,
+        )
+        return made
+
+    def add(rows, row, target, arrived):
+        def one(i, carry):
+            at = pl.ds(pl.multiple_of(row + i * 16, 16), 16)
+            held = own[(*target, at, slice(None))].astype(jnp.float32)
+            incoming = arrived[0][(*arrived[1], at, slice(None))].astype(jnp.float32)
+            own[(*target, at, slice(None))] = (held + incoming).astype(jnp.bfloat16)
+            return carry
+
+        lax.fori_loop(0, rows // 16, one, 0)
+
+    def add_blocks(number, count, target, arrived):
+        matrix, row, rows, route = chunks[number]
+
+        def one(i, carry):
+            ref, index = arrived(i)
+            add(rows, row, (matrix, *target(i)), (ref, (matrix, *index)))
+            return carry
+
+        lax.fori_loop(0, count, one, 0)
+
+    def finalize(number, ref, index):
+        matrix, row, rows, route = chunks[number]
+
+        def one(i, carry):
+            at = pl.ds(pl.multiple_of(row + i * 16, 16), 16)
+            sums[matrix][at, :] = own[matrix, 0, z, at, :].astype(jnp.float32) + ref[
+                (matrix, *index, at, slice(None))
+            ].astype(jnp.float32)
+            return carry
+
+        lax.fori_loop(0, rows // 16, one, 0)
+
+    def act(number, step):
+        made = moves(number)
+        straight = chunks[number][3] < 2
+        count = 2 if straight else 4
+        slots = 1 if straight else 2
+
+        def from_outer():
+            made["outer"]().wait_recv()
+            add_blocks(
+                number,
+                count,
+                lambda i: (i // 2, far_at + i % 2),
+                lambda i: (outer_in, (i // 2, i % 2)),
+            )
+            made["mirror"]().start()
+
+        def from_mirror():
+            made["mirror"]().wait_recv()
+            add_blocks(
+                number,
+                count,
+                lambda i: (i // 2, pair_at + i % 2),
+                lambda i: (mirror_in, (i // 2, i % 2)),
+            )
+
+        if step == 0:
+            for slot in (1, 0):
+                made["first", slot]().start()
+                made["load", slot]().start()
+        elif step == 1:
+            for slot in (1, 0):
+                made["first", slot]().wait_recv()
+                made["load", slot]().wait()
+                add_blocks(
+                    number,
+                    ZS,
+                    lambda i, slot=slot: (slot, i),
+                    lambda i, slot=slot: (first_in, (slot, i)),
                 )
-                for step in range(3)
-            ]
-        elif (stage == 1) == (route == 0):
-            part = whole.at[:, y, span, mine] if stage == 1 else whole.at[:, :, span, mine]
-            made = [remote(part, part, sems, base + 2 + stage, peers[0])]
+                if straight and slot == 1:
+                    made["second"]().start()
+            if not straight:
+                pl.when(outer)(lambda: made["outer"]().start())
+        elif straight:
+            if step == 2:
+                made["second"]().wait_recv()
+                add_blocks(number, ZS, lambda i: (0, i), lambda i: (second_in, (i,)))
+                pl.when(outer)(lambda: made["outer"]().start())
+            elif step == 3:
+                pl.when(inner)(from_outer)
+            elif step == 4:
+                pl.when(inner)(from_mirror)
+                made["near"]().start()
+            else:
+                made["near"]().wait_recv()
+                finalize(number, near_in, (0,))
+        elif step == 2:
+            pl.when(inner)(from_outer)
+        elif step == 3:
+            pl.when(inner)(from_mirror)
+            made["near"]().start()
+        elif step == 4:
+            made["near"]().wait_recv()
+            add_blocks(number, 2, lambda i: (i, z), lambda i: (near_in, (i,)))
+            made["last"]().start()
         else:
-            part = whole.at[:, y, span, mine] if stage == 1 else whole.at[:, y, span, :]
-            made = [remote(part, part, sems, base + 2 + stage, peers[1])]
-        for copy in made:
-            copy.start()
-        copies[number, stage] = made
-
-    def settle(number, stage):
-        for copy in copies[number, stage]:
-            copy.wait_recv()
-
-    total = len(chunks)
-    for tick in range(total + 3):
-        for stage in (2, 1, 0):
-            pair = tick - stage
-            if not 0 <= pair < total:
-                continue
-            for route in range(2):
-                number = pair * 2 + route
-                if stage > 0:
-                    settle(number, stage - 1)
-                if stage == 1 and route == 0 and chunks[pair][0][1] == 0:
-                    keeps[chunks[pair][0][0]].wait()
-                launch(number, stage, chunks[pair][route])
-        pair = tick - 3
-        if 0 <= pair < total:
-            for route in range(2):
-                settle(pair * 2 + route, 2)
-    for made in copies.values():
-        for copy in made:
-            copy.wait_send()
-
-
-def gather_weights(shards, ident):
-    rows, width = shards[0].shape
-    shape = jax.ShapeDtypeStruct((ZS, YS, rows, XS * width), jnp.bfloat16)
-    count = len(PAIRS) * 2 * 5
-    wholes = pl.pallas_call(
-        gather_kernel,
-        out_shape=[shape] * 3,
-        in_specs=[VMEM] * 3,
-        out_specs=[HBM] * 3,
-        scratch_shapes=[
-            pltpu.SemaphoreType.DMA((count,)),
-            pltpu.SemaphoreType.DMA((count,)),
-            pltpu.SemaphoreType.DMA((3,)),
-        ],
+            made["last"]().wait_recv()
+            finalize(number, last_in, ())
+
+    def finish():
+        for number in range(len(chunks)):
+            made = moves(number)
+            for name in made:
+                if name not in ("outer", "mirror") and name[0] != "load":
+                    made[name]().wait_send()
+            pl.when(outer)(lambda made=made: made["outer"]().wait_send())
+            pl.when(inner)(lambda made=made: made["mirror"]().wait_send())
+
+    return ticks_of(members, SCATTER_STEPS, act), finish
+
+
+def scatter_scratch(groups, matrices, rows, width):
+    count = sum(len(group) for group in groups)
+
+    def wide(*lead):
+        return pltpu.VMEM((matrices, *lead, rows, width), jnp.bfloat16)
+
+    return [
+        wide(2, ZS),
+        wide(2, ZS),
+        wide(ZS),
+        wide(2, 2),
+        wide(2, 2),
+        wide(2),
+        wide(),
+        pltpu.SemaphoreType.DMA((count * 6,)),
+        pltpu.SemaphoreType.DMA((count * 6,)),
+        pltpu.SemaphoreType.DMA((count * 2,)),
+    ]
+
+
+def line_peers():
+    z, y, x, core = place()
+    return [
+        device(z, y, 1 - x, core),
+        device(z, 1 - y, x, core),
+        device(flip_z(z, 1), y, x, core),
+        device(3 - z, y, x, core),
+    ]
+
+
+def gather_kernel(groups, matrices, *refs):
+    shards, wholes, scratch = refs[:matrices], refs[matrices : 2 * matrices], refs[2 * matrices :]
+    greet(line_peers())
+    start, ticks, finish = gather_plan(groups, shards, wholes, *scratch)
+    start()
+    for tick in ticks:
+        tick()
+    finish()
+
+
+def whole_shape(shard):
+    rows, width = shard.shape
+    return jax.ShapeDtypeStruct((ZS, YS, rows, XS * width), jnp.bfloat16)
+
+
+def gather_weights(shards, ident, unit=16):
+    count = len(shards)
+    groups = grouped(range(count), shards[0].shape[0], unit)
+    return pl.pallas_call(
+        partial(gather_kernel, groups, count),
+        out_shape=[whole_shape(shard) for shard in shards],
+        in_specs=[VMEM] * count,
+        out_specs=[HBM] * count,
+        scratch_shapes=gather_scratch(groups, count),
         compiler_params=pltpu.CompilerParams(collective_id=ident, has_side_effects=True),
         name="gather_weights",
     )(*shards)
-    return [whole.reshape(ZS * YS * rows, XS * width) for whole in wholes]
-
-
-def scatter_kernel(*refs):
-    parts, sums = refs[:3], refs[3:6]
-    own, first_in, second_in, third_in, sends, recvs, local = refs[6:]
-    sems = (sends, recvs)
-    z, y, x, core = place()
-    peers = grid_peers()
-    width = sums[0].shape[1]
-    greet(peers)
-    mine = pl.ds(pl.multiple_of(x * width, LANES), width)
-    theirs = pl.ds(pl.multiple_of((1 - x) * width, LANES), width)
-    chunks = chunk_list()
-    copies = {}
-    loads = {}
-
-    def launch(number, stage, chunk):
-        matrix, row, rows, route = chunk
-        part, span = parts[matrix], pl.ds(row, rows)
-        base = number * 3
-        if stage == 0:
-            made = []
-            for slot in range(2):
-                if route == 0:
-                    column = mine if slot == 0 else theirs
-                    source = part.at[:, 1 - y, span, column]
-                    kept = part.at[:, y, span, column]
-                    where = peers[1]
-                else:
-                    line = y if slot == 0 else 1 - y
-                    source = part.at[:, line, span, theirs]
-                    kept = part.at[:, line, span, mine]
-                    where = peers[0]
-                copy = remote(source, first_in.at[matrix, slot, :, span, :], sems, base + slot, where)
-                made.append(copy)
-                load = pltpu.make_async_copy(
-                    kept, own.at[matrix, slot, :, span, :], local.at[number * 2 + slot]
-                )
-                load.start()
-                loads[number, slot] = load
-        elif stage == 1:
-            where = peers[0] if route == 0 else peers[1]
-            made = [
-                remote(
-                    own.at[matrix, 1, :, span, :],
-                    second_in.at[matrix, :, span, :],
-                    sems,
-                    base + 2,
-                    where,
-                )
-            ]
-        else:
-            made = [
-                remote(
-                    own.at[matrix, 0, flip_z(z, step), span, :],
-                    third_in.at[matrix, step - 1, span, :],
-                    sems,
-                    third[number] + step - 1,
-                    peers[1 + step],
-                )
-                for step in (1, 2, 3)
-            ]
-        for copy in made:
-            copy.start()
-        copies[number, stage] = made
-
-    third = {n: len(chunks) * 2 * 3 + n * 3 for n in range(len(chunks) * 2)}
-
-    def add_into(target, arrived, rows):
-        def step(i, carry):
-            at = pl.ds(pl.multiple_of(i * 16, 16), 16)
-            target[at, :] = (
-                target[at, :].astype(jnp.float32) + arrived[at, :].astype(jnp.float32)
-            ).astype(jnp.bfloat16)
-            return carry
-
-        lax.fori_loop(0, rows // 16, step, 0)
-
-    def merge(number, stage, chunk):
-        matrix, row, rows, route = chunk
-        span = pl.ds(row, rows)
-        for copy in copies[number, stage]:
-            copy.wait_recv()
-        if stage == 0:
-            for slot in range(2):
-                loads[number, slot].wait()
-
-                def one(i, carry, slot=slot):
-                    add_into(
-                        own.at[matrix, slot, i, span, :],
-                        first_in.at[matrix, slot, i, span, :],
-                        rows,
-                    )
-                    return carry
-
-                lax.fori_loop(0, ZS, one, 0)
-        elif stage == 1:
-
-            def two(i, carry):
-                add_into(own.at[matrix, 0, i, span, :], second_in.at[matrix, i, span, :], rows)
-                return carry
-
-            lax.fori_loop(0, ZS, two, 0)
-        else:
-
-            def step(i, carry):
-                at = pl.ds(pl.multiple_of(row + i * 16, 16), 16)
-                total = own[matrix, 0, z, at, :].astype(jnp.float32)
-                for k in range(3):
-                    total = total + third_in[matrix, k, at, :].astype(jnp.float32)
-                sums[matrix][at, :] = total
-                return carry
-
-            lax.fori_loop(0, rows // 16, step, 0)
-
-    total = len(chunks)
-    for tick in range(total + 3):
-        for stage in (2, 1, 0):
-            pair = tick - stage
-            if not 0 <= pair < total:
-                continue
-            for route in range(2):
-                number = pair * 2 + route
-                if stage > 0:
-                    merge(number, stage - 1, chunks[pair][route])
-                launch(number, stage, chunks[pair][route])
-        pair = tick - 3
-        if 0 <= pair < total:
-            for route in range(2):
-                merge(pair * 2 + route, 2, chunks[pair][route])
-    for made in copies.values():
-        for copy in made:
-            copy.wait_send()
-
-
-def scatter_grads(parts, ident):
-    rows, width = parts[0].shape[0] // (ZS * YS), parts[0].shape[1] // XS
-    parts = [part.reshape(ZS, YS, rows, XS * width) for part in parts]
-    pairs = len(PAIRS) * 2
+
+
+def scatter_kernel(groups, matrices, *refs):
+    parts, sums, scratch = refs[:matrices], refs[matrices : 2 * matrices], refs[2 * matrices :]
+    greet(line_peers())
+    ticks, finish = scatter_plan(groups, parts, sums, scratch[:7], *scratch[7:])
+    for tick in ticks:
+        tick()
+    finish()
+
+
+def split_rows(part):
+    return part.reshape(ZS, YS, part.shape[0] // (ZS * YS), part.shape[1])
+
+
+def scatter_grads(parts, ident, unit=16):
+    parts = [split_rows(part) for part in parts]
+    count = len(parts)
+    rows, width = parts[0].shape[2], parts[0].shape[3] // XS
+    groups = grouped(range(count), rows, unit)
     return pl.pallas_call(
-        scatter_kernel,
-        out_shape=[jax.ShapeDtypeStruct((rows, width), jnp.float32)] * 3,
-        in_specs=[HBM] * 3,
-        out_specs=[VMEM] * 3,
-        scratch_shapes=[
-            pltpu.VMEM((3, 2, ZS, rows, width), jnp.bfloat16),
-            pltpu.VMEM((3, 2, ZS, rows, width), jnp.bfloat16),
-            pltpu.VMEM((3, ZS, rows, width), jnp.bfloat16),
-            pltpu.VMEM((3, 3, rows, width), jnp.bfloat16),
-            pltpu.SemaphoreType.DMA((pairs * 6,)),
-            pltpu.SemaphoreType.DMA((pairs * 6,)),
-            pltpu.SemaphoreType.DMA((pairs * 2,)),
-        ],
+        partial(scatter_kernel, groups, count),
+        out_shape=[jax.ShapeDtypeStruct((rows, width), jnp.float32)] * count,
+        in_specs=[HBM] * count,
+        out_specs=[VMEM] * count,
+        scratch_shapes=scatter_scratch(groups, count, rows, width),
         compiler_params=pltpu.CompilerParams(
             collective_id=ident, has_side_effects=True, vmem_limit_bytes=60 * 2**20
         ),
@@ -712,13 +887,23 @@
     return values * cosine - swapped if back else values * cosine + swapped
 
 
-def attend_kernel(heads, scale, *refs):
+def spread(ticks, index, trips):
+    for number, tick in enumerate(ticks):
+        pl.when(index == number * trips // len(ticks))(tick)
+
+
+def attend_kernel(heads, scale, groups, *refs):
     projected, (cos_ref, left_ref, right_ref, hide_ref) = refs[:2], refs[2:6]
-    out_refs = refs[6:8]
-    query_ref, key_ref, value_ref, logsum_ref, held = refs[8:]
+    shards, out_refs = refs[6:8], refs[8:10]
+    query_ref, key_ref, value_ref, logsum_ref = refs[10:14]
+    wholes, held, gather_scratch_refs = refs[14:16], refs[16], refs[17:]
     slots = cos_ref.shape[0]
     per = heads // 2
     blocks = slots // BLOCK
+    greet(line_peers())
+    start, ticks, end = gather_plan(groups, shards, wholes, *gather_scratch_refs)
+    start()
+    ticks[0]()
 
     def prepare(i, carry):
         at = pl.ds(pl.multiple_of(i * BLOCK, BLOCK), BLOCK)
@@ -741,6 +926,7 @@
     lax.fori_loop(0, blocks, prepare, 0)
 
     def attend(i, carry):
+        spread(ticks[1:], i, heads * blocks)
         head, block = i // blocks, i % blocks
         at = pl.ds(pl.multiple_of(block * BLOCK, BLOCK), BLOCK)
         scores = contract(query_ref[head, at, :], key_ref[head], 1, 1)
@@ -768,14 +954,17 @@
         return carry
 
     lax.fori_loop(0, blocks, finish, 0)
-
-
-def attend(projected, tables, heads, scale):
+    end()
+
+
+def attend(projected, tables, shards, heads, scale, ident):
     slots = projected[0].shape[0]
+    count = len(shards)
+    groups = grouped(range(count), shards[0].shape[0], 16)
     packed = jax.ShapeDtypeStruct((heads, slots, LANES), jnp.bfloat16)
     half = jax.ShapeDtypeStruct((slots, heads // 2 * HEAD), jnp.bfloat16)
     results = pl.pallas_call(
-        partial(attend_kernel, heads, scale),
+        partial(attend_kernel, heads, scale, groups),
         out_shape=[
             half,
             half,
@@ -783,24 +972,32 @@
             packed,
             packed,
             jax.ShapeDtypeStruct((heads, slots, LANES), jnp.float32),
-        ],
-        in_specs=[VMEM] * 6,
-        out_specs=[VMEM] * 6,
-        scratch_shapes=[pltpu.VMEM((heads, slots, LANES), jnp.float32)],
-        compiler_params=pltpu.CompilerParams(vmem_limit_bytes=60 * 2**20),
+        ]
+        + [whole_shape(shard) for shard in shards],
+        in_specs=[VMEM] * (6 + count),
+        out_specs=[VMEM] * 6 + [HBM] * count,
+        scratch_shapes=[pltpu.VMEM((heads, slots, LANES), jnp.float32)]
+        + gather_scratch(groups, count),
+        compiler_params=pltpu.CompilerParams(
+            collective_id=ident, has_side_effects=True, vmem_limit_bytes=60 * 2**20
+        ),
         name="attend",
-    )(*projected, *tables)
-    return results[:2], results[2:]
-
-
-def attend_back_kernel(heads, scale, *refs):
+    )(*projected, *tables, *shards)
+    return results[:2], results[2:6], results[6:]
+
+
+def attend_back_kernel(heads, scale, groups, *refs):
     query_ref, key_ref, value_ref, logsum_ref = refs[:4]
     grads, (cos_ref, left_ref, right_ref) = refs[4:6], refs[6:9]
-    out_refs = refs[9:11]
-    held, grad_q, grad_k, grad_v = refs[11:]
+    parts, out_refs, sums = refs[9:11], refs[11:13], refs[13:15]
+    held, grad_q, grad_k, grad_v = refs[15:19]
+    buffers, semaphores = refs[19:26], refs[26:]
     slots = cos_ref.shape[0]
     per = heads // 2
     blocks = slots // BLOCK
+    greet(line_peers())
+    ticks, end = scatter_plan(groups, parts, sums, buffers, *semaphores)
+    ticks[0]()
 
     def prepare(i, carry):
         at = pl.ds(pl.multiple_of(i * BLOCK, BLOCK), BLOCK)
@@ -814,6 +1011,7 @@
     lax.fori_loop(0, blocks, prepare, 0)
 
     def attend(i, carry):
+        spread(ticks[1:], i, heads * blocks)
         head, block = i // blocks, i % blocks
         at = pl.ds(pl.multiple_of(block * BLOCK, BLOCK), BLOCK)
         query, grad = query_ref[head, at, :], held[head, at, :]
@@ -857,21 +1055,29 @@
         return carry
 
     lax.fori_loop(0, blocks, finish, 0)
-
-
-def attend_back(saved, grads, tables, heads, scale):
+    end()
+
+
+def attend_back(saved, grads, tables, parts, heads, scale, ident):
+    parts = [split_rows(part) for part in parts]
+    count, rows, width = len(parts), parts[0].shape[2], parts[0].shape[3] // XS
+    groups = grouped(range(count), rows, 16)
     slots = grads[0].shape[0]
     half = jax.ShapeDtypeStruct((slots, 3 * (heads // 2) * HEAD), jnp.bfloat16)
     wide = pltpu.VMEM((heads, slots, LANES), jnp.float32)
-    return pl.pallas_call(
-        partial(attend_back_kernel, heads, scale),
-        out_shape=[half, half],
-        in_specs=[VMEM] * 9,
-        out_specs=[VMEM] * 2,
-        scratch_shapes=[pltpu.VMEM((heads, slots, LANES), jnp.bfloat16), wide, wide, wide],
-        compiler_params=pltpu.CompilerParams(vmem_limit_bytes=60 * 2**20),
+    results = pl.pallas_call(
+        partial(attend_back_kernel, heads, scale, groups),
+        out_shape=[half, half] + [jax.ShapeDtypeStruct((rows, width), jnp.float32)] * count,
+        in_specs=[VMEM] * 9 + [HBM] * count,
+        out_specs=[VMEM] * (2 + count),
+        scratch_shapes=[pltpu.VMEM((heads, slots, LANES), jnp.bfloat16), wide, wide, wide]
+        + scatter_scratch(groups, count, rows, width),
+        compiler_params=pltpu.CompilerParams(
+            collective_id=ident, has_side_effects=True, vmem_limit_bytes=63 * 2**20
+        ),
         name="attend_back",
-    )(*saved, *grads, *tables[:3])
+    )(*saved, *grads, *tables[:3], *parts)
+    return results[:2], results[2:]
 
 
 def turn_tables(positions, visible):
@@ -945,7 +1151,7 @@
         w_up.astype(bf16),
         w_down.T.astype(bf16),
     ]
-    first, up_full, down_full = gather_weights(shards, 2)
+    first = gather_weights(shards[:1], 2)[0].reshape(model_width, -1)
     biases = jnp.concatenate([b_qkv.reshape(-1), b_up])
     other_biases = lax.ppermute(biases, "tensor", X_SWAP)
     low_biases = jnp.where(x == 0, biases, other_biases)
@@ -973,7 +1179,8 @@
         matrix = first[:, half * joined : half * joined + 8 * LANES]
         row = jnp.pad(bias[:qkv_width], (0, 8 * LANES - qkv_width))
         projected.append(jnp.dot(hidden_one, matrix, preferred_element_type=jnp.float32) + row)
-    attended, saved = attend(projected, tables, heads, scale)
+    attended, saved, wholes = attend(projected, tables, shards[1:], heads, scale, 3)
+    up_full, down_full = (whole.reshape(model_width, -1) for whole in wholes)
     out_parts = [first[:, half * joined + qkv_width : (half + 1) * joined] for half in range(2)]
     branch_one = (
         own_sum(contract(attended[0], out_parts[0], 1, 1) + contract(attended[1], out_parts[1], 1, 1))
@@ -1016,7 +1223,9 @@
         jnp.dot(grad_rows_one, part, preferred_element_type=jnp.float32).astype(bf16)
         for part in out_parts
     ]
-    grad_projected = attend_back(saved, grad_attended, tables, heads, scale)
+    grad_projected, (sum_down, sum_up) = attend_back(
+        saved, grad_attended, tables, [grad_down, grad_wup], heads, scale, 6
+    )
     first_parts, hidden_terms, bias_terms = [], 0.0, []
     for half in range(2):
         first_parts.append(contract(hidden_one, grad_projected[half], 0, 0).astype(bf16))
@@ -1030,7 +1239,7 @@
     grad_scale_one = jnp.sum(grad_hidden_one * normal_one, 0)
     grad_input = grad_middle + norm_back(grad_hidden_one, normal_one, inverse_one, scale_one)
 
-    sum_down, sum_up, sum_first = scatter_grads([grad_down, grad_wup, grad_first], 3)
+    sum_first = scatter_grads([grad_first], 7)[0]
     grad_wqkv = sum_first[:, :qkv_width].reshape(shard_rows, 3, feat)
     grad_wout = sum_first[:, qkv_width:].T
     grad_wdown = sum_down.T

time: 723 us -> 675 us (0.934)
  Pallas kernels: 473 us -> 424 us
    pallas_call x4, Pallas kernels: 427 us -> 379 us  [the longest x1 133 us: attend_back(): pl.pallas_call(partial(attend_back_kernel, heads, scale, groups), out_sha...]
    dot_general x1, matrix products: 17.2 us -> 25.8 us  [image_device(): jnp.dot(grad_rows_two, down_full, preferred_element_type=jnp.float32)]
  transfers between devices with their start and end apart: 10 -> 10, of which waited for: 0 -> 1; matrix products, arithmetic and copies ran while one was open for 15% -> 16% of each run, Pallas kernels for 49% -> 22%
where the time goes in v2:
time: 675 us; the launch traced here: 670 us
  Pallas kernels  424 us (63%)
  matrix products  126 us (19%)
  local copies, waits for them, and re-layouts  58.1 us (9%)
  other arithmetic  55.2 us (8%)
    pallas_call x1, Pallas kernels, attend_back(): pl.pallas_call(partial(attend_back_kernel, heads, scale, groups), out_sha...  133 us
    pallas_call x1, Pallas kernels, attend(): pl.pallas_call(partial(attend_kernel, heads, scale, groups), out_shape=[h...  119 us
    dot_general x14, matrix products, contract(): lax.dot_general(left, right, (((left_dim,), (right_dim,)), ((), ())), pre...  68.6 us
    pallas_call x1, Pallas kernels, gather_weights(): pl.pallas_call(partial(gather_kernel, groups, count), out_shape=[whole_sh...  64.7 us
    pallas_call x1, Pallas kernels, scatter_grads(): pl.pallas_call(partial(scatter_kernel, groups, count), out_shape=[jax.Sha...  62.8 us
    pallas_call x4, Pallas kernels, exchange(): pl.pallas_call(partial(exchange_kernel, kind, gather), out_shape=jax.Shap...  45.3 us
    dot_general x1, matrix products, image_device(): jnp.dot(grad_rows_two, down_full, preferred_element_type=jnp.float32)  25.8 us
    dot_general x2, matrix products, image_device(): jnp.dot(hidden_one, matrix, preferred_element_type=jnp.float32) + row  14.5 us
  transfers between devices with their start and end apart: 10, of which 1 were waited for; matrix products, arithmetic and copies ran while one was open for 16% of the time, Pallas kernels for 22%

profile of v2, /device:TPU:0, one launch (start us, length us, event | category | flops | bytes accessed | tf_op | source)
XLA Modules:
  0.0 670.2 jit_solution(18257290832595866228)
XLA Ops:
  9.3 8.6 %exchange_dp.1 = f32[8,18,128]{2,1,0:T(8,128)} custom-call(f32[18,128]{1,0:T(8,128)} %reshape.252.blocks), custom_call_target="tpu_custom_call" | custom-call | tf_op jit(solution)/shard_map/exchange_dp/pallas_call | solution.py:863
  23.2 11.8 %exchange_all.2 = f32[32,8,216]{2,1,0:T(8,128)} custom-call(f32[32,8,216]{2,1,0:T(8,128)} %bitcast.66), custom_call_target="tpu_custom_call" | custom-call | tf_op jit(solution)/shard_map/exchange_all/pallas_call | solution.py:863
  54.5 4.0 fusion.26
  61.1 64.7 %gather_weights.1 = bf16[4,2,144,2304]{3,2,1,0:T(8,128)(2,1)} custom-call(bf16[144,1152]{1,0:T(8,128)(2,1)} %pad_maximum_fusion.11.refs_0_), custom_call_target="tpu_custom_call" | custom-call | tf_op jit(solution)/shard_map/gather_weights/pallas_call | solution.py:781
  127.2 7.3 %broadcast_add_fusion.refs_1_ = f32[1024,1024]{1,0:T(8,128)} fusion(f32[1024]{0:T(1024)S(1)} %get-tuple-element.136, bf16[1152,2304]{1,0:T(8,128)(2,1)} %bitcast.55, bf16[512,1152]{1,0:T(8,128)(2,1)} %collective-permute-done, bf16[512,1152]{1,0:T(8,128)(2,1)} %add_convert_fusion.1), kind=kOutput, calls=%fused_computation.62 | convolution fusion | flops 2421686272 | bytes 8916992 | tf_op jit(solution)/shard_map/dot_general | solution.py:1181
  134.5 7.2 %broadcast_add_fusion.1.refs_0_ = f32[1024,1024]{1,0:T(8,128)} fusion(f32[1024]{0:T(1024)S(1)} %get-tuple-element.137, bf16[1152,2304]{1,0:T(8,128)(2,1)} %bitcast.56, bf16[512,1152]{1,0:T(8,128)(2,1)} %collective-permute-done, bf16[512,1152]{1,0:T(8,128)(2,1)} %add_convert_fusion.1), kind=kOutput, calls=%fused_computation.63 | convolution fusion | flops 2421686272 | bytes 8916992 | tf_op jit(solution)/shard_map/dot_general | solution.py:1181
  141.7 118.5 %attend.1 = (bf16[1024,288]{1,0:T(8,128)(2,1)}, bf16[1024,288]{1,0:T(8,128)(2,1)}, bf16[8,1024,128]{2,1,0:T(8,128)(2,1)}, bf16[8,1024,128]{2,1,0:T(8,128)(2,1)},...) custom-call(f32[1024,1024]{1,0:T(8,128)} %broadcast_add_fusion.1.ref, ...), custom_call_target="tpu_custom_call" | custom-call | tf_op jit(solution)/shard_map/attend/pallas_call | solution.py:966
  281.9 11.6 %fusion.19 = f32[1024,2304]{1,0:T(8,128)} fusion(bf16[1152,2304]{1,0:T(8,128)(2,1)} %bitcast.79, bf16[512,1152]{1,0:T(8,128)(2,1)} %collective-permute-done.3, bf16[512,1152]{1,0:T(8,128)(2,1)S(1)} %add_convert_fusion), kind=kOutput, calls=%fused_computation.69 | convolution fusion | flops 5440536576 | bytes 17104896 | tf_op jit(solution)/shard_map/dot_general | solution.py:1193
  293.5 11.0 %fusion.55 = f32[1024,1152]{1,0:T(8,128)S(1)} fusion(bf16[1152,2304]{1,0:T(8,128)(2,1)S(1)} %bitcast.85, f32[1024,2304]{1,0:T(8,128)} %fusion.19, f32[2304]{0:T(1024)S(1)} %pad_maximum_fusion.12), kind=kOutput, calls=%fused_computation.171 | convolution fusion | flops 5459410944 | bytes 19473408 | tf_op jit(solution)/shard_map/dot_general | solution.py:44
  304.6 25.8 %convert_reduce_fusion = (f32[2304]{0:T(1024)S(1)}, bf16[1024,2304]{1,0:T(8,128)(2,1)}) fusion(bf16[1152,2304]{1,0:T(8,128)(2,1)S(1)} %bitcast.86, bf16[512,1152]{1,0:T(8,128)(2,1)} %collective-permute-done.5, bf16[512,1152]{1,0:T(8,128)(2,1)S(1)} %multiply_convert_fusion.2, f32[1024,2304]{1,0:T(8,128)} %fusion.19, f32[2304]{0:T(1024)S(1)} %pad_maximum_fusion.12), kind=kOutput, calls=%fused_computation.12 | convolution fusion | flops 5504235520 | bytes 21841920 | tf_op jit(solution)/shard_map/dot_general | solution.py:1211
  330.3 8.2 %fusion.61 = f32[1024,1152]{1,0:T(8,128)S(1)} fusion(bf16[1024,2304]{1,0:T(8,128)(2,1)} %get-tuple-element.139, bf16[1152,2304]{1,0:T(8,128)(2,1)S(1)} %bitcast.82), kind=kOutput, calls=%fused_computation.177 | convolution fusion | flops 5435817984 | bytes 14745600 | tf_op jit(solution)/shard_map/dot_general | solution.py:44
  339.4 11.6 %convolution_convert_fusion.1 = bf16[1152,2304]{1,0:T(8,128)(2,1)} fusion(bf16[512,1152]{1,0:T(8,128)(2,1)} %collective-permute-done.5, bf16[512,1152]{1,0:T(8,128)(2,1)S(1)} %multiply_convert_fusion.2, f32[1024,2304]{1,0:T(8,128)} %fusion.19, f32[2304]{0:T(1024)S(1)} %pad_maximum_fusion.12), kind=kOutput, calls=%fused_computation.5 | convolution fusion | flops 5466783744 | bytes 17114112 | tf_op jit(solution)/shard_map/dot_general | solution.py:44
  353.3 4.5 multiply_reduce_fusion
  359.9 10.2 %convolution_convert_fusion = bf16[1152,2304]{1,0:T(8,128)(2,1)} fusion(bf16[1024,2304]{1,0:T(8,128)(2,1)} %get-tuple-element.139, bf16[512,1152]{1,0:T(8,128)(2,1)} %collective-permute-done.3, bf16[512,1152]{1,0:T(8,128)(2,1)S(1)} %copy-done.20), kind=kOutput, calls=%fused_computation.4 | convolution fusion | flops 5443190784 | bytes 12386304 | tf_op jit(solution)/shard_map/dot_general | solution.py:44
  379.8 132.6 %attend_back.1 = (bf16[1024,864]{1,0:T(8,128)(2,1)}, bf16[1024,864]{1,0:T(8,128)(2,1)}, f32[144,1152]{1,0:T(8,128)}, f32[144,1152]{1,0:T(8,128)}) custom-call(bf16[8,1024,128]{2,1,0:T(8,128)(2,1)} %get-tuple-element.29.refs_0_, bf16[8,1024,128]{2,1,0:T(8,128)(2,1)} %get-tuple-element.30.refs_1_, bf16[8,1024,128]{2,1,0:T(8,128)(2,1)} %get-tuple-element.31.refs_2_, ...), custom_call_target="tpu_custom_call" | custom-call | tf_op jit(solution)/shard_map/attend_back/pallas_call | solution.py:1068
  512.4 5.1 fusion.13
  517.5 4.7 convolution_add_fusion.1
  526.8 4.2 convolution_convert_fusion.3
  531.0 4.4 convolution_convert_fusion.2
  538.2 8.5 %copy.54 = bf16[1152,2304]{1,0:T(8,128)(2,1)} copy(bf16[1152,2304]{0,1:T(8,128)(2,1)} %pad_maximum_fusion) | data formatting | bytes 10616832 | tf_op jit(solution)/shard_map/concatenate | solution.py:1236
  546.8 62.8 %scatter_grads.1 = f32[144,1152]{1,0:T(8,128)} custom-call(bf16[4,2,144,2304]{3,2,1,0:T(8,128)(2,1)} %bitcast.54), custom_call_target="tpu_custom_call" | custom-call | tf_op jit(solution)/shard_map/scatter_grads/pallas_call | solution.py:810
  626.5 4.7 multiply_add_fusion.2
  634.0 12.7 %exchange_same_core.1 = f32[16,48,128]{2,1,0:T(8,128)} custom-call(f32[16,48,128]{2,1,0:T(8,128)} %bitcast.65), custom_call_target="tpu_custom_call" | custom-call | tf_op jit(solution)/shard_map/exchange_same_core/pallas_call | solution.py:863
  652.3 12.2 %exchange_all.3 = f32[32,8,128]{2,1,0:T(8,128)} custom-call(f32[32,8,128]{2,1,0:T(8,128)} %reshape.242.blocks), custom_call_target="tpu_custom_call" | custom-call | tf_op jit(solution)/shard_map/exchange_all/pallas_call | solution.py:863
  (268 shorter events, 111.5 us)
Async XLA Ops:
  0.7 18.2 %copy-start.16 = (f32[144,6,288]{2,0,1:T(8,128)S(1)}, f32[144,6,288]{2,0,1:T(8,128)}, u32[]{:S(2)}) copy-start(f32[144,6,288]{2,0,1:T(8,128)} %param.19) | copy-start | bytes 2985988
  2.9 122.8 %collective-permute-start.1 = (f32[2016]{0:T(1024)}, f32[2016]{0:T(1024)}, u32[]{:S(2)}, u32[]{:S(2)}) collective-permute-start(f32[2016]{0:T(1024)} %pad_maximum_fusion.13), channel_id=1, source_target_pairs={{0,2},{2,0},{1,3},{3,1},{4,6},{6,4},{5,7},{7,5},{8,10},{10,8},{9,1... | collective-permute-start | bytes 24200 | tf_op jit(solution)/shard_map/ppermute | solution.py:1156
  20.1 22.0 %copy-start = (f32[512,1152]{1,0:T(8,128)S(1)}, f32[512,1152]{1,0:T(8,128)}, u32[]{:S(2)}) copy-start(f32[512,1152]{1,0:T(8,128)} %param.15) | copy-start | bytes 7077892
  22.0 22.2 %copy-start.10 = (bf16[144,1728]{1,0:T(8,128)(2,1)}, bf16[144,1728]{1,0:T(8,128)(2,1)S(1)}, u32[]{:S(2)}) copy-start(bf16[144,1728]{1,0:T(8,128)(2,1)S(1)} %reshape.227) | copy-start | bytes 1492996
  44.2 82.9 %collective-permute-start = (bf16[512,1152]{1,0:T(8,128)(2,1)}, bf16[512,1152]{1,0:T(8,128)(2,1)}, u32[]{:S(2)}, u32[]{:S(2)}) collective-permute-start(bf16[512,1152]{1,0:T(8,128)(2,1)} %add_convert_fusion.1), channel_id=1, source_target_pairs={{0,1},{1,0},{2,3},{3,2},{4,5},{5,4},{6,7},{7,6},{8,9},{9,8},{10,11... | collective-permute-start | bytes 3538952 | tf_op jit(solution)/shard_map/ppermute | solution.py:1126
  61.0 64.7 %copy-start.44 = (f32[1152]{0:T(1024)S(1)}, f32[1152]{0:T(1024)}, u32[]{:S(2)}) copy-start(f32[1152]{0:T(1024)} %param.26) | copy-start | bytes 13828
  61.1 66.1 %copy-start.53 = (pred[1024]{0:T(1024)(128)(4,1)S(1)}, pred[1024]{0:T(1024)(128)(4,1)}, u32[]{:S(2)}) copy-start(pred[1024]{0:T(1024)(128)(4,1)} %constant.116.clone.1) | copy-start | bytes 3076
  269.5 4.7 collective-permute-start.2
  271.4 7.7 %collective-permute-start.5 = (bf16[512,1152]{1,0:T(8,128)(2,1)S(1)}, bf16[512,1152]{1,0:T(8,128)(2,1)}, u32[]{:S(2)}, u32[]{:S(2)}) collective-permute-start(bf16[512,1152]{1,0:T(8,128)(2,1)S(1)} %multiply_convert_fusion.2), channel_id=1, source_target_pairs={{0,1},{1,0},{2,3},{3,2},{4,5},{5,4},{6,7},{7,6},{8,9},{9,8},{10,11... | collective-permute-start | bytes 3538952 | tf_op jit(solution)/shard_map/ppermute | solution.py:1126
  278.9 14.7 %copy-start.19 = (bf16[512,1152]{1,0:T(8,128)(2,1)}, bf16[512,1152]{1,0:T(8,128)(2,1)S(1)}, u32[]{:S(2)}) copy-start(bf16[512,1152]{1,0:T(8,128)(2,1)S(1)} %add_convert_fusion) | copy-start | bytes 3538948
  278.9 3.0 collective-permute-start.3
  279.1 14.4 %slice-start.4 = ((s8[5308416]{0:T(1024)(128)(4,1)}), s8[4194304]{0:T(1024)(128)(4,1)S(1)}, s32[]{:S(2)}) async-start(s8[5308416]{0:T(1024)(128)(4,1)} %bitcast.83), calls=%async_computation.4 | async-start | bytes 8388608
  293.5 36.8 %slice-start.2 = ((s8[5308416]{0:T(1024)(128)(4,1)}), s8[4194304]{0:T(1024)(128)(4,1)S(1)}, s32[]{:S(2)}) async-start(s8[5308416]{0:T(1024)(128)(4,1)} %bitcast.80), calls=%async_computation.2 | async-start | bytes 8388608
  304.5 25.8 %slice-start.3 = ((s8[5308416]{0:T(1024)(128)(4,1)}), s8[1114112]{0:T(1024)(128)(4,1)S(1)}, s32[]{:S(2)}) async-start(s8[5308416]{0:T(1024)(128)(4,1)} %bitcast.80), calls=%async_computation.3 | async-start | bytes 2228224
  338.5 14.3 %slice-start = ((s8[4718592]{0:T(1024)(128)(4,1)}), s8[4194304]{0:T(1024)(128)(4,1)S(1)}, s32[]{:S(2)}) async-start(s8[4718592]{0:T(1024)(128)(4,1)} %bitcast.52), calls=%async_computation | async-start | bytes 8388608
  338.8 14.1 %slice-start.1 = ((s8[4718592]{0:T(1024)(128)(4,1)}), s8[524288]{0:T(1024)(128)(4,1)S(1)}, s32[]{:S(2)}) async-start(s8[4718592]{0:T(1024)(128)(4,1)} %bitcast.52), calls=%async_computation.1 | async-start | bytes 1048576
  338.8 14.0 %collective-permute-start.4 = (bf16[512,1152]{1,0:T(8,128)(2,1)S(1)}, bf16[512,1152]{1,0:T(8,128)(2,1)S(1)}, u32[]{:S(2)}, u32[]{:S(2)}) collective-permute-start(bf16[512,1152]{1,0:T(8,128)(2,1)S(1)} %slice.298), channel_id=1, source_target_pairs={{0,1},{1,0},{2,3},{3,2},{4,5},{5,4},{6,7},{7,6},{8,9},{9,8},{10,11... | collective-permute-start | bytes 3538952 | tf_op jit(solution)/shard_map/ppermute | solution.py:1126
  339.0 12.6 %collective-permute-start.6 = (bf16[512,1152]{1,0:T(8,128)(2,1)S(1)}, bf16[512,1152]{1,0:T(8,128)(2,1)S(1)}, u32[]{:S(2)}, u32[]{:S(2)}) collective-permute-start(bf16[512,1152]{1,0:T(8,128)(2,1)S(1)} %slice.297), channel_id=1, source_target_pairs={{0,1},{1,0},{2,3},{3,2},{4,5},{5,4},{6,7},{7,6},{8,9},{9,8},{10,11... | collective-permute-start | bytes 3538952 | tf_op jit(solution)/shard_map/ppermute | solution.py:1126
  358.0 18.1 %copy-start.8 = (bf16[512,1152]{1,0:T(8,128)(2,1)}, bf16[512,1152]{1,0:T(8,128)(2,1)S(1)}, u32[]{:S(2)}) copy-start(bf16[512,1152]{1,0:T(8,128)(2,1)S(1)} %multiply_convert_fusion.1) | copy-start | bytes 3538948
  358.0 13.9 %collective-permute-start.7 = (bf16[512,1152]{1,0:T(8,128)(2,1)S(1)}, bf16[512,1152]{1,0:T(8,128)(2,1)S(1)}, u32[]{:S(2)}, u32[]{:S(2)}) collective-permute-start(bf16[512,1152]{1,0:T(8,128)(2,1)S(1)} %multiply_convert_fusion.1), channel_id=1, source_target_pairs={{0,1},{1,0},{2,3},{3,2},{4,5},{5,4},{6,7},{7,6},{8,9},{9,8},{10,11... | collective-permute-start | bytes 3538952 | tf_op jit(solution)/shard_map/ppermute | solution.py:1126
  523.6 96.4 %collective-permute-start.8 = (bf16[512,1152]{1,0:T(8,128)(2,1)}, bf16[512,1152]{1,0:T(8,128)(2,1)S(1)}, u32[]{:S(2)}, u32[]{:S(2)}) collective-permute-start(bf16[512,1152]{1,0:T(8,128)(2,1)} %slice.296), channel_id=1, source_target_pairs={{0,1},{1,0},{2,3},{3,2},{4,5},{5,4},{6,7},{7,6},{8,9},{9,8},{10,11... | collective-permute-start | bytes 3538952 | tf_op jit(solution)/shard_map/ppermute | solution.py:1126
  626.5 4.7 collective-permute-start.9
  631.2 17.5 %copy-start.11 = (bf16[144,1728]{1,0:T(8,128)(2,1)S(1)}, bf16[144,1728]{1,0:T(8,128)(2,1)}, u32[]{:S(2)}) copy-start(bf16[144,1728]{1,0:T(8,128)(2,1)} %copy-done.10) | copy-start | bytes 1492996
  634.0 31.6 %copy-start.41 = (f32[2,1152]{1,0:T(2,128)S(1)}, f32[2,1152]{1,0:T(2,128)}, u32[]{:S(2)}) copy-start(f32[2,1152]{1,0:T(2,128)} %param.16) | copy-start | bytes 27652
  (47 other events, 207.1 us)

commit v3 on v2

--- a/solution.py
+++ b/solution.py
@@ -331,6 +331,7 @@
 MESH_ID = pl.DeviceIdType.MESH
 CORE_SWAP = [(0, 1), (1, 0), (2, 3), (3, 2)]
 X_SWAP = [(0, 2), (2, 0), (1, 3), (3, 1)]
+Y_SWAP = [(i, i ^ 1) for i in range(ZS * YS)]
 LOG2E = 1.0 / math.log(2.0)
 HBM = pl.BlockSpec(memory_space=pl.ANY)
 VMEM = pl.BlockSpec(memory_space=pltpu.VMEM)
@@ -365,50 +366,63 @@
     pl.semaphore_wait(barrier, len(targets))
 
 
-GATHER_STEPS, SCATTER_STEPS = 5, 6
-
-
-def grouped(matrices, rows, unit):
-    groups = []
-    for matrix in matrices:
-        for row in range(0, rows, 3 * unit):
-            short = len(groups) % 2
-            groups.append(
-                [
-                    (matrix, row, unit, 2),
-                    (matrix, row + unit, unit, 3),
-                    (matrix, row + 2 * unit, unit, short),
-                ]
-            )
-    return groups
-
-
-def numbered(groups):
-    chunks, members = [], []
-    for group in groups:
-        members.append(range(len(chunks), len(chunks) + len(group)))
-        chunks.extend(group)
-    return chunks, members
-
-
-def ticks_of(members, steps, act):
-    def tick(time):
-        for group, numbers in enumerate(members):
-            step = time - group
-            if 0 <= step < steps:
-                for number in numbers:
-                    act(number, step)
-
-    return [partial(tick, time) for time in range(len(members) + steps - 1)]
-
-
-def gather_plan(groups, shards, wholes, sends, recvs, local):
-    chunks, members = numbered(groups)
+GATHER_STEPS, SCATTER_STEPS = 5, 5
+GATHER_SPACING, SCATTER_SPACING = 8.0, 8.0
+GATHER_WEIGHTS, SCATTER_WEIGHTS = (1, 1, 1, 1, 1), (1, 1, 1, 1, 1)
+
+
+def grouped(matrices, rows, units):
+    chunks = []
+    for matrix in range(matrices):
+        unit = units[matrix]
+        for number, row in enumerate(range(0, rows, 3 * unit)):
+            short = (matrix + number) % 2
+            chunks.append((matrix, row, unit, 2))
+            chunks.append((matrix, row + unit, unit, 3))
+            chunks.append((matrix, row + 2 * unit, unit, short))
+    return chunks
+
+
+def in_order(count, steps, spacing, act):
+    events = sorted((c + s * spacing, c, s) for c in range(count) for s in range(steps))
+    return [(s, partial(act, c, s)) for time, c, s in events]
+
+
+def run_all(events):
+    for _, event in events:
+        event()
+
+
+def table_of(events, weights, trips):
+    total = sum(weights[step] for step, _ in events)
+    table, sent = [[] for _ in range(trips)], 0
+    for step, event in events:
+        table[min(sent * trips // total, trips - 1)].append(event)
+        sent += weights[step]
+    return table
+
+
+def dispatch(table, index, low, high):
+    if not any(table[low:high]):
+        return
+    if high - low == 1:
+        for event in table[low]:
+            event()
+        return
+    middle = (low + high) // 2
+    pl.when(index < middle)(lambda: dispatch(table, index, low, middle))
+    pl.when(index >= middle)(lambda: dispatch(table, index, middle, high))
+
+
+def gather_plan(chunks, spacing, shards, wholes, sends, recvs, local):
     z, y, x, core = place()
     inner = jnp.logical_or(z == 1, z == 2)
-    width = shards[0].shape[1]
-    mine = pl.ds(pl.multiple_of(x * width, LANES), width)
     every = slice(None)
+
+    def mine_of(matrix):
+        width = shards[matrix].shape[1]
+        return pl.ds(pl.multiple_of(x * width, LANES), width)
+
     at_x, at_y = device(z, y, 1 - x, core), device(z, 1 - y, x, core)
     beside, mirror = device(flip_z(z, 1), y, x, core), device(3 - z, y, x, core)
     pair = pl.ds(z // 2 * 2, 2)
@@ -426,7 +440,7 @@
 
     def moves(number):
         matrix, row, rows, route = chunks[number]
-        whole, span = wholes[matrix], pl.ds(row, rows)
+        whole, span, mine = wholes[matrix], pl.ds(row, rows), mine_of(matrix)
         own, shard = whole.at[z, y, span, mine], shards[matrix].at[span, :]
         lines, columns = (every if route == 3 else y), (every if route == 2 else mine)
         made = {}
@@ -451,7 +465,7 @@
 
     def keep(matrix):
         return pltpu.make_async_copy(
-            shards[matrix], wholes[matrix].at[z, y, :, mine], local.at[matrix]
+            shards[matrix], wholes[matrix].at[z, y, :, mine_of(matrix)], local.at[matrix]
         )
 
     kept = []
@@ -510,11 +524,11 @@
 
             pl.when(inner)(rest)
 
-    return start, ticks_of(members, GATHER_STEPS, act), finish
-
-
-def gather_scratch(groups, matrices):
-    count = sum(len(group) for group in groups)
+    return start, in_order(len(chunks), GATHER_STEPS, spacing, act), finish
+
+
+def gather_scratch(chunks, matrices):
+    count = len(chunks)
     return [
         pltpu.SemaphoreType.DMA((count * 5,)),
         pltpu.SemaphoreType.DMA((count * 4,)),
@@ -522,232 +536,182 @@
     ]
 
 
-def scatter_plan(groups, parts, sums, buffers, sends, recvs, local):
-    chunks, members = numbered(groups)
-    own, first_in, second_in, outer_in, mirror_in, near_in, last_in = buffers
+def send_off(part, flip, after):
+    z, y, x, core = place()
+    rows, width = part.shape[0] // (ZS * YS), part.shape[1] // XS
+    blocks = part.reshape(ZS, YS, rows, XS * width)
+    split = rows // 32 * 16
+    split = split if flip else rows - split
+    by_y, by_x = blocks[:, :, :split], blocks[:, :, split:]
+    low, high = by_x[..., :width], by_x[..., width:]
+    send_y = lax.dynamic_index_in_dim(by_y, 1 - y, 1, False)
+    keep_y = lax.dynamic_index_in_dim(by_y, y, 1, False)
+    send_x, keep_x = jnp.where(x == 0, high, low), jnp.where(x == 0, low, high)
+    send_y, send_x, after = lax.optimization_barrier((send_y, send_x, after))
+    got_y = lax.ppermute(send_y, "dp", Y_SWAP)
+    got_x = lax.ppermute(send_x, "tensor", X_SWAP)
+    return (keep_y, got_y, keep_x, got_x), after
+
+
+def arrive_before(sent, after):
+    keep_y, got_y, keep_x, got_x = sent
+    got_y, got_x, after = lax.optimization_barrier((got_y, got_x, after))
+    return (keep_y, got_y, keep_x, got_x), after
+
+
+def settle(sent):
+    z, y, x, core = place()
+    keep_y, got_y, keep_x, got_x = sent
+    sum_y = (keep_y.astype(jnp.float32) + got_y.astype(jnp.float32)).astype(jnp.bfloat16)
+    sum_x = (keep_x.astype(jnp.float32) + got_x.astype(jnp.float32)).astype(jnp.bfloat16)
+    width = sum_x.shape[-1]
+    low, high = sum_y[..., :width], sum_y[..., width:]
+    return [
+        jnp.where(x == 0, low, high),
+        jnp.where(x == 0, high, low),
+        lax.dynamic_index_in_dim(sum_x, y, 1, False),
+        lax.dynamic_index_in_dim(sum_x, 1 - y, 1, False),
+    ]
+
+
+def scatter_chunks(pieces, units):
+    chunks = []
+    for matrix, unit in enumerate(units):
+        parts, start = [], 0
+        for side in range(2):
+            rows = pieces[matrix][2 * side].shape[1]
+            parts.append(
+                [(matrix, side, row, start + row, min(unit, rows - row)) for row in range(0, rows, unit)]
+            )
+            start += rows
+        for i in range(max(len(part) for part in parts)):
+            chunks.extend(part[i] for part in parts if i < len(part))
+    return chunks
+
+
+def scatter_plan(chunks, spacing, pieces, sums, buffers, sends, recvs):
     z, y, x, core = place()
     inner = jnp.logical_or(z == 1, z == 2)
     outer = jnp.logical_or(z == 0, z == 3)
-    width = sums[0].shape[1]
-    mine = pl.ds(pl.multiple_of(x * width, LANES), width)
-    theirs = pl.ds(pl.multiple_of((1 - x) * width, LANES), width)
     at_x, at_y = device(z, y, 1 - x, core), device(z, 1 - y, x, core)
     z_near = flip_z(z, 1)
     beside, mirror = device(z_near, y, x, core), device(3 - z, y, x, core)
     pair_at, far_at = z // 2 * 2, 2 - z // 2 * 2
-    pair, far = pl.ds(pair_at, 2), pl.ds(far_at, 2)
+    far = pl.ds(far_at, 2)
 
     def copy(number, index, source, target, where):
         return pltpu.make_async_remote_copy(
             src_ref=source,
             dst_ref=target,
-            send_sem=sends.at[number * 6 + index],
-            recv_sem=recvs.at[number * 6 + index],
+            send_sem=sends.at[number * 4 + index],
+            recv_sem=recvs.at[number * 4 + index],
             device_id=where,
             device_id_type=MESH_ID,
         )
 
     def moves(number):
-        matrix, row, rows, route = chunks[number]
-        part, span = parts[matrix], pl.ds(row, rows)
-        by_y = route in (0, 2)
-        made = {}
-        for slot in range(2):
-            if by_y:
-                column = mine if slot == 0 else theirs
-                source, kept = part.at[:, 1 - y, span, column], part.at[:, y, span, column]
-            else:
-                line = y if slot == 0 else 1 - y
-                source, kept = part.at[:, line, span, theirs], part.at[:, line, span, mine]
-            made["first", slot] = partial(
+        matrix, side, row, at, rows = chunks[number]
+        here, span = pl.ds(row, rows), pl.ds(at, rows)
+        arrived, outer_in, mirror_in, near_in = buffers[4 * matrix : 4 * matrix + 4]
+        give, two = pieces[4 * matrix + 2 * side + 1], arrived.at[far, span, :]
+        return {
+            "first": partial(
                 copy,
                 number,
-                slot,
-                source,
-                first_in.at[matrix, slot, :, span, :],
-                at_y if by_y else at_x,
+                0,
+                give.at[:, here, :],
+                arrived.at[:, span, :],
+                at_y if side else at_x,
+            ),
+            "outer": partial(copy, number, 1, two, outer_in.at[:, span, :], beside),
+            "mirror": partial(copy, number, 2, two, mirror_in.at[:, span, :], mirror),
+            "near": partial(
+                copy, number, 3, arrived.at[z_near, span, :], near_in.at[span, :], beside
+            ),
+        }
+
+    def add(number, count, base, source, from_row):
+        matrix, side, row, at, rows = chunks[number]
+        arrived, tiles = buffers[4 * matrix], rows // 16
+
+        def one(i, carry):
+            block, line = i // tiles, i % tiles
+            to = pl.ds(pl.multiple_of(at + line * 16, 16), 16)
+            origin = pl.ds(pl.multiple_of(from_row + line * 16, 16), 16)
+            held = arrived[base + block, to, :].astype(jnp.float32)
+            arrived[base + block, to, :] = (
+                held + source[block, origin, :].astype(jnp.float32)
+            ).astype(jnp.bfloat16)
+            return carry
+
+        lax.fori_loop(0, count * tiles, one, 0)
+
+    def finalize(number):
+        matrix, side, row, at, rows = chunks[number]
+        arrived, near_in = buffers[4 * matrix], buffers[4 * matrix + 3]
+
+        def one(i, carry):
+            to = pl.ds(pl.multiple_of(at + i * 16, 16), 16)
+            sums[matrix][to, :] = arrived[z, to, :].astype(jnp.float32) + near_in[to, :].astype(
+                jnp.float32
             )
-            made["load", slot] = partial(
-                pltpu.make_async_copy,
-                kept, own.at[matrix, slot, :, span, :], local.at[number * 2 + slot]
-            )
-        if route < 2:
-            made["second"] = partial(
-                copy,
-                number,
-                2,
-                own.at[matrix, 1, :, span, :],
-                second_in.at[matrix, :, span, :],
-                at_x if by_y else at_y,
-            )
-            slots = 0
-        else:
-            made["last"] = partial(
-                copy,
-                number,
-                2,
-                own.at[matrix, 1, z, span, :],
-                last_in.at[matrix, span, :],
-                at_x if by_y else at_y,
-            )
-            slots = slice(None)
-        made["outer"] = partial(
-                copy,
-            number,
-            3,
-            own.at[matrix, slots, far, span, :],
-            outer_in.at[matrix, slots, :, span, :],
-            beside,
-        )
-        made["mirror"] = partial(
-                copy,
-            number,
-            4,
-            own.at[matrix, slots, far, span, :],
-            mirror_in.at[matrix, slots, :, span, :],
-            mirror,
-        )
-        made["near"] = partial(
-                copy,
-            number,
-            5,
-            own.at[matrix, slots, z_near, span, :],
-            near_in.at[matrix, slots, span, :],
-            beside,
-        )
-        return made
-
-    def add(rows, row, target, arrived):
-        def one(i, carry):
-            at = pl.ds(pl.multiple_of(row + i * 16, 16), 16)
-            held = own[(*target, at, slice(None))].astype(jnp.float32)
-            incoming = arrived[0][(*arrived[1], at, slice(None))].astype(jnp.float32)
-            own[(*target, at, slice(None))] = (held + incoming).astype(jnp.bfloat16)
             return carry
 
         lax.fori_loop(0, rows // 16, one, 0)
 
-    def add_blocks(number, count, target, arrived):
-        matrix, row, rows, route = chunks[number]
-
-        def one(i, carry):
-            ref, index = arrived(i)
-            add(rows, row, (matrix, *target(i)), (ref, (matrix, *index)))
-            return carry
-
-        lax.fori_loop(0, count, one, 0)
-
-    def finalize(number, ref, index):
-        matrix, row, rows, route = chunks[number]
-
-        def one(i, carry):
-            at = pl.ds(pl.multiple_of(row + i * 16, 16), 16)
-            sums[matrix][at, :] = own[matrix, 0, z, at, :].astype(jnp.float32) + ref[
-                (matrix, *index, at, slice(None))
-            ].astype(jnp.float32)
-            return carry
-
-        lax.fori_loop(0, rows // 16, one, 0)
-
     def act(number, step):
+        matrix, side, row, at, rows = chunks[number]
         made = moves(number)
-        straight = chunks[number][3] < 2
-        count = 2 if straight else 4
-        slots = 1 if straight else 2
+        stay = pieces[4 * matrix + 2 * side]
+        arrived, outer_in, mirror_in, near_in = buffers[4 * matrix : 4 * matrix + 4]
 
         def from_outer():
             made["outer"]().wait_recv()
-            add_blocks(
-                number,
-                count,
-                lambda i: (i // 2, far_at + i % 2),
-                lambda i: (outer_in, (i // 2, i % 2)),
-            )
+            add(number, 2, far_at, outer_in, at)
             made["mirror"]().start()
 
         def from_mirror():
             made["mirror"]().wait_recv()
-            add_blocks(
-                number,
-                count,
-                lambda i: (i // 2, pair_at + i % 2),
-                lambda i: (mirror_in, (i // 2, i % 2)),
-            )
+            add(number, 2, pair_at, mirror_in, at)
 
         if step == 0:
-            for slot in (1, 0):
-                made["first", slot]().start()
-                made["load", slot]().start()
+            made["first"]().start()
         elif step == 1:
-            for slot in (1, 0):
-                made["first", slot]().wait_recv()
-                made["load", slot]().wait()
-                add_blocks(
-                    number,
-                    ZS,
-                    lambda i, slot=slot: (slot, i),
-                    lambda i, slot=slot: (first_in, (slot, i)),
-                )
-                if straight and slot == 1:
-                    made["second"]().start()
-            if not straight:
-                pl.when(outer)(lambda: made["outer"]().start())
-        elif straight:
-            if step == 2:
-                made["second"]().wait_recv()
-                add_blocks(number, ZS, lambda i: (0, i), lambda i: (second_in, (i,)))
-                pl.when(outer)(lambda: made["outer"]().start())
-            elif step == 3:
-                pl.when(inner)(from_outer)
-            elif step == 4:
-                pl.when(inner)(from_mirror)
-                made["near"]().start()
-            else:
-                made["near"]().wait_recv()
-                finalize(number, near_in, (0,))
+            made["first"]().wait_recv()
+            add(number, ZS, 0, stay, row)
+            pl.when(outer)(lambda: made["outer"]().start())
         elif step == 2:
             pl.when(inner)(from_outer)
         elif step == 3:
             pl.when(inner)(from_mirror)
             made["near"]().start()
-        elif step == 4:
+        else:
             made["near"]().wait_recv()
-            add_blocks(number, 2, lambda i: (i, z), lambda i: (near_in, (i,)))
-            made["last"]().start()
-        else:
-            made["last"]().wait_recv()
-            finalize(number, last_in, ())
+            finalize(number)
 
     def finish():
         for number in range(len(chunks)):
             made = moves(number)
-            for name in made:
-                if name not in ("outer", "mirror") and name[0] != "load":
-                    made[name]().wait_send()
+            made["first"]().wait_send()
+            made["near"]().wait_send()
             pl.when(outer)(lambda made=made: made["outer"]().wait_send())
             pl.when(inner)(lambda made=made: made["mirror"]().wait_send())
 
-    return ticks_of(members, SCATTER_STEPS, act), finish
-
-
-def scatter_scratch(groups, matrices, rows, width):
-    count = sum(len(group) for group in groups)
-
-    def wide(*lead):
-        return pltpu.VMEM((matrices, *lead, rows, width), jnp.bfloat16)
-
-    return [
-        wide(2, ZS),
-        wide(2, ZS),
-        wide(ZS),
-        wide(2, 2),
-        wide(2, 2),
-        wide(2),
-        wide(),
-        pltpu.SemaphoreType.DMA((count * 6,)),
-        pltpu.SemaphoreType.DMA((count * 6,)),
-        pltpu.SemaphoreType.DMA((count * 2,)),
-    ]
+    return in_order(len(chunks), SCATTER_STEPS, spacing, act), finish
+
+
+def scatter_scratch(chunks, shapes):
+    wide = []
+    for rows, width in shapes:
+        for lead in ((ZS,), (2,), (2,), ()):
+            wide.append(pltpu.VMEM((*lead, rows, width), jnp.bfloat16))
+    count = len(chunks) * 4
+    return wide + [pltpu.SemaphoreType.DMA((count,)), pltpu.SemaphoreType.DMA((count,))]
+
+
+def sum_shape(piece):
+    rows = piece[0].shape[1] + piece[2].shape[1]
+    return rows, piece[0].shape[2]
 
 
 def line_peers():
@@ -760,118 +724,220 @@
     ]
 
 
-def gather_kernel(groups, matrices, *refs):
-    shards, wholes, scratch = refs[:matrices], refs[matrices : 2 * matrices], refs[2 * matrices :]
-    greet(line_peers())
-    start, ticks, finish = gather_plan(groups, shards, wholes, *scratch)
-    start()
-    for tick in ticks:
-        tick()
-    finish()
-
-
-def whole_shape(shard):
-    rows, width = shard.shape
-    return jax.ShapeDtypeStruct((ZS, YS, rows, XS * width), jnp.bfloat16)
-
-
-def gather_weights(shards, ident, unit=16):
-    count = len(shards)
-    groups = grouped(range(count), shards[0].shape[0], unit)
-    return pl.pallas_call(
-        partial(gather_kernel, groups, count),
-        out_shape=[whole_shape(shard) for shard in shards],
-        in_specs=[VMEM] * count,
-        out_specs=[HBM] * count,
-        scratch_shapes=gather_scratch(groups, count),
-        compiler_params=pltpu.CompilerParams(collective_id=ident, has_side_effects=True),
-        name="gather_weights",
-    )(*shards)
-
-
-def scatter_kernel(groups, matrices, *refs):
-    parts, sums, scratch = refs[:matrices], refs[matrices : 2 * matrices], refs[2 * matrices :]
-    greet(line_peers())
-    ticks, finish = scatter_plan(groups, parts, sums, scratch[:7], *scratch[7:])
-    for tick in ticks:
-        tick()
-    finish()
-
-
-def split_rows(part):
-    return part.reshape(ZS, YS, part.shape[0] // (ZS * YS), part.shape[1])
-
-
-def scatter_grads(parts, ident, unit=16):
-    parts = [split_rows(part) for part in parts]
-    count = len(parts)
-    rows, width = parts[0].shape[2], parts[0].shape[3] // XS
-    groups = grouped(range(count), rows, unit)
-    return pl.pallas_call(
-        partial(scatter_kernel, groups, count),
-        out_shape=[jax.ShapeDtypeStruct((rows, width), jnp.float32)] * count,
-        in_specs=[HBM] * count,
-        out_specs=[VMEM] * count,
-        scratch_shapes=scatter_scratch(groups, count, rows, width),
-        compiler_params=pltpu.CompilerParams(
-            collective_id=ident, has_side_effects=True, vmem_limit_bytes=60 * 2**20
-        ),
-        name="scatter_grads",
-    )(*parts)
-
-
-def group_of(kind):
+DEVICES = ZS * YS * XS * CORES
+
+
+def numbers():
     z, y, x, core = place()
-    data, tensor = z * YS + y, x * CORES + core
-    if kind == "dp":
-        return ZS * YS, data, lambda i: (i, tensor)
-    if kind == "same_core":
-        return ZS * YS * XS, data * XS + x, lambda i: (i // XS, (i % XS) * CORES + core)
-    return (
-        ZS * YS * XS * CORES,
-        data * XS * CORES + tensor,
-        lambda i: (i // (XS * CORES), i % (XS * CORES)),
-    )
-
-
-def exchange_kernel(kind, gather, blocks, arrived, sends, recvs):
-    count, me, device_of = group_of(kind)
-    targets = [(me + step) % count for step in range(1, count)]
-    greet([device_of(target) for target in targets])
+    data = z * YS + y
+    return (data * XS + x) * CORES + core, data, data * XS + x
+
+
+def device_at(number):
+    return (number // (XS * CORES), number % (XS * CORES))
+
+
+def greet_all():
+    me = numbers()[0]
+    greet([device_at((me + step) % DEVICES) for step in range(1, DEVICES)])
+
+
+def send_each(count, me, source_of, arrived, device_of, sends, recvs):
     copies = []
-    for step, target in enumerate(targets):
+    for step in range(1, count):
+        target = (me + step) % count
         copy = pltpu.make_async_remote_copy(
-            src_ref=blocks if gather else blocks.at[target],
+            src_ref=source_of(target),
             dst_ref=arrived.at[me],
-            send_sem=sends.at[step],
-            recv_sem=recvs.at[step],
+            send_sem=sends.at[step - 1],
+            recv_sem=recvs.at[step - 1],
             device_id=device_of(target),
             device_id_type=MESH_ID,
         )
         copy.start()
         copies.append(copy)
-    arrived[me] = blocks[...] if gather else blocks[me]
-    for copy in copies:
-        copy.wait_send()
+    return copies
+
+
+def receive(copies):
     for copy in copies:
         copy.wait_recv()
 
 
-def exchange(blocks, kind, ident, gather=False):
-    count = {"dp": ZS * YS, "same_core": ZS * YS * XS, "all": ZS * YS * XS * CORES}[kind]
-    shape = blocks.shape if gather else blocks.shape[1:]
+def semaphores_of(*counts):
+    return [pltpu.SemaphoreType.DMA((count,)) for count in counts for _ in range(2)]
+
+
+def gather_kernel(chunks, *refs):
+    shard, silu_blocks, matrix_ref, bias_ref = refs[:4]
+    whole, silu_in, mod_ref = refs[4:7]
+    parts, mod_in, silu_sends, silu_recvs, mod_sends, mod_recvs = refs[7:13]
+    me, data, _ = numbers()
+    z, y, x, core = place()
+    greet_all()
+    silu_copies = send_each(
+        ZS * YS,
+        data,
+        lambda target: silu_blocks.at[target],
+        silu_in,
+        lambda target: (target, lax.axis_index("tensor")),
+        silu_sends,
+        silu_recvs,
+    )
+    start, events, finish = gather_plan(chunks, GATHER_SPACING, [shard], [whole], *refs[13:])
+    start()
+    early = len(chunks) // 2
+    run_all(events[:early])
+    silu_in[data] = silu_blocks[data]
+    receive(silu_copies)
+    rows = silu_in[...].reshape(silu_in.shape[0] * silu_in.shape[1], silu_in.shape[2])
+    product = jnp.dot(
+        rows.astype(jnp.bfloat16), matrix_ref[...], preferred_element_type=jnp.float32
+    )
+    product = product + bias_ref[...]
+    lines = product.shape[1] // LANES
+    for line in range(lines):
+        piece = product[:, line * LANES : (line + 1) * LANES]
+        parts[:, :, line, :] = piece.reshape(parts.shape[0], parts.shape[1], LANES)
+    for line in range(lines, parts.shape[2]):
+        parts[:, :, line, :] = jnp.zeros((parts.shape[0], parts.shape[1], LANES), jnp.float32)
+    run_all(events[early : 2 * early])
+    mod_copies = send_each(
+        DEVICES,
+        me,
+        lambda target: parts.at[target // (XS * CORES), target % (XS * CORES) // CORES],
+        mod_in,
+        device_at,
+        mod_sends,
+        mod_recvs,
+    )
+    mod_in[me] = parts[data, x]
+    run_all(events[2 * early :])
+    receive(mod_copies)
+    for column in range(XS * CORES):
+        total = mod_in[column]
+        for row in range(1, ZS * YS):
+            total = total + mod_in[row * XS * CORES + column]
+        mod_ref[column] = total
+    for copy in silu_copies + mod_copies:
+        copy.wait_send()
+    finish()
+
+
+def whole_shape(shard):
+    rows, width = shard.shape
+    return jax.ShapeDtypeStruct((ZS, YS, rows, XS * width), jnp.bfloat16)
+
+
+def gather_first(shard, silu_blocks, matrix, bias, ident):
+    chunks = grouped(1, shard.shape[0], [16])
+    groups, rows, _ = silu_blocks.shape
+    lines = -(-matrix.shape[1] // (8 * LANES)) * 8
     return pl.pallas_call(
-        partial(exchange_kernel, kind, gather),
-        out_shape=jax.ShapeDtypeStruct((count,) + shape, blocks.dtype),
-        in_specs=[VMEM],
-        out_specs=VMEM,
+        partial(gather_kernel, chunks),
+        out_shape=[
+            whole_shape(shard),
+            jax.ShapeDtypeStruct(silu_blocks.shape, jnp.float32),
+            jax.ShapeDtypeStruct((XS * CORES, lines, LANES), jnp.float32),
+        ],
+        in_specs=[VMEM] * 4,
+        out_specs=[HBM, VMEM, VMEM],
         scratch_shapes=[
-            pltpu.SemaphoreType.DMA((count - 1,)),
-            pltpu.SemaphoreType.DMA((count - 1,)),
+            pltpu.VMEM((groups, rows, lines, LANES), jnp.float32),
+            pltpu.VMEM((DEVICES, lines, LANES), jnp.float32),
+        ]
+        + semaphores_of(groups - 1, DEVICES - 1)
+        + gather_scratch(chunks, 1),
+        compiler_params=pltpu.CompilerParams(collective_id=ident, has_side_effects=True),
+        name="gather_first",
+    )(shard, silu_blocks, matrix, bias)
+
+
+def scatter_kernel(chunks, matrices, lines, *refs):
+    pieces, (small_ref, matrix_ref) = refs[: 4 * matrices], refs[4 * matrices : 4 * matrices + 2]
+    refs = refs[4 * matrices + 2 :]
+    sums, (small_in, cond_ref), refs = refs[:matrices], refs[matrices : matrices + 2], refs[matrices + 2 :]
+    silu_parts, cond_in, small_sends, small_recvs, cond_sends, cond_recvs = refs[:6]
+    buffers, semaphores = refs[6 : 6 + 4 * matrices], refs[6 + 4 * matrices :]
+    me, data, chip = numbers()
+    z, y, x, core = place()
+    chips = ZS * YS * XS
+    greet_all()
+    small_copies = send_each(
+        chips,
+        chip,
+        lambda target: small_ref.at[target % XS],
+        small_in,
+        lambda target: (target // XS, target % XS * CORES + core),
+        small_sends,
+        small_recvs,
+    )
+    events, finish = scatter_plan(chunks, SCATTER_SPACING, pieces, sums, buffers, *semaphores)
+    run_all(events[: len(chunks)])
+    small_in[chip] = small_ref[x]
+    silu_parts[...] = jnp.zeros_like(silu_parts)
+    receive(small_copies)
+    total = jnp.zeros((chips, matrix_ref.shape[0]), jnp.float32)
+    for line in range(lines):
+        total = total + contract(
+            small_in[:, line, :].astype(jnp.bfloat16),
+            matrix_ref[:, line * LANES : (line + 1) * LANES],
+            1,
+            1,
+        )
+    for image in range(chips):
+        at = image % XS
+        silu_parts[image // XS, at : at + 1, :] = total[image : image + 1, :]
+    middle = 2 * len(chunks)
+    run_all(events[len(chunks) : middle])
+    cond_copies = send_each(
+        DEVICES,
+        me,
+        lambda target: silu_parts.at[target // (XS * CORES)],
+        cond_in,
+        device_at,
+        cond_sends,
+        cond_recvs,
+    )
+    cond_in[me] = silu_parts[data]
+    run_all(events[middle:])
+    receive(cond_copies)
+    for row in range(ZS * YS):
+        total = cond_in[row * XS * CORES]
+        for column in range(1, XS * CORES):
+            total = total + cond_in[row * XS * CORES + column]
+        cond_ref[row] = total
+    for copy in small_copies + cond_copies:
+        copy.wait_send()
+    finish()
+
+
+def scatter_last(pieces, units, small, matrix, lines, ident):
+    count = len(pieces)
+    chunks = scatter_chunks(pieces, units)
+    shapes = [sum_shape(piece) for piece in pieces]
+    depth = matrix.shape[0]
+    results = pl.pallas_call(
+        partial(scatter_kernel, chunks, count, lines),
+        out_shape=[jax.ShapeDtypeStruct(shape, jnp.float32) for shape in shapes]
+        + [
+            jax.ShapeDtypeStruct((ZS * YS * XS,) + small.shape[1:], jnp.float32),
+            jax.ShapeDtypeStruct((ZS * YS, 8, depth), jnp.float32),
         ],
-        compiler_params=pltpu.CompilerParams(collective_id=ident, has_side_effects=True),
-        name="exchange_" + kind,
-    )(blocks)
+        in_specs=[VMEM] * (4 * count + 2),
+        out_specs=[VMEM] * (count + 2),
+        scratch_shapes=[
+            pltpu.VMEM((ZS * YS, 8, depth), jnp.float32),
+            pltpu.VMEM((DEVICES, 8, depth), jnp.float32),
+        ]
+        + semaphores_of(ZS * YS * XS - 1, DEVICES - 1)
+        + scatter_scratch(chunks, shapes),
+        compiler_params=pltpu.CompilerParams(
+            collective_id=ident, has_side_effects=True, vmem_limit_bytes=60 * 2**20
+        ),
+        name="scatter_last",
+    )(*[array for piece in pieces for array in piece], small, matrix)
+    return results[:count], results[count], results[count + 1]
 
 
 QUARTER = HEAD // 4
@@ -887,23 +953,26 @@
     return values * cosine - swapped if back else values * cosine + swapped
 
 
-def spread(ticks, index, trips):
-    for number, tick in enumerate(ticks):
-        pl.when(index == number * trips // len(ticks))(tick)
-
-
-def attend_kernel(heads, scale, groups, *refs):
-    projected, (cos_ref, left_ref, right_ref, hide_ref) = refs[:2], refs[2:6]
-    shards, out_refs = refs[6:8], refs[8:10]
-    query_ref, key_ref, value_ref, logsum_ref = refs[10:14]
-    wholes, held, gather_scratch_refs = refs[14:16], refs[16], refs[17:]
-    slots = cos_ref.shape[0]
+def head_lanes(source, at, start, end):
+    short = max(start + LANES - end, 0)
+    values = source[at, start - short : start - short + LANES]
+    return pltpu.roll(values, LANES - short, axis=1) if short else values
+
+
+def attend_kernel(heads, scale, chunks, matrices, *refs):
+    projected, (cos_ref, left_ref, right_ref, hide_ref) = refs[0], refs[1:5]
+    shards, refs = refs[5 : 5 + matrices], refs[5 + matrices :]
+    out_ref, (query_ref, key_ref, value_ref, logsum_ref) = refs[0], refs[1:5]
+    wholes, held, gather_refs = refs[5 : 5 + matrices], refs[5 + matrices], refs[6 + matrices :]
+    slots, half_width = cos_ref.shape[0], projected.shape[1] // XS
     per = heads // 2
     blocks = slots // BLOCK
     greet(line_peers())
-    start, ticks, end = gather_plan(groups, shards, wholes, *gather_scratch_refs)
+    start, events, end = gather_plan(chunks, GATHER_SPACING, shards, wholes, *gather_refs)
     start()
-    ticks[0]()
+    table = table_of(events, GATHER_WEIGHTS, heads * blocks + 1)
+    for event in table[0]:
+        event()
 
     def prepare(i, carry):
         at = pl.ds(pl.multiple_of(i * BLOCK, BLOCK), BLOCK)
@@ -911,10 +980,10 @@
         hide = hide_ref[at, :]
         lane = lax.broadcasted_iota(jnp.int32, (BLOCK, LANES), 1)
         for head in range(heads):
-            source, local = projected[head // per], head % per
+            half, local = head // per, head % per
             for part, target in enumerate((query_ref, key_ref, value_ref)):
-                start = (part * per + local) * HEAD
-                values = source[at, start : start + LANES]
+                start = half * half_width + (part * per + local) * HEAD
+                values = head_lanes(projected, at, start, XS * half_width)
                 if part == 2:
                     values = jnp.where(lane < HEAD, values, 0.0)
                 else:
@@ -926,7 +995,7 @@
     lax.fori_loop(0, blocks, prepare, 0)
 
     def attend(i, carry):
-        spread(ticks[1:], i, heads * blocks)
+        dispatch(table[1:], i, 0, heads * blocks)
         head, block = i // blocks, i % blocks
         at = pl.ds(pl.multiple_of(block * BLOCK, BLOCK), BLOCK)
         scores = contract(query_ref[head, at, :], key_ref[head], 1, 1)
@@ -943,67 +1012,69 @@
         return carry
 
     lax.fori_loop(0, heads * blocks, attend, 0)
+    out_half = out_ref.shape[1] // XS
 
     def finish(i, carry):
         at = pl.ds(pl.multiple_of(i * BLOCK, BLOCK), BLOCK)
+        padding = jnp.zeros((BLOCK, out_half - per * HEAD), jnp.float32)
         for half in range(2):
-            row = jnp.concatenate(
-                [held[half * per + local, at, :][:, :HEAD] for local in range(per)], 1
-            )
-            out_refs[half][at, :] = row.astype(jnp.bfloat16)
+            pieces = [held[half * per + local, at, :][:, :HEAD] for local in range(per)]
+            row = jnp.concatenate(pieces + [padding], 1)
+            out_ref[at, half * out_half : (half + 1) * out_half] = row.astype(jnp.bfloat16)
         return carry
 
     lax.fori_loop(0, blocks, finish, 0)
     end()
 
 
-def attend(projected, tables, shards, heads, scale, ident):
-    slots = projected[0].shape[0]
+def attend(projected, tables, shards, units, out_half, heads, scale, ident):
+    slots = projected.shape[0]
     count = len(shards)
-    groups = grouped(range(count), shards[0].shape[0], 16)
+    chunks = grouped(count, shards[0].shape[0], units)
     packed = jax.ShapeDtypeStruct((heads, slots, LANES), jnp.bfloat16)
-    half = jax.ShapeDtypeStruct((slots, heads // 2 * HEAD), jnp.bfloat16)
     results = pl.pallas_call(
-        partial(attend_kernel, heads, scale, groups),
+        partial(attend_kernel, heads, scale, chunks, count),
         out_shape=[
-            half,
-            half,
+            jax.ShapeDtypeStruct((slots, XS * out_half), jnp.bfloat16),
             packed,
             packed,
             packed,
             jax.ShapeDtypeStruct((heads, slots, LANES), jnp.float32),
         ]
         + [whole_shape(shard) for shard in shards],
-        in_specs=[VMEM] * (6 + count),
-        out_specs=[VMEM] * 6 + [HBM] * count,
+        in_specs=[VMEM] * (5 + count),
+        out_specs=[VMEM] * 5 + [HBM] * count,
         scratch_shapes=[pltpu.VMEM((heads, slots, LANES), jnp.float32)]
-        + gather_scratch(groups, count),
+        + gather_scratch(chunks, count),
         compiler_params=pltpu.CompilerParams(
             collective_id=ident, has_side_effects=True, vmem_limit_bytes=60 * 2**20
         ),
         name="attend",
-    )(*projected, *tables, *shards)
-    return results[:2], results[2:6], results[6:]
-
-
-def attend_back_kernel(heads, scale, groups, *refs):
+    )(projected, *tables, *shards)
+    return results[0], results[1:5], results[5:]
+
+
+def attend_back_kernel(heads, scale, chunks, matrices, *refs):
     query_ref, key_ref, value_ref, logsum_ref = refs[:4]
-    grads, (cos_ref, left_ref, right_ref) = refs[4:6], refs[6:9]
-    parts, out_refs, sums = refs[9:11], refs[11:13], refs[13:15]
-    held, grad_q, grad_k, grad_v = refs[15:19]
-    buffers, semaphores = refs[19:26], refs[26:]
-    slots = cos_ref.shape[0]
+    grads, (cos_ref, left_ref, right_ref) = refs[4], refs[5:8]
+    pieces, refs = refs[8 : 8 + 4 * matrices], refs[8 + 4 * matrices :]
+    out_ref, sums, refs = refs[0], refs[1 : 1 + matrices], refs[1 + matrices :]
+    held, grad_q, grad_k, grad_v = refs[:4]
+    buffers, semaphores = refs[4 : 4 + 4 * matrices], refs[4 + 4 * matrices :]
+    slots, grad_half, out_half = cos_ref.shape[0], grads.shape[1] // XS, out_ref.shape[1] // XS
     per = heads // 2
     blocks = slots // BLOCK
     greet(line_peers())
-    ticks, end = scatter_plan(groups, parts, sums, buffers, *semaphores)
-    ticks[0]()
+    events, end = scatter_plan(chunks, SCATTER_SPACING, pieces, sums, buffers, *semaphores)
+    table = table_of(events, SCATTER_WEIGHTS, heads * blocks + 1)
+    for event in table[0]:
+        event()
 
     def prepare(i, carry):
         at = pl.ds(pl.multiple_of(i * BLOCK, BLOCK), BLOCK)
         for head in range(heads):
-            local = head % per
-            piece = grads[head // per][at, local * HEAD : (local + 1) * HEAD]
+            start = head // per * grad_half + head % per * HEAD
+            piece = grads[at, start : start + HEAD]
             padding = jnp.zeros((BLOCK, LANES - HEAD), piece.dtype)
             held[head, at, :] = jnp.concatenate([piece, padding], 1)
         return carry
@@ -1011,7 +1082,7 @@
     lax.fori_loop(0, blocks, prepare, 0)
 
     def attend(i, carry):
-        spread(ticks[1:], i, heads * blocks)
+        dispatch(table[1:], i, 0, heads * blocks)
         head, block = i // blocks, i % blocks
         at = pl.ds(pl.multiple_of(block * BLOCK, BLOCK), BLOCK)
         query, grad = query_ref[head, at, :], held[head, at, :]
@@ -1043,41 +1114,43 @@
     def finish(i, carry):
         at = pl.ds(pl.multiple_of(i * BLOCK, BLOCK), BLOCK)
         tables = cos_ref[at, :], left_ref[at, :], right_ref[at, :]
+        padding = jnp.zeros((BLOCK, out_half - 3 * per * HEAD), jnp.float32)
         for half in range(2):
-            pieces = []
+            row = []
             for part, source in enumerate((grad_q, grad_k, grad_v)):
                 for local in range(per):
                     values = source[half * per + local, at, :]
                     if part < 2:
                         values = turn(values, tables, True)
-                    pieces.append(values[:, :HEAD])
-            out_refs[half][at, :] = jnp.concatenate(pieces, 1).astype(jnp.bfloat16)
+                    row.append(values[:, :HEAD])
+            row = jnp.concatenate(row + [padding], 1)
+            out_ref[at, half * out_half : (half + 1) * out_half] = row.astype(jnp.bfloat16)
         return carry
 
     lax.fori_loop(0, blocks, finish, 0)
     end()
 
 
-def attend_back(saved, grads, tables, parts, heads, scale, ident):
-    parts = [split_rows(part) for part in parts]
-    count, rows, width = len(parts), parts[0].shape[2], parts[0].shape[3] // XS
-    groups = grouped(range(count), rows, 16)
-    slots = grads[0].shape[0]
-    half = jax.ShapeDtypeStruct((slots, 3 * (heads // 2) * HEAD), jnp.bfloat16)
+def attend_back(saved, grads, tables, pieces, units, out_half, heads, scale, ident):
+    count = len(pieces)
+    chunks = scatter_chunks(pieces, units)
+    shapes = [sum_shape(piece) for piece in pieces]
+    slots = grads.shape[0]
     wide = pltpu.VMEM((heads, slots, LANES), jnp.float32)
     results = pl.pallas_call(
-        partial(attend_back_kernel, heads, scale, groups),
-        out_shape=[half, half] + [jax.ShapeDtypeStruct((rows, width), jnp.float32)] * count,
-        in_specs=[VMEM] * 9 + [HBM] * count,
-        out_specs=[VMEM] * (2 + count),
+        partial(attend_back_kernel, heads, scale, chunks, count),
+        out_shape=[jax.ShapeDtypeStruct((slots, XS * out_half), jnp.bfloat16)]
+        + [jax.ShapeDtypeStruct(shape, jnp.float32) for shape in shapes],
+        in_specs=[VMEM] * (8 + 4 * count),
+        out_specs=[VMEM] * (1 + count),
         scratch_shapes=[pltpu.VMEM((heads, slots, LANES), jnp.bfloat16), wide, wide, wide]
-        + scatter_scratch(groups, count, rows, width),
+        + scatter_scratch(chunks, shapes),
         compiler_params=pltpu.CompilerParams(
             collective_id=ident, has_side_effects=True, vmem_limit_bytes=63 * 2**20
         ),
         name="attend_back",
-    )(*saved, *grads, *tables[:3], *parts)
-    return results[:2], results[2:]
+    )(*saved, grads, *tables[:3], *[array for piece in pieces for array in piece])
+    return results[0], results[1:]
 
 
 def turn_tables(positions, visible):
@@ -1131,33 +1204,36 @@
     def own_sum(terms):
         return terms[:own_rows] + swap(terms[own_rows:].astype(bf16)).astype(jnp.float32)
 
-    silu_cond = jax.nn.silu(conditioning).astype(bf16)
-    every = exchange(
-        silu_cond.astype(jnp.float32).reshape(-1, LANES), "dp", 0, gather=True
-    ).reshape(images, model_width)
-    silu_rows = lax.dynamic_slice_in_dim(every, data * shard_rows, shard_rows, 1).astype(bf16)
-    mod_matrix = w_mod.astype(bf16).reshape(shard_rows, 6 * feat)
-    mod_part = jnp.dot(silu_rows, mod_matrix, preferred_element_type=jnp.float32)
-    mod_part = mod_part + jnp.where(data == 0, b_mod.reshape(-1), 0.0)
-    mod_part = jnp.broadcast_to(
-        mod_part.reshape(images, 1, 8, -1), (images, CORES, 8, 6 * feat // 8)
-    ).reshape(images * CORES, 8, -1)
-    mod_parts = exchange(mod_part, "all", 1).reshape(ZS * YS, XS * CORES, 6, feat)
-    mod = mod_parts.sum(0).transpose(1, 0, 2).reshape(6, model_width)
+    qkv_width = 3 * feat
+    qkv_half, out_half = -(-qkv_width // LANES) * LANES, -(-feat // LANES) * LANES
+    qkv_shard = jnp.pad(
+        w_qkv.reshape(shard_rows, qkv_width).astype(bf16), ((0, 0), (0, qkv_half - qkv_width))
+    )
+    out_shard = jnp.pad(w_out.T.astype(bf16), ((0, 0), (0, out_half - feat)))
+    shards = [out_shard, w_up.astype(bf16), w_down.T.astype(bf16)]
+
+    depth, lines = -(-shard_rows // LANES) * LANES, 6 * out_half // LANES
+    silu_cond = jax.nn.silu(conditioning).astype(bf16).astype(jnp.float32)
+    silu_blocks = silu_cond.reshape(XS, ZS * YS, shard_rows).transpose(1, 0, 2)
+    silu_blocks = jnp.pad(silu_blocks, ((0, 0), (0, 8 - XS), (0, depth - shard_rows)))
+    mod_matrix = jnp.pad(
+        w_mod.astype(bf16), ((0, depth - shard_rows), (0, 0), (0, out_half - feat))
+    ).reshape(depth, -1)
+    mod_bias = jnp.pad(jnp.where(data == 0, b_mod, 0.0), ((0, 0), (0, out_half - feat)))
+    whole, silu_in, mod_parts = gather_first(
+        qkv_shard, silu_blocks, mod_matrix, mod_bias.reshape(1, -1), 2
+    )
+    qkv_full = whole.reshape(model_width, -1)
+    silu_rows = silu_in[:, :XS, :shard_rows].reshape(images, shard_rows).astype(bf16)
+    mod_parts = mod_parts[:, :lines].reshape(XS * CORES, 6, out_half)[:, :, :feat]
+    mod = mod_parts.transpose(1, 0, 2).reshape(6, model_width)
     shift_one, scale_one, gate_one, shift_two, scale_two, gate_two = (mod[i] for i in range(6))
-
-    shards = [
-        jnp.concatenate([w_qkv.reshape(shard_rows, 3 * feat), w_out.T], 1).astype(bf16),
-        w_up.astype(bf16),
-        w_down.T.astype(bf16),
-    ]
-    first = gather_weights(shards[:1], 2)[0].reshape(model_width, -1)
-    biases = jnp.concatenate([b_qkv.reshape(-1), b_up])
+    biases = jnp.concatenate([jnp.pad(b_qkv.reshape(-1), (0, qkv_half - qkv_width)), b_up])
     other_biases = lax.ppermute(biases, "tensor", X_SWAP)
     low_biases = jnp.where(x == 0, biases, other_biases)
     high_biases = jnp.where(x == 0, other_biases, biases)
-    qkv_width = 3 * feat
-    joined = first.shape[1] // XS
+    bias_qkv = jnp.concatenate([low_biases[:qkv_half], high_biases[:qkv_half]])
+    bias_up = jnp.concatenate([low_biases[qkv_half:], high_biases[qkv_half:]])
 
     own_slots = core * own_rows + jnp.arange(own_rows)
     other_slots = (1 - core) * own_rows + jnp.arange(own_rows)
@@ -1173,23 +1249,22 @@
     tables = turn_tables(places, visible)
 
     normal_one, inverse_one = row_norm(block_input)
-    hidden_one = both((normal_one * (1.0 + scale_one) + shift_one).astype(bf16))
-    projected = []
-    for half, bias in enumerate((low_biases, high_biases)):
-        matrix = first[:, half * joined : half * joined + 8 * LANES]
-        row = jnp.pad(bias[:qkv_width], (0, 8 * LANES - qkv_width))
-        projected.append(jnp.dot(hidden_one, matrix, preferred_element_type=jnp.float32) + row)
-    attended, saved, wholes = attend(projected, tables, shards[1:], heads, scale, 3)
-    up_full, down_full = (whole.reshape(model_width, -1) for whole in wholes)
-    out_parts = [first[:, half * joined + qkv_width : (half + 1) * joined] for half in range(2)]
-    branch_one = (
-        own_sum(contract(attended[0], out_parts[0], 1, 1) + contract(attended[1], out_parts[1], 1, 1))
-        + b_out
-    )
+    normal_other = row_norm(swap(block_input))[0]
+    hidden_one = jnp.concatenate(
+        [
+            (normal * (1.0 + scale_one) + shift_one).astype(bf16)
+            for normal in (normal_one, normal_other)
+        ]
+    )
+    projected = jnp.dot(hidden_one, qkv_full, preferred_element_type=jnp.float32) + bias_qkv
+    attended, saved, wholes = attend(
+        projected, tables, shards, [48, 16, 16], out_half, heads, scale, 3
+    )
+    out_full, up_full, down_full = (whole.reshape(model_width, -1) for whole in wholes)
+    branch_one = own_sum(contract(attended, out_full, 1, 1)) + b_out
     middle = block_input + gate_one * branch_one
     normal_two, inverse_two = row_norm(middle)
     hidden_two = both((normal_two * (1.0 + scale_two) + shift_two).astype(bf16))
-    bias_up = jnp.concatenate([low_biases[qkv_width:], high_biases[qkv_width:]])
     up_pre = jnp.dot(hidden_two, up_full, preferred_element_type=jnp.float32) + bias_up
     activated = gelu_tanh(up_pre).astype(bf16)
     branch_two = own_sum(contract(activated, down_full, 1, 1)) + b_down
@@ -1208,10 +1283,13 @@
     grad_rows_two = both((cotangent * gate_two).astype(bf16))
     grad_bdown = column_sum(grad_rows_two)
     grad_down = contract(grad_rows_two, activated, 0, 0).astype(bf16)
+    sent_down, grad_rows_two = send_off(grad_down, 0, grad_rows_two)
     grad_activated = jnp.dot(grad_rows_two, down_full, preferred_element_type=jnp.float32)
     grad_up = jax.vjp(gelu_tanh, up_pre)[1](grad_activated)[0].astype(bf16)
     grad_bup = column_sum(grad_up)
     grad_wup = contract(hidden_two, grad_up, 0, 0).astype(bf16)
+    sent_down, grad_up = arrive_before(sent_down, grad_up)
+    sent_up, grad_up = send_off(grad_wup, 1, grad_up)
     grad_hidden_two = own_sum(contract(grad_up, up_full, 1, 1))
     grad_shift_two = jnp.sum(grad_hidden_two, 0)
     grad_scale_two = jnp.sum(grad_hidden_two * normal_two, 0)
@@ -1219,30 +1297,27 @@
     grad_gate_one = jnp.sum(grad_middle * branch_one, 0)
     grad_rows_one = both((grad_middle * gate_one).astype(bf16))
     grad_bout = column_sum(grad_rows_one)
-    grad_attended = [
-        jnp.dot(grad_rows_one, part, preferred_element_type=jnp.float32).astype(bf16)
-        for part in out_parts
-    ]
+    grad_out = contract(grad_rows_one, attended, 0, 0).astype(bf16)
+    sent_out, grad_rows_one = send_off(grad_out, 1, grad_rows_one)
+    grad_attended = jnp.dot(grad_rows_one, out_full, preferred_element_type=jnp.float32)
     grad_projected, (sum_down, sum_up) = attend_back(
-        saved, grad_attended, tables, [grad_down, grad_wup], heads, scale, 6
-    )
-    first_parts, hidden_terms, bias_terms = [], 0.0, []
-    for half in range(2):
-        first_parts.append(contract(hidden_one, grad_projected[half], 0, 0).astype(bf16))
-        first_parts.append(contract(grad_rows_one, attended[half], 0, 0).astype(bf16))
-        matrix = first[:, half * joined : half * joined + qkv_width]
-        hidden_terms = hidden_terms + contract(grad_projected[half], matrix, 1, 1)
-        bias_terms.append(column_sum(grad_projected[half]))
-    grad_first = jnp.concatenate(first_parts, 1)
-    grad_hidden_one = own_sum(hidden_terms)
+        saved,
+        grad_attended.astype(bf16),
+        tables,
+        [settle(sent_down), settle(sent_up)],
+        [16, 16],
+        qkv_half,
+        heads,
+        scale,
+        6,
+    )
+    grad_qkv = contract(hidden_one, grad_projected, 0, 0).astype(bf16)
+    sent_qkv, grad_projected = send_off(grad_qkv, 0, grad_projected)
+    bias_terms = column_sum(grad_projected).reshape(2, qkv_half)
+    grad_hidden_one = own_sum(contract(grad_projected, qkv_full, 1, 1))
     grad_shift_one = jnp.sum(grad_hidden_one, 0)
     grad_scale_one = jnp.sum(grad_hidden_one * normal_one, 0)
     grad_input = grad_middle + norm_back(grad_hidden_one, normal_one, inverse_one, scale_one)
-
-    sum_first = scatter_grads([grad_first], 7)[0]
-    grad_wqkv = sum_first[:, :qkv_width].reshape(shard_rows, 3, feat)
-    grad_wout = sum_first[:, qkv_width:].T
-    grad_wdown = sum_down.T
 
     grad_mod = jnp.stack(
         [
@@ -1257,8 +1332,9 @@
     grad_mod = (grad_mod + swap(grad_mod)).astype(bf16).astype(jnp.float32)
     grad_mod = grad_mod.reshape(6, XS, CORES, feat)
     grad_mod = lax.dynamic_index_in_dim(grad_mod, core, 2, False)
-    small = 6 * feat + qkv_width + units + 2 * model_width
-    lines = -(-small // LANES)
+    grad_mod = jnp.pad(grad_mod, ((0, 0), (0, 0), (0, out_half - feat)))
+    small = qkv_half + units + 2 * model_width
+    rest = -(-(lines * LANES + small) // (8 * LANES)) * 8 * LANES - lines * LANES - small
     sends = []
     for half in range(2):
         flat = jnp.concatenate(
@@ -1268,29 +1344,28 @@
                 grad_bup[half * units : (half + 1) * units],
                 grad_bout,
                 grad_bdown,
+                jnp.zeros(rest, jnp.float32),
             ]
         )
-        sends.append(jnp.pad(flat, (0, lines * LANES - small)).reshape(1, lines, LANES))
-    blocks = jnp.broadcast_to(jnp.stack(sends, 1), (ZS * YS, 2, lines, LANES))
-    small_all = exchange(blocks.reshape(images, lines, LANES), "same_core", 4).reshape(images, -1)
-    mod_all = small_all[:, : 6 * feat]
+        sends.append(flat.reshape(-1, LANES))
+    (sum_out, sum_qkv), small_all, silu_sum = scatter_last(
+        [settle(sent_out), settle(sent_qkv)], [48, 16], jnp.stack(sends), mod_matrix, lines, 7
+    )
+    grad_wqkv = sum_qkv[:, :qkv_width].reshape(shard_rows, 3, feat)
+    grad_wout = sum_out[:, :feat].T
+    grad_wdown = sum_down.T
     summed = jnp.sum(small_all, 0)
-    grad_bmod = summed[: 6 * feat].reshape(6, feat)
-    offset = 6 * feat
-    grad_bqkv = summed[offset : offset + qkv_width].reshape(3, feat)
-    offset += qkv_width
-    grad_bup = summed[offset : offset + units]
-    offset += units
+    grad_bmod = summed[:lines].reshape(6, out_half)[:, :feat]
+    summed = summed[lines:].reshape(-1)
+    grad_bqkv = summed[:qkv_width].reshape(3, feat)
+    grad_bup = summed[qkv_half : qkv_half + units]
+    offset = qkv_half + units
     grad_bout = summed[offset : offset + model_width]
     grad_bdown = summed[offset + model_width : offset + 2 * model_width]
-    mod_all = mod_all.astype(bf16)
+    mod_all = small_all[:, :lines].reshape(images, 6, out_half)[:, :, :feat]
+    mod_all = mod_all.reshape(images, 6 * feat).astype(bf16)
     grad_wmod = contract(silu_rows, mod_all, 0, 0).reshape(shard_rows, 6, feat)
-    silu_part = contract(mod_all, mod_matrix, 1, 1).reshape(ZS * YS, 1, -1)
-    silu_part = jnp.pad(silu_part, ((0, 0), (0, 0), (0, 8 * LANES - XS * shard_rows)))
-    silu_part = jnp.broadcast_to(silu_part, (ZS * YS, XS * CORES, 8 * LANES))
-    silu_all = exchange(silu_part.reshape(-1, 8, LANES), "all", 5)
-    silu_all = silu_all.reshape(ZS * YS, XS * CORES, -1)[:, :, : XS * shard_rows].sum(1)
-    grad_silu = silu_all.reshape(ZS * YS, XS, shard_rows).transpose(1, 0, 2).reshape(XS, model_width)
+    grad_silu = silu_sum[:, :XS, :shard_rows].transpose(1, 0, 2).reshape(XS, model_width)
     grad_cond = jax.vjp(jax.nn.silu, conditioning)[1](grad_silu)[0]
     return (
         block_output,
@@ -1307,7 +1382,6 @@
         grad_wdown,
         grad_bdown,
     )
-
 
 def solution(mesh):
     body = image_device if image_per_chip(mesh) else per_device

time: 675 us -> 609 us (0.902)
  Pallas kernels: 424 us -> 327 us
  waiting for transfers between devices: 0.36 us -> 38.1 us
  matrix products: 126 us -> 104 us
    pallas_call x8 -> x4, Pallas kernels: 424 us -> 327 us  [the longest x1 141 us: attend(): pl.pallas_call(partial(attend_kernel, heads, scale, chunks, count), out_s...]
    ppermute x0 -> x8, waiting for transfers between devices: none -> 38.1 us  [the longest x4 19.8 us: send_off(): got_x = lax.ppermute(send_x, 'tensor', X_SWAP)]
    unnamed x128 -> x145, local copies, waits for them, and re-layouts: 12.3 us -> 24.7 us
    dot_general x5 -> x2, matrix products: 20.3 us -> 11.1 us  [the longest x1 7.7 us: image_device(): jnp.dot(hidden_one, qkv_full, preferred_element_type=jnp.float32) + bias_qkv]
    concatenate x1 -> x0, local copies, waits for them, and re-layouts: 8.54 us -> none  [image_device(): grad_first = jnp.concatenate(first_parts, 1)]
    select_n x2 -> x10, other arithmetic: 0.78 us -> 8.14 us  [the longest x4 4.3 us: settle(): jnp.where(x == 0, high, low)]
    dot_general x14 -> x9, matrix products: 68.6 us -> 61.3 us  [contract(): lax.dot_general(left, right, (((left_dim,), (right_dim,)), ((), ())), pre...]
  transfers between devices with their start and end apart: 10 -> 18, of which waited for: 1 -> 4; matrix products, arithmetic and copies ran while one was open for 16% -> 20% of each run, Pallas kernels for 22% -> 10%
where the time goes in v3:
time: 609 us; the launch traced here: 598 us
  Pallas kernels  327 us (54%)
  matrix products  104 us (17%)
  local copies, waits for them, and re-layouts  59.8 us (10%)
  other arithmetic  57.7 us (9%)
  waiting for transfers between devices  38.1 us (6%)
  starting transfers between devices  10.3 us (2%)
    pallas_call x1, Pallas kernels, attend(): pl.pallas_call(partial(attend_kernel, heads, scale, chunks, count), out_s...  141 us
    pallas_call x1, Pallas kernels, attend_back(): pl.pallas_call(partial(attend_back_kernel, heads, scale, chunks, count),...  74.1 us
    dot_general x9, matrix products, contract(): lax.dot_general(left, right, (((left_dim,), (right_dim,)), ((), ())), pre...  61.3 us
    pallas_call x1, Pallas kernels, gather_first(): pl.pallas_call(partial(gather_kernel, chunks), out_shape=[whole_shape(sha...  59.4 us
    pallas_call x1, Pallas kernels, scatter_last(): pl.pallas_call(partial(scatter_kernel, chunks, count, lines), out_shape=[...  51.9 us
    unnamed x145, local copies, waits for them, and re-layouts  24.7 us
    ppermute x4, waiting for transfers between devices, send_off(): got_x = lax.ppermute(send_x, 'tensor', X_SWAP)  19.8 us
    dot_general x1, matrix products, image_device(): jnp.dot(grad_rows_two, down_full, preferred_element_type=jnp.float32)  19.6 us
  transfers between devices with their start and end apart: 18, of which 4 were waited for; matrix products, arithmetic and copies ran while one was open for 20% of the time, Pallas kernels for 10%

profile of v3, /device:TPU:0, one launch (start us, length us, event | category | flops | bytes accessed | tf_op | source)
XLA Modules:
  0.0 598.5 jit_solution(14701757119605519478)
XLA Ops:
  2.8 3.0 collective-permute-start.1
  17.8 59.4 %gather_first.1 = (bf16[4,2,144,1792]{3,2,1,0:T(8,128)(2,1)}, f32[8,8,256]{2,1,0:T(8,128)}, f32[4,24,128]{2,1,0:T(8,128)}) custom-call(bf16[144,896]{1,0:T(8,128)(2,1)} %pad.30.refs_0_, f32[8,8,256]{2,1,0:T(8,128)} %pad_convert_fusion.refs_1_, bf16[256,2304]{1,0:T(8,128)(2,1)} %copy.46.refs_2_.refs_9_, f32[1,2304]{1,0:T(1,128)} %bitcast.140), custom_call_target="tpu_custom_call" | custom-call | tf_op jit(solution)/shard_map/gather_first/pallas_call | solution.py:836
  79.6 4.1 fusion.14
  90.2 2.6 add_convert_fusion.4
  93.1 7.7 %broadcast_add_fusion.refs_0_ = f32[1024,1792]{1,0:T(8,128)} fusion(f32[1792]{0:T(1024)S(1)} %pad_maximum_fusion.12, bf16[1152,1792]{1,0:T(8,128)(2,1)S(1)} %bitcast.151, bf16[512,1152]{1,0:T(8,128)(2,1)S(1)} %get-tuple-element.171, bf16[512,1152]{1,0:T(8,128)(2,1)S(1)} %get-tuple-element.170), kind=kOutput, calls=%fused_computation.18 | convolution fusion | flops 4234412032 | bytes 13835264 | tf_op jit(solution)/shard_map/dot_general | solution.py:1259
  100.8 141.4 %attend.1 = (bf16[1024,768]{1,0:T(8,128)(2,1)}, bf16[8,1024,128]{2,1,0:T(8,128)(2,1)}, bf16[8,1024,128]{2,1,0:T(8,128)(2,1)}, bf16[8,1024,128]{2,1,0:T(8,128)(2,...) custom-call(f32[1024,1792]{1,0:T(8,128)} %broadcast_add_fusion.refs_, ...), custom_call_target="tpu_custom_call" | custom-call | tf_op jit(solution)/shard_map/attend/pallas_call | solution.py:1035
  242.2 4.2 fusion.45
  254.3 2.8 fusion.41
  264.4 11.6 %fusion.11 = f32[1024,2304]{1,0:T(8,128)} fusion(bf16[1152,2304]{1,0:T(8,128)(2,1)} %bitcast.147, bf16[512,1152]{1,0:T(8,128)(2,1)} %collective-permute-done.3, bf16[512,1152]{1,0:T(8,128)(2,1)S(1)} %add_convert_fusion.2), kind=kOutput, calls=%fused_computation.66 | convolution fusion | flops 5440536576 | bytes 17104896 | tf_op jit(solution)/shard_map/dot_general | solution.py:1268
  276.0 9.7 %convolution_convert_fusion.1 = bf16[1152,2304]{1,0:T(8,128)(2,1)S(1)} fusion(bf16[512,1152]{1,0:T(8,128)(2,1)} %collective-permute-done.5, bf16[512,1152]{1,0:T(8,128)(2,1)S(1)} %multiply_convert_fusion.2, f32[1024,2304]{1,0:T(8,128)} %fusion.11, f32[2304]{0:T(1024)S(1)} %pad_maximum_fusion.11), kind=kOutput, calls=%fused_computation.5 | convolution fusion | flops 5466783744 | bytes 17114112 | tf_op jit(solution)/shard_map/dot_general | solution.py:44
  288.6 12.5 %fusion.40 = f32[1024,1152]{1,0:T(8,128)S(1)} fusion(bf16[1152,2304]{1,0:T(8,128)(2,1)} %bitcast.149, f32[1024,2304]{1,0:T(8,128)} %fusion.11, f32[2304]{0:T(1024)S(1)} %pad_maximum_fusion.11), kind=kOutput, calls=%fused_computation.203 | convolution fusion | flops 5459410944 | bytes 19473408 | tf_op jit(solution)/shard_map/dot_general | solution.py:44
  301.1 19.6 %convert_reduce_fusion = (f32[2304]{0:T(1024)}, bf16[1024,2304]{1,0:T(8,128)(2,1)}) fusion(f32[1024,2304]{1,0:T(8,128)} %fusion.11, f32[2304]{0:T(1024)S(1)} %pad_maximum_fusion.11, bf16[1024,1152]{1,0:T(8,128)(2,1)S(1)} %pad_maximum_fusion.2, bf16[1152,2304]{1,0:T(8,128)(2,1)} %bitcast.150), kind=kOutput, calls=%fused_computation.12 | convolution fusion | flops 5499516928 | bytes 21841920 | tf_op jit(solution)/shard_map/dot_general | solution.py:1287
  322.4 9.0 %convolution_convert_fusion = bf16[1152,2304]{1,0:T(8,128)(2,1)S(1)} fusion(bf16[1024,2304]{1,0:T(8,128)(2,1)} %get-tuple-element.56, bf16[512,1152]{1,0:T(8,128)(2,1)} %collective-permute-done.3, bf16[512,1152]{1,0:T(8,128)(2,1)S(1)} %copy-done.25), kind=kOutput, calls=%fused_computation.4 | convolution fusion | flops 5443190784 | bytes 12386304 | tf_op jit(solution)/shard_map/dot_general | solution.py:44
  333.9 10.3 %fusion.46 = f32[1024,1152]{1,0:T(8,128)S(1)} fusion(bf16[1024,2304]{1,0:T(8,128)(2,1)} %get-tuple-element.56, bf16[1152,2304]{1,0:T(8,128)(2,1)} %bitcast.148), kind=kOutput, calls=%fused_computation.208 | convolution fusion | flops 5435817984 | bytes 14745600 | tf_op jit(solution)/shard_map/dot_general | solution.py:44
  352.9 5.2 multiply_reduce_fusion
  358.4 16.9 %collective-permute-done.10 = bf16[4,64,2304]{2,1,0:T(8,128)(2,1)S(1)} collective-permute-done((bf16[4,64,2304]{2,1,0:T(8,128)(2,1)S(1)}, bf16[4,64,2304]{2,1,0:T(8,128)(2,1)S(1)}, u32[]{:S(2)}, u32[]{:S(2)}) %collective-permute-start.10) | collective-permute-done | bytes 1179680 | tf_op jit(solution)/shard_map/ppermute | solution.py:551
  378.5 4.1 collective-permute-done.11
  391.7 3.4 convolution_convert_fusion.4.refs_4_
  395.1 74.1 %attend_back.1 = (bf16[1024,1792]{1,0:T(8,128)(2,1)}, f32[144,1152]{1,0:T(8,128)}, f32[144,1152]{1,0:T(8,128)}) custom-call(bf16[8,1024,128]{2,1,0:T(8,128)(2,1)} %get-tuple-element.57.refs_0_, bf16[8,1024,128]{2,1,0:T(8,128)(2,1)} %get-tuple-element.58.refs_1_, bf16[8,1024,128]{2,1,0:T(8,128)(2,1)} %get-tuple-element.59.refs_2_, ...), custom_call_target="tpu_custom_call" | custom-call | tf_op jit(solution)/shard_map/attend_back/pallas_call | solution.py:1140
  469.2 7.3 %convolution_convert_fusion.2 = bf16[1152,1792]{1,0:T(8,128)(2,1)S(1)} fusion(bf16[1024,1792]{1,0:T(8,128)(2,1)} %get-tuple-element.67, bf16[512,1152]{1,0:T(8,128)(2,1)} %copy-done.23, bf16[512,1152]{1,0:T(8,128)(2,1)} %copy-done.22), kind=kOutput, calls=%fused_computation.14 | convolution fusion | flops 4234641408 | bytes 10158080 | tf_op jit(solution)/shard_map/dot_general | solution.py:44
  479.8 4.9 fusion.47
  490.9 15.7 %collective-permute-done.16 = bf16[4,2,64,896]{3,2,1,0:T(8,128)(2,1)S(1)} collective-permute-done((bf16[4,2,64,896]{3,2,1,0:T(8,128)(2,1)S(1)}, bf16[4,2,64,896]{3,2,1,0:T(8,128)(2,1)S(1)}, u32[]{:S(2)}, u32[]{:S(2)}) %collective-permute-start.16) | collective-permute-done | bytes 917536 | tf_op jit(solution)/shard_map/ppermute | solution.py:552
  515.8 4.9 multiply_add_fusion.2
  533.0 51.9 %scatter_last.1 = (f32[144,384]{1,0:T(8,128)}, f32[144,896]{1,0:T(8,128)}, f32[16,56,128]{2,1,0:T(8,128)}, f32[8,8,256]{2,1,0:T(8,128)}) custom-call(bf16[4,64,384]{2,1,0:T(8,128)(2,1)} %get-tuple-element.164.refs_0_, bf16[4,64,384]{2,1,0:T(8,128)(2,1)} %get-tuple-element.163.refs_1_, bf16[4,80,384]{2,1,0:T(8,128)(2,1)} %get-tuple-element.162.refs_2_, ...), custom_call_target="tpu_custom_call" | custom-call | tf_op jit(solution)/shard_map/scatter_last/pallas_call | solution.py:920
  (312 shorter events, 110.3 us)
Async XLA Ops:
  2.8 83.9 %collective-permute-start.1 = (f32[2048]{0:T(1024)}, f32[2048]{0:T(1024)}, u32[]{:S(2)}, u32[]{:S(2)}) collective-permute-start(f32[2048]{0:T(1024)} %select_maximum_fusion), channel_id=1, source_target_pairs={{0,2},{2,0},{1,3},{3,1},{4,6},{6,4},{5,7},{7,5},{8,10},{10,8},{9,1... | collective-permute-start | bytes 24584 | tf_op jit(solution)/shard_map/ppermute | solution.py:1232
  5.8 82.3 %collective-permute-start = (f32[512,1152]{1,0:T(8,128)}, f32[512,1152]{1,0:T(8,128)}, u32[]{:S(2)}, u32[]{:S(2)}) collective-permute-start(f32[512,1152]{1,0:T(8,128)} %param.15), channel_id=1, source_target_pairs={{0,1},{1,0},{2,3},{3,2},{4,5},{5,4},{6,7},{7,6},{8,9},{9,8},{10,11... | collective-permute-start | bytes 7077896 | tf_op jit(solution)/shard_map/ppermute | solution.py:1199
  16.3 61.8 %copy-start = (f32[512,1152]{1,0:T(8,128)S(1)}, f32[512,1152]{1,0:T(8,128)}, u32[]{:S(2)}) copy-start(f32[512,1152]{1,0:T(8,128)} %param.15) | copy-start | bytes 7077892
  17.8 60.8 %copy-start.58 = (pred[128]{0:T(512)(128)(4,1)S(1)}, pred[128]{0:T(512)(128)(4,1)}, u32[]{:S(2)}) copy-start(pred[128]{0:T(512)(128)(4,1)} %iota_compare_fusion.1) | copy-start | bytes 388
  17.8 61.8 %copy-start.55 = (pred[128]{0:T(512)(128)(4,1)S(1)}, pred[128]{0:T(512)(128)(4,1)}, u32[]{:S(2)}) copy-start(pred[128]{0:T(512)(128)(4,1)} %iota_compare_fusion.3) | copy-start | bytes 388
  17.8 61.8 %copy-start.56 = (pred[128]{0:T(512)(128)(4,1)S(1)}, pred[128]{0:T(512)(128)(4,1)}, u32[]{:S(2)}) copy-start(pred[128]{0:T(512)(128)(4,1)} %get-tuple-element.193) | copy-start | bytes 388
  17.8 61.8 %copy-start.57 = (pred[128]{0:T(512)(128)(4,1)S(1)}, pred[128]{0:T(512)(128)(4,1)}, u32[]{:S(2)}) copy-start(pred[128]{0:T(512)(128)(4,1)} %get-tuple-element.194) | copy-start | bytes 388
  17.8 61.8 %copy-start.59 = (f32[128]{0:T(128)S(1)}, f32[128]{0:T(128)}, u32[]{:S(2)}) copy-start(f32[128]{0:T(128)} %fusion.31) | copy-start | bytes 1540
  249.6 4.7 collective-permute-start.2
  251.5 9.2 %collective-permute-start.5 = (bf16[512,1152]{1,0:T(8,128)(2,1)S(1)}, bf16[512,1152]{1,0:T(8,128)(2,1)}, u32[]{:S(2)}, u32[]{:S(2)}) collective-permute-start(bf16[512,1152]{1,0:T(8,128)(2,1)S(1)} %multiply_convert_fusion.2), channel_id=1, source_target_pairs={{0,1},{1,0},{2,3},{3,2},{4,5},{5,4},{6,7},{7,6},{8,9},{9,8},{10,11... | collective-permute-start | bytes 3538952 | tf_op jit(solution)/shard_map/ppermute | solution.py:1199
  259.0 5.4 collective-permute-start.3
  287.2 45.7 %collective-permute-start.7 = (bf16[4,2,64,1152]{3,2,1,0:T(8,128)(2,1)}, bf16[4,2,64,1152]{3,2,1,0:T(8,128)(2,1)S(1)}, u32[]{:S(2)}, u32[]{:S(2)}) collective-permute-start(bf16[4,2,64,1152]{3,2,1,0:T(8,128)(2,1)} %broadcast_select_fusion.1), channel_id=1, source_target_pairs={{0,2},{2,0},{1,3},{3,1},{4,6},{6,4},{5,7},{7,5},{8,10},{10,8},{9,1... | collective-permute-start | bytes 3538952 | tf_op jit(solution)/shard_map/ppermute | solution.py:552
  287.8 46.1 %collective-permute-start.6 = (bf16[4,80,2304]{2,1,0:T(8,128)(2,1)S(1)}, bf16[4,80,2304]{2,1,0:T(8,128)(2,1)S(1)}, u32[]{:S(2)}, u32[]{:S(2)}) collective-permute-start(bf16[4,80,2304]{2,1,0:T(8,128)(2,1)S(1)} %dynamic-slice_bitcast_fusion), channel_id=1, source_target_pairs={{0,4},{4,0},{8,12},{12,8},{16,20},{20,16},{24,28},{28,24},{1,5},{5... | collective-permute-start | bytes 4423688 | tf_op jit(solution)/shard_map/ppermute | solution.py:551
  321.8 30.7 %collective-permute-start.4 = (bf16[512,1152]{1,0:T(8,128)(2,1)}, bf16[512,1152]{1,0:T(8,128)(2,1)}, u32[]{:S(2)}, u32[]{:S(2)}) collective-permute-start(bf16[512,1152]{1,0:T(8,128)(2,1)} %slice.454), channel_id=1, source_target_pairs={{0,1},{1,0},{2,3},{3,2},{4,5},{5,4},{6,7},{7,6},{8,9},{9,8},{10,11... | collective-permute-start | bytes 3538952 | tf_op jit(solution)/shard_map/ppermute | solution.py:1199
  344.4 6.9 %collective-permute-start.8 = (bf16[512,1152]{1,0:T(8,128)(2,1)S(1)}, bf16[512,1152]{1,0:T(8,128)(2,1)S(1)}, u32[]{:S(2)}, u32[]{:S(2)}) collective-permute-start(bf16[512,1152]{1,0:T(8,128)(2,1)S(1)} %slice.453), channel_id=1, source_target_pairs={{0,1},{1,0},{2,3},{3,2},{4,5},{5,4},{6,7},{7,6},{8,9},{9,8},{10,11... | collective-permute-start | bytes 3538952 | tf_op jit(solution)/shard_map/ppermute | solution.py:1199
  347.4 27.8 %collective-permute-start.10 = (bf16[4,64,2304]{2,1,0:T(8,128)(2,1)S(1)}, bf16[4,64,2304]{2,1,0:T(8,128)(2,1)S(1)}, u32[]{:S(2)}, u32[]{:S(2)}) collective-permute-start(bf16[4,64,2304]{2,1,0:T(8,128)(2,1)S(1)} %copy-done.21), channel_id=1, source_target_pairs={{0,4},{4,0},{8,12},{12,8},{16,20},{20,16},{24,28},{28,24},{1,5},{5... | collective-permute-start | bytes 3538952 | tf_op jit(solution)/shard_map/ppermute | solution.py:551
  348.7 33.9 %collective-permute-start.11 = (bf16[4,2,80,1152]{3,2,1,0:T(8,128)(2,1)S(1)}, bf16[4,2,80,1152]{3,2,1,0:T(8,128)(2,1)S(1)}, u32[]{:S(2)}, u32[]{:S(2)}) collective-permute-start(bf16[4,2,80,1152]{3,2,1,0:T(8,128)(2,1)S(1)} %broadcast_select_fusion), channel_id=1, source_target_pairs={{0,2},{2,0},{1,3},{3,1},{4,6},{6,4},{5,7},{7,5},{8,10},{10,8},{9,1... | collective-permute-start | bytes 4423688 | tf_op jit(solution)/shard_map/ppermute | solution.py:552
  358.3 26.1 %collective-permute-start.9 = (bf16[512,1152]{1,0:T(8,128)(2,1)S(1)}, bf16[512,1152]{1,0:T(8,128)(2,1)S(1)}, u32[]{:S(2)}, u32[]{:S(2)}) collective-permute-start(bf16[512,1152]{1,0:T(8,128)(2,1)S(1)} %multiply_convert_fusion.1), channel_id=1, source_target_pairs={{0,1},{1,0},{2,3},{3,2},{4,5},{5,4},{6,7},{7,6},{8,9},{9,8},{10,11... | collective-permute-start | bytes 3538952 | tf_op jit(solution)/shard_map/ppermute | solution.py:1199
  476.8 12.2 %collective-permute-start.13 = (bf16[4,64,768]{2,1,0:T(8,128)(2,1)}, bf16[4,64,768]{2,1,0:T(8,128)(2,1)S(1)}, u32[]{:S(2)}, u32[]{:S(2)}) collective-permute-start(bf16[4,64,768]{2,1,0:T(8,128)(2,1)} %dynamic-slice_bitcast_fusion.9), channel_id=1, source_target_pairs={{0,4},{4,0},{8,12},{12,8},{16,20},{20,16},{24,28},{28,24},{1,5},{5... | collective-permute-start | bytes 1179656 | tf_op jit(solution)/shard_map/ppermute | solution.py:551
  477.3 12.6 %collective-permute-start.14 = (bf16[4,2,80,384]{3,2,1,0:T(8,128)(2,1)}, bf16[4,2,80,384]{3,2,1,0:T(8,128)(2,1)S(1)}, u32[]{:S(2)}, u32[]{:S(2)}) collective-permute-start(bf16[4,2,80,384]{3,2,1,0:T(8,128)(2,1)} %broadcast_select_fusion.9), channel_id=1, source_target_pairs={{0,2},{2,0},{1,3},{3,1},{4,6},{6,4},{5,7},{7,5},{8,10},{10,8},{9,1... | collective-permute-start | bytes 1474568 | tf_op jit(solution)/shard_map/ppermute | solution.py:552
  484.7 21.9 %collective-permute-start.16 = (bf16[4,2,64,896]{3,2,1,0:T(8,128)(2,1)S(1)}, bf16[4,2,64,896]{3,2,1,0:T(8,128)(2,1)S(1)}, u32[]{:S(2)}, u32[]{:S(2)}) collective-permute-start(bf16[4,2,64,896]{3,2,1,0:T(8,128)(2,1)S(1)} %broadcast_select_fusion.2), channel_id=1, source_target_pairs={{0,2},{2,0},{1,3},{3,1},{4,6},{6,4},{5,7},{7,5},{8,10},{10,8},{9,1... | collective-permute-start | bytes 2752520 | tf_op jit(solution)/shard_map/ppermute | solution.py:552
  485.3 24.1 %collective-permute-start.15 = (bf16[4,80,1792]{2,1,0:T(8,128)(2,1)S(1)}, bf16[4,80,1792]{2,1,0:T(8,128)(2,1)S(1)}, u32[]{:S(2)}, u32[]{:S(2)}) collective-permute-start(bf16[4,80,1792]{2,1,0:T(8,128)(2,1)S(1)} %dynamic-slice_bitcast_fusion.2), channel_id=1, source_target_pairs={{0,4},{4,0},{8,12},{12,8},{16,20},{20,16},{24,28},{28,24},{1,5},{5... | collective-permute-start | bytes 3440648 | tf_op jit(solution)/shard_map/ppermute | solution.py:551
  486.1 24.7 %collective-permute-start.12 = (bf16[512,1152]{1,0:T(8,128)(2,1)S(1)}, bf16[512,1152]{1,0:T(8,128)(2,1)S(1)}, u32[]{:S(2)}, u32[]{:S(2)}) collective-permute-start(bf16[512,1152]{1,0:T(8,128)(2,1)S(1)} %slice.452), channel_id=1, source_target_pairs={{0,1},{1,0},{2,3},{3,2},{4,5},{5,4},{6,7},{7,6},{8,9},{9,8},{10,11... | collective-permute-start | bytes 3538952 | tf_op jit(solution)/shard_map/ppermute | solution.py:1199
  515.8 4.9 collective-permute-start.17
  (60 other events, 460.8 us)

commit v4 on v3

--- a/solution.py
+++ b/solution.py
@@ -1267,8 +1267,6 @@
     hidden_two = both((normal_two * (1.0 + scale_two) + shift_two).astype(bf16))
     up_pre = jnp.dot(hidden_two, up_full, preferred_element_type=jnp.float32) + bias_up
     activated = gelu_tanh(up_pre).astype(bf16)
-    branch_two = own_sum(contract(activated, down_full, 1, 1)) + b_down
-    block_output = middle + gate_two * branch_two
 
     def norm_back(grad_hidden, normal, inverse, factor):
         grad_normal = grad_hidden * (1.0 + factor)
@@ -1279,7 +1277,6 @@
     def column_sum(values):
         return jnp.sum(values.astype(jnp.float32), 0)
 
-    grad_gate_two = jnp.sum(cotangent * branch_two, 0)
     grad_rows_two = both((cotangent * gate_two).astype(bf16))
     grad_bdown = column_sum(grad_rows_two)
     grad_down = contract(grad_rows_two, activated, 0, 0).astype(bf16)
@@ -1290,13 +1287,20 @@
     grad_wup = contract(hidden_two, grad_up, 0, 0).astype(bf16)
     sent_down, grad_up = arrive_before(sent_down, grad_up)
     sent_up, grad_up = send_off(grad_wup, 1, grad_up)
-    grad_hidden_two = own_sum(contract(grad_up, up_full, 1, 1))
+    hidden_terms = contract(grad_up, up_full, 1, 1)
+    other_terms = swap(hidden_terms[own_rows:].astype(bf16))
+    other_terms, activated = lax.optimization_barrier((other_terms, activated))
+    grad_hidden_two = hidden_terms[:own_rows] + other_terms.astype(jnp.float32)
+    branch_two = own_sum(contract(activated, down_full, 1, 1)) + b_down
+    block_output = middle + gate_two * branch_two
+    grad_gate_two = jnp.sum(cotangent * branch_two, 0)
     grad_shift_two = jnp.sum(grad_hidden_two, 0)
     grad_scale_two = jnp.sum(grad_hidden_two * normal_two, 0)
     grad_middle = cotangent + norm_back(grad_hidden_two, normal_two, inverse_two, scale_two)
     grad_gate_one = jnp.sum(grad_middle * branch_one, 0)
     grad_rows_one = both((grad_middle * gate_one).astype(bf16))
     grad_bout = column_sum(grad_rows_one)
+    sent_up, grad_rows_one = arrive_before(sent_up, grad_rows_one)
     grad_out = contract(grad_rows_one, attended, 0, 0).astype(bf16)
     sent_out, grad_rows_one = send_off(grad_out, 1, grad_rows_one)
     grad_attended = jnp.dot(grad_rows_one, out_full, preferred_element_type=jnp.float32)

time: 609 us -> 598 us (0.982)
  matrix products: 104 us -> 91.4 us
  waiting for transfers between devices: 38.1 us -> 27.8 us
    ppermute x4, waiting for transfers between devices: 18.3 us -> 6.38 us  [send_off(): got_y = lax.ppermute(send_y, 'dp', Y_SWAP)]
    dot_general x9, matrix products: 61.3 us -> 52.2 us  [contract(): lax.dot_general(left, right, (((left_dim,), (right_dim,)), ((), ())), pre...]
    unnamed x145 -> x171, local copies, waits for them, and re-layouts: 24.7 us -> 30.1 us
  transfers between devices with their start and end apart: 18 -> 18, of which waited for: 4 -> 6; matrix products, arithmetic and copies ran while one was open for 20% -> 17% of each run, Pallas kernels for 10% -> 10%
where the time goes in v4:
time: 598 us; the launch traced here: 587 us
  Pallas kernels  326 us (55%)
  matrix products  91.4 us (15%)
  local copies, waits for them, and re-layouts  65.5 us (11%)
  other arithmetic  61.5 us (10%)
  waiting for transfers between devices  27.8 us (5%)
  starting transfers between devices  11.8 us (2%)
    pallas_call x1, Pallas kernels, attend(): pl.pallas_call(partial(attend_kernel, heads, scale, chunks, count), out_s...  141 us
    pallas_call x1, Pallas kernels, attend_back(): pl.pallas_call(partial(attend_back_kernel, heads, scale, chunks, count),...  74.2 us
    pallas_call x1, Pallas kernels, gather_first(): pl.pallas_call(partial(gather_kernel, chunks), out_shape=[whole_shape(sha...  59.4 us
    dot_general x9, matrix products, contract(): lax.dot_general(left, right, (((left_dim,), (right_dim,)), ((), ())), pre...  52.2 us
    pallas_call x1, Pallas kernels, scatter_last(): pl.pallas_call(partial(scatter_kernel, chunks, count, lines), out_shape=[...  51.4 us
    unnamed x171, local copies, waits for them, and re-layouts  30.1 us
    ppermute x4, waiting for transfers between devices, send_off(): got_x = lax.ppermute(send_x, 'tensor', X_SWAP)  20.2 us
    dot_general x1, matrix products, image_device(): jnp.dot(grad_rows_two, down_full, preferred_element_type=jnp.float32)  15.2 us
  transfers between devices with their start and end apart: 18, of which 6 were waited for; matrix products, arithmetic and copies ran while one was open for 17% of the time, Pallas kernels for 10%

profile of v4, /device:TPU:0, one launch (start us, length us, event | category | flops | bytes accessed | tf_op | source)
XLA Modules:
  0.0 586.5 jit_solution(932659732548921904)
XLA Ops:
  2.8 3.0 collective-permute-start.1
  17.8 59.4 %gather_first.1 = (bf16[4,2,144,1792]{3,2,1,0:T(8,128)(2,1)}, f32[8,8,256]{2,1,0:T(8,128)}, f32[4,24,128]{2,1,0:T(8,128)}) custom-call(bf16[144,896]{1,0:T(8,128)(2,1)} %pad.30.refs_0_, f32[8,8,256]{2,1,0:T(8,128)} %pad_convert_fusion.refs_1_, bf16[256,2304]{1,0:T(8,128)(2,1)} %copy.46.refs_2_.refs_9_, f32[1,2304]{1,0:T(1,128)} %bitcast.145), custom_call_target="tpu_custom_call" | custom-call | tf_op jit(solution)/shard_map/gather_first/pallas_call | solution.py:836
  79.6 4.1 fusion.14
  93.1 7.7 %broadcast_add_fusion.refs_0_ = f32[1024,1792]{1,0:T(8,128)} fusion(f32[1792]{0:T(1024)S(1)} %pad_maximum_fusion.12, bf16[1152,1792]{1,0:T(8,128)(2,1)S(1)} %bitcast.160, bf16[512,1152]{1,0:T(8,128)(2,1)S(1)} %get-tuple-element.181, bf16[512,1152]{1,0:T(8,128)(2,1)S(1)} %get-tuple-element.180), kind=kOutput, calls=%fused_computation.18 | convolution fusion | flops 4234412032 | bytes 13835264 | tf_op jit(solution)/shard_map/dot_general | solution.py:1259
  100.8 141.4 %attend.1 = (bf16[1024,768]{1,0:T(8,128)(2,1)}, bf16[8,1024,128]{2,1,0:T(8,128)(2,1)}, bf16[8,1024,128]{2,1,0:T(8,128)(2,1)}, bf16[8,1024,128]{2,1,0:T(8,128)(2,...) custom-call(f32[1024,1792]{1,0:T(8,128)} %broadcast_add_fusion.refs_, ...), custom_call_target="tpu_custom_call" | custom-call | tf_op jit(solution)/shard_map/attend/pallas_call | solution.py:1035
  242.3 4.2 fusion.44
  254.6 2.8 fusion.40
  262.3 13.0 %multiply_convert_fusion = (bf16[1024,2304]{1,0:T(8,128)(2,1)S(1)}, f32[1024,2304]{1,0:T(8,128)}) fusion(f32[2304]{0:T(1024)S(1)} %pad_maximum_fusion.11, bf16[1152,2304]{1,0:T(8,128)(2,1)} %bitcast.156, bf16[512,1152]{1,0:T(8,128)(2,1)} %collective-permute-done.3, bf16[512,1152]{1,0:T(8,128)(2,1)S(1)} %add_convert_fusion.2), kind=kOutput, calls=%fused_computation.13 | convolution fusion | flops 5464129536 | bytes 21832704 | tf_op jit(solution)/shard_map/dot_general | solution.py:1268
  275.3 8.4 %convolution_convert_fusion.1 = bf16[1152,2304]{1,0:T(8,128)(2,1)S(1)} fusion(bf16[1024,2304]{1,0:T(8,128)(2,1)S(1)} %get-tuple-element.62, bf16[512,1152]{1,0:T(8,128)(2,1)} %collective-permute-done.4, bf16[512,1152]{1,0:T(8,128)(2,1)S(1)} %multiply_convert_fusion.2), kind=kOutput, calls=%fused_computation.5 | convolution fusion | flops 5443190784 | bytes 12386304 | tf_op jit(solution)/shard_map/dot_general | solution.py:44
  288.1 15.2 %convert_reduce_fusion = (f32[2304]{0:T(1024)}, bf16[1024,2304]{1,0:T(8,128)(2,1)S(1)}) fusion(f32[1024,2304]{1,0:T(8,128)} %get-tuple-element.204, f32[2304]{0:T(1024)S(1)} %pad_maximum_fusion.11, bf16[1024,1152]{1,0:T(8,128)(2,1)S(1)} %pad_maximum_fusion.2, bf16[1152,2304]{1,0:T(8,128)(2,1)S(1)} %bitcast.155), kind=kOutput, calls=%fused_computation.12 | convolution fusion | flops 5499516928 | bytes 21841920 | tf_op jit(solution)/shard_map/dot_general | solution.py:1284
  303.3 7.5 %convolution_convert_fusion = bf16[1152,2304]{1,0:T(8,128)(2,1)S(1)} fusion(bf16[1024,2304]{1,0:T(8,128)(2,1)S(1)} %get-tuple-element.61, bf16[512,1152]{1,0:T(8,128)(2,1)} %collective-permute-done.3, bf16[512,1152]{1,0:T(8,128)(2,1)S(1)} %copy-done.31), kind=kOutput, calls=%fused_computation.4 | convolution fusion | flops 5443190784 | bytes 12386304 | tf_op jit(solution)/shard_map/dot_general | solution.py:44
  314.9 6.3 %collective-permute-done.5 = bf16[4,80,2304]{2,1,0:T(8,128)(2,1)S(1)} collective-permute-done((bf16[4,80,2304]{2,1,0:T(8,128)(2,1)S(1)}, bf16[4,80,2304]{2,1,0:T(8,128)(2,1)S(1)}, u32[]{:S(2)}, u32[]{:S(2)}) %collective-permute-start.5) | collective-permute-done | bytes 1474592 | tf_op jit(solution)/shard_map/ppermute | solution.py:551
  321.2 6.3 %fusion.45 = f32[1024,1152]{1,0:T(8,128)S(1)} fusion(bf16[1024,2304]{1,0:T(8,128)(2,1)S(1)} %get-tuple-element.61, bf16[1152,2304]{1,0:T(8,128)(2,1)S(1)} %bitcast.159), kind=kOutput, calls=%fused_computation.207 | convolution fusion | flops 5435817984 | bytes 14745600 | tf_op jit(solution)/shard_map/dot_general | solution.py:44
  332.3 2.8 convert_reduce_fusion.2
  337.3 10.1 %fusion.46 = f32[1024,1152]{1,0:T(8,128)S(1)} fusion(bf16[1024,2304]{1,0:T(8,128)(2,1)} %copy-done.70, bf16[1152,2304]{1,0:T(8,128)(2,1)} %bitcast.152), kind=kOutput, calls=%fused_computation.208 | convolution fusion | flops 5435817984 | bytes 14745600 | tf_op jit(solution)/shard_map/dot_general | solution.py:44
  352.2 5.0 multiply_reduce_fusion
  366.9 3.5 collective-permute-done.10
  379.5 3.4 convolution_convert_fusion.4.refs_4_
  382.9 74.2 %attend_back.1 = (bf16[1024,1792]{1,0:T(8,128)(2,1)}, f32[144,1152]{1,0:T(8,128)}, f32[144,1152]{1,0:T(8,128)}) custom-call(bf16[8,1024,128]{2,1,0:T(8,128)(2,1)} %get-tuple-element.64.refs_0_, bf16[8,1024,128]{2,1,0:T(8,128)(2,1)} %get-tuple-element.65.refs_1_, bf16[8,1024,128]{2,1,0:T(8,128)(2,1)} %get-tuple-element.66.refs_2_, ...), custom_call_target="tpu_custom_call" | custom-call | tf_op jit(solution)/shard_map/attend_back/pallas_call | solution.py:1140
  457.1 7.3 %convolution_convert_fusion.2 = bf16[1152,1792]{1,0:T(8,128)(2,1)S(1)} fusion(bf16[1024,1792]{1,0:T(8,128)(2,1)} %get-tuple-element.77, bf16[512,1152]{1,0:T(8,128)(2,1)} %copy-done.29, bf16[512,1152]{1,0:T(8,128)(2,1)} %copy-done.28), kind=kOutput, calls=%fused_computation.14 | convolution fusion | flops 4234641408 | bytes 10158080 | tf_op jit(solution)/shard_map/dot_general | solution.py:44
  467.7 4.9 fusion.47
  481.7 14.5 %collective-permute-done.16 = bf16[4,2,64,896]{3,2,1,0:T(8,128)(2,1)S(1)} collective-permute-done((bf16[4,2,64,896]{3,2,1,0:T(8,128)(2,1)S(1)}, bf16[4,2,64,896]{3,2,1,0:T(8,128)(2,1)S(1)}, u32[]{:S(2)}, u32[]{:S(2)}) %collective-permute-start.16) | collective-permute-done | bytes 917536 | tf_op jit(solution)/shard_map/ppermute | solution.py:552
  504.6 4.9 multiply_add_fusion.2
  521.7 51.4 %scatter_last.1 = (f32[144,384]{1,0:T(8,128)}, f32[144,896]{1,0:T(8,128)}, f32[16,56,128]{2,1,0:T(8,128)}, f32[8,8,256]{2,1,0:T(8,128)}) custom-call(bf16[4,64,384]{2,1,0:T(8,128)(2,1)} %get-tuple-element.174.refs_0_, bf16[4,64,384]{2,1,0:T(8,128)(2,1)} %get-tuple-element.173.refs_1_, bf16[4,80,384]{2,1,0:T(8,128)(2,1)} %get-tuple-element.172.refs_2_, ...), custom_call_target="tpu_custom_call" | custom-call | tf_op jit(solution)/shard_map/scatter_last/pallas_call | solution.py:920
  (341 shorter events, 123.4 us)
Async XLA Ops:
  2.8 83.9 %collective-permute-start.1 = (f32[2048]{0:T(1024)}, f32[2048]{0:T(1024)}, u32[]{:S(2)}, u32[]{:S(2)}) collective-permute-start(f32[2048]{0:T(1024)} %select_maximum_fusion), channel_id=1, source_target_pairs={{0,2},{2,0},{1,3},{3,1},{4,6},{6,4},{5,7},{7,5},{8,10},{10,8},{9,1... | collective-permute-start | bytes 24584 | tf_op jit(solution)/shard_map/ppermute | solution.py:1232
  5.8 82.3 %collective-permute-start = (f32[512,1152]{1,0:T(8,128)}, f32[512,1152]{1,0:T(8,128)}, u32[]{:S(2)}, u32[]{:S(2)}) collective-permute-start(f32[512,1152]{1,0:T(8,128)} %param.15), channel_id=1, source_target_pairs={{0,1},{1,0},{2,3},{3,2},{4,5},{5,4},{6,7},{7,6},{8,9},{9,8},{10,11... | collective-permute-start | bytes 7077896 | tf_op jit(solution)/shard_map/ppermute | solution.py:1199
  16.3 61.8 %copy-start = (f32[512,1152]{1,0:T(8,128)S(1)}, f32[512,1152]{1,0:T(8,128)}, u32[]{:S(2)}) copy-start(f32[512,1152]{1,0:T(8,128)} %param.15) | copy-start | bytes 7077892
  17.8 60.8 %copy-start.64 = (pred[128]{0:T(512)(128)(4,1)S(1)}, pred[128]{0:T(512)(128)(4,1)}, u32[]{:S(2)}) copy-start(pred[128]{0:T(512)(128)(4,1)} %iota_compare_fusion.1) | copy-start | bytes 388
  17.8 61.8 %copy-start.61 = (pred[128]{0:T(512)(128)(4,1)S(1)}, pred[128]{0:T(512)(128)(4,1)}, u32[]{:S(2)}) copy-start(pred[128]{0:T(512)(128)(4,1)} %iota_compare_fusion.3) | copy-start | bytes 388
  17.8 61.8 %copy-start.62 = (pred[128]{0:T(512)(128)(4,1)S(1)}, pred[128]{0:T(512)(128)(4,1)}, u32[]{:S(2)}) copy-start(pred[128]{0:T(512)(128)(4,1)} %get-tuple-element.205) | copy-start | bytes 388
  17.8 61.8 %copy-start.63 = (pred[128]{0:T(512)(128)(4,1)S(1)}, pred[128]{0:T(512)(128)(4,1)}, u32[]{:S(2)}) copy-start(pred[128]{0:T(512)(128)(4,1)} %get-tuple-element.206) | copy-start | bytes 388
  17.8 61.8 %copy-start.65 = (f32[128]{0:T(128)S(1)}, f32[128]{0:T(128)}, u32[]{:S(2)}) copy-start(f32[128]{0:T(128)} %fusion.31) | copy-start | bytes 1540
  249.8 4.7 collective-permute-start.2
  251.8 7.6 %collective-permute-start.4 = (bf16[512,1152]{1,0:T(8,128)(2,1)S(1)}, bf16[512,1152]{1,0:T(8,128)(2,1)}, u32[]{:S(2)}, u32[]{:S(2)}) collective-permute-start(bf16[512,1152]{1,0:T(8,128)(2,1)S(1)} %multiply_convert_fusion.2), channel_id=1, source_target_pairs={{0,1},{1,0},{2,3},{3,2},{4,5},{5,4},{6,7},{7,6},{8,9},{9,8},{10,11... | collective-permute-start | bytes 3538952 | tf_op jit(solution)/shard_map/ppermute | solution.py:1199
  259.2 3.0 collective-permute-start.3
  286.5 28.4 %collective-permute-start.6 = (bf16[4,2,64,1152]{3,2,1,0:T(8,128)(2,1)S(1)}, bf16[4,2,64,1152]{3,2,1,0:T(8,128)(2,1)S(1)}, u32[]{:S(2)}, u32[]{:S(2)}) collective-permute-start(bf16[4,2,64,1152]{3,2,1,0:T(8,128)(2,1)S(1)} %broadcast_select_fusion.1), channel_id=1, source_target_pairs={{0,2},{2,0},{1,3},{3,1},{4,6},{6,4},{5,7},{7,5},{8,10},{10,8},{9,1... | collective-permute-start | bytes 3538952 | tf_op jit(solution)/shard_map/ppermute | solution.py:552
  287.1 34.1 %collective-permute-start.5 = (bf16[4,80,2304]{2,1,0:T(8,128)(2,1)S(1)}, bf16[4,80,2304]{2,1,0:T(8,128)(2,1)S(1)}, u32[]{:S(2)}, u32[]{:S(2)}) collective-permute-start(bf16[4,80,2304]{2,1,0:T(8,128)(2,1)S(1)} %dynamic-slice_bitcast_fusion), channel_id=1, source_target_pairs={{0,4},{4,0},{8,12},{12,8},{16,20},{20,16},{24,28},{28,24},{1,5},{5... | collective-permute-start | bytes 4423688 | tf_op jit(solution)/shard_map/ppermute | solution.py:551
  330.8 6.5 %collective-permute-start.7 = (bf16[512,1152]{1,0:T(8,128)(2,1)}, bf16[512,1152]{1,0:T(8,128)(2,1)}, u32[]{:S(2)}, u32[]{:S(2)}) collective-permute-start(bf16[512,1152]{1,0:T(8,128)(2,1)} %slice.454), channel_id=1, source_target_pairs={{0,1},{1,0},{2,3},{3,2},{4,5},{5,4},{6,7},{7,6},{8,9},{9,8},{10,11... | collective-permute-start | bytes 3538952 | tf_op jit(solution)/shard_map/ppermute | solution.py:1199
  335.0 31.9 %collective-permute-start.9 = (bf16[4,64,2304]{2,1,0:T(8,128)(2,1)}, bf16[4,64,2304]{2,1,0:T(8,128)(2,1)S(1)}, u32[]{:S(2)}, u32[]{:S(2)}) collective-permute-start(bf16[4,64,2304]{2,1,0:T(8,128)(2,1)} %dynamic-slice_bitcast_fusion.1), channel_id=1, source_target_pairs={{0,4},{4,0},{8,12},{12,8},{16,20},{20,16},{24,28},{28,24},{1,5},{5... | collective-permute-start | bytes 3538952 | tf_op jit(solution)/shard_map/ppermute | solution.py:551
  335.8 34.6 %collective-permute-start.10 = (bf16[4,2,80,1152]{3,2,1,0:T(8,128)(2,1)}, bf16[4,2,80,1152]{3,2,1,0:T(8,128)(2,1)S(1)}, u32[]{:S(2)}, u32[]{:S(2)}) collective-permute-start(bf16[4,2,80,1152]{3,2,1,0:T(8,128)(2,1)} %broadcast_select_fusion), channel_id=1, source_target_pairs={{0,2},{2,0},{1,3},{3,1},{4,6},{6,4},{5,7},{7,5},{8,10},{10,8},{9,1... | collective-permute-start | bytes 4423688 | tf_op jit(solution)/shard_map/ppermute | solution.py:552
  347.6 4.6 collective-permute-start.8
  357.5 8.2 %collective-permute-start.11 = (bf16[512,1152]{1,0:T(8,128)(2,1)S(1)}, bf16[512,1152]{1,0:T(8,128)(2,1)S(1)}, u32[]{:S(2)}, u32[]{:S(2)}) collective-permute-start(bf16[512,1152]{1,0:T(8,128)(2,1)S(1)} %multiply_convert_fusion.1), channel_id=1, source_target_pairs={{0,1},{1,0},{2,3},{3,2},{4,5},{5,4},{6,7},{7,6},{8,9},{9,8},{10,11... | collective-permute-start | bytes 3538952 | tf_op jit(solution)/shard_map/ppermute | solution.py:1199
  464.6 12.9 %collective-permute-start.13 = (bf16[4,64,768]{2,1,0:T(8,128)(2,1)}, bf16[4,64,768]{2,1,0:T(8,128)(2,1)S(1)}, u32[]{:S(2)}, u32[]{:S(2)}) collective-permute-start(bf16[4,64,768]{2,1,0:T(8,128)(2,1)} %dynamic-slice_bitcast_fusion.9), channel_id=1, source_target_pairs={{0,4},{4,0},{8,12},{12,8},{16,20},{20,16},{24,28},{28,24},{1,5},{5... | collective-permute-start | bytes 1179656 | tf_op jit(solution)/shard_map/ppermute | solution.py:551
  466.3 14.3 %collective-permute-start.14 = (bf16[4,2,80,384]{3,2,1,0:T(8,128)(2,1)}, bf16[4,2,80,384]{3,2,1,0:T(8,128)(2,1)S(1)}, u32[]{:S(2)}, u32[]{:S(2)}) collective-permute-start(bf16[4,2,80,384]{3,2,1,0:T(8,128)(2,1)} %broadcast_select_fusion.9), channel_id=1, source_target_pairs={{0,2},{2,0},{1,3},{3,1},{4,6},{6,4},{5,7},{7,5},{8,10},{10,8},{9,1... | collective-permute-start | bytes 1474568 | tf_op jit(solution)/shard_map/ppermute | solution.py:552
  472.6 23.6 %collective-permute-start.16 = (bf16[4,2,64,896]{3,2,1,0:T(8,128)(2,1)S(1)}, bf16[4,2,64,896]{3,2,1,0:T(8,128)(2,1)S(1)}, u32[]{:S(2)}, u32[]{:S(2)}) collective-permute-start(bf16[4,2,64,896]{3,2,1,0:T(8,128)(2,1)S(1)} %broadcast_select_fusion.2), channel_id=1, source_target_pairs={{0,2},{2,0},{1,3},{3,1},{4,6},{6,4},{5,7},{7,5},{8,10},{10,8},{9,1... | collective-permute-start | bytes 2752520 | tf_op jit(solution)/shard_map/ppermute | solution.py:552
  473.4 24.3 %collective-permute-start.15 = (bf16[4,80,1792]{2,1,0:T(8,128)(2,1)S(1)}, bf16[4,80,1792]{2,1,0:T(8,128)(2,1)S(1)}, u32[]{:S(2)}, u32[]{:S(2)}) collective-permute-start(bf16[4,80,1792]{2,1,0:T(8,128)(2,1)S(1)} %dynamic-slice_bitcast_fusion.2), channel_id=1, source_target_pairs={{0,4},{4,0},{8,12},{12,8},{16,20},{20,16},{24,28},{28,24},{1,5},{5... | collective-permute-start | bytes 3440648 | tf_op jit(solution)/shard_map/ppermute | solution.py:551
  474.9 24.3 %collective-permute-start.12 = (bf16[512,1152]{1,0:T(8,128)(2,1)S(1)}, bf16[512,1152]{1,0:T(8,128)(2,1)S(1)}, u32[]{:S(2)}, u32[]{:S(2)}) collective-permute-start(bf16[512,1152]{1,0:T(8,128)(2,1)S(1)} %slice.452), channel_id=1, source_target_pairs={{0,1},{1,0},{2,3},{3,2},{4,5},{5,4},{6,7},{7,6},{8,9},{9,8},{10,11... | collective-permute-start | bytes 3538952 | tf_op jit(solution)/shard_map/ppermute | solution.py:1199
  504.6 4.9 collective-permute-start.17
  (73 other events, 554.2 us)

commit v5 on v4

--- a/solution.py
+++ b/solution.py
@@ -383,6 +383,15 @@
     return chunks
 
 
+def two_hops(matrix, rows):
+    split = y_rows(rows)
+    return [(matrix, row, 16, 4 if row < split else 5) for row in range(0, rows, 16)]
+
+
+def y_rows(rows):
+    return rows - rows // 32 * 16
+
+
 def in_order(count, steps, spacing, act):
     events = sorted((c + s * spacing, c, s) for c in range(count) for s in range(steps))
     return [(s, partial(act, c, s)) for time, c, s in events]
@@ -440,6 +449,7 @@
 
     def moves(number):
         matrix, row, rows, route = chunks[number]
+        complete, route = route < 4, route % 4
         whole, span, mine = wholes[matrix], pl.ds(row, rows), mine_of(matrix)
         own, shard = whole.at[z, y, span, mine], shards[matrix].at[span, :]
         lines, columns = (every if route == 3 else y), (every if route == 2 else mine)
@@ -460,7 +470,9 @@
             last = whole.at[:, y, span, :]
         else:
             last = whole.at[:, :, span, mine]
-        made["third"] = partial(copy, number, 4, 3, last, last, at_y if route in (0, 2) else at_x)
+        if complete:
+            where = at_y if route in (0, 2) else at_x
+            made["third"] = partial(copy, number, 4, 3, last, last, where)
         return made
 
     def keep(matrix):
@@ -478,7 +490,7 @@
 
     def act(number, step):
         made = moves(number)
-        straight = chunks[number][3] < 2
+        straight = chunks[number][3] % 4 < 2
         if step == 0:
             made["near" if straight else "first"]().start()
         elif step == 1:
@@ -503,8 +515,9 @@
             else:
                 made["mirror"]().wait_recv()
                 pl.when(inner)(lambda: made["forward"]().start())
-            made["third"]().start()
-        else:
+            if "third" in made:
+                made["third"]().start()
+        elif "third" in made:
             made["third"]().wait_recv()
 
     def start():
@@ -1030,7 +1043,8 @@
 def attend(projected, tables, shards, units, out_half, heads, scale, ident):
     slots = projected.shape[0]
     count = len(shards)
-    chunks = grouped(count, shards[0].shape[0], units)
+    rows = shards[0].shape[0]
+    chunks = grouped(count - 1, rows, units) + two_hops(count - 1, rows)
     packed = jax.ShapeDtypeStruct((heads, slots, LANES), jnp.bfloat16)
     results = pl.pallas_call(
         partial(attend_kernel, heads, scale, chunks, count),
@@ -1260,7 +1274,13 @@
     attended, saved, wholes = attend(
         projected, tables, shards, [48, 16, 16], out_half, heads, scale, 3
     )
-    out_full, up_full, down_full = (whole.reshape(model_width, -1) for whole in wholes)
+    out_full, up_full = (whole.reshape(model_width, -1) for whole in wholes[:2])
+    split = y_rows(shard_rows)
+    part_y = lax.dynamic_index_in_dim(wholes[2][:, :, :split], y, 1, False)
+    low, high = wholes[2][:, :, split:, :units], wholes[2][:, :, split:, units:]
+    part_x = jnp.where(x == 0, low, high)
+    got_y = lax.ppermute(part_y, "dp", Y_SWAP)
+    got_x = lax.ppermute(part_x, "tensor", X_SWAP)
     branch_one = own_sum(contract(attended, out_full, 1, 1)) + b_out
     middle = block_input + gate_one * branch_one
     normal_two, inverse_two = row_norm(middle)
@@ -1280,7 +1300,16 @@
     grad_rows_two = both((cotangent * gate_two).astype(bf16))
     grad_bdown = column_sum(grad_rows_two)
     grad_down = contract(grad_rows_two, activated, 0, 0).astype(bf16)
-    sent_down, grad_rows_two = send_off(grad_down, 0, grad_rows_two)
+    sent_down, (grad_rows_two, got_y, got_x) = send_off(
+        grad_down, 0, (grad_rows_two, got_y, got_x)
+    )
+    rows_y = jnp.stack(
+        [jnp.where(y == 0, part_y, got_y), jnp.where(y == 0, got_y, part_y)], 1
+    )
+    rows_x = jnp.concatenate(
+        [jnp.where(x == 0, part_x, got_x), jnp.where(x == 0, got_x, part_x)], -1
+    )
+    down_full = jnp.concatenate([rows_y, rows_x], 2).reshape(model_width, -1)
     grad_activated = jnp.dot(grad_rows_two, down_full, preferred_element_type=jnp.float32)
     grad_up = jax.vjp(gelu_tanh, up_pre)[1](grad_activated)[0].astype(bf16)
     grad_bup = column_sum(grad_up)
@@ -1300,7 +1329,6 @@
     grad_gate_one = jnp.sum(grad_middle * branch_one, 0)
     grad_rows_one = both((grad_middle * gate_one).astype(bf16))
     grad_bout = column_sum(grad_rows_one)
-    sent_up, grad_rows_one = arrive_before(sent_up, grad_rows_one)
     grad_out = contract(grad_rows_one, attended, 0, 0).astype(bf16)
     sent_out, grad_rows_one = send_off(grad_out, 1, grad_rows_one)
     grad_attended = jnp.dot(grad_rows_one, out_full, preferred_element_type=jnp.float32)

time: 598 us -> 608 us (1.017)
  waiting for transfers between devices: 27.8 us -> 43 us
  Pallas kernels: 326 us -> 312 us
  other arithmetic: 61.5 us -> 71.6 us
    pallas_call x1, Pallas kernels: 141 us -> 128 us  [attend(): pl.pallas_call(partial(attend_kernel, heads, scale, chunks, count), out_s...]
    ppermute x0 -> x2, waiting for transfers between devices: none -> 12.4 us  [the longest x1 6.77 us: image_device(): got_y = lax.ppermute(part_y, 'dp', Y_SWAP)]
    unnamed x171 -> x145, local copies, waits for them, and re-layouts: 30.1 us -> 18.8 us
    ppermute x4, waiting for transfers between devices: 6.38 us -> 14.4 us  [send_off(): got_y = lax.ppermute(send_y, 'dp', Y_SWAP)]
  transfers between devices with their start and end apart: 18 -> 20, of which waited for: 6 -> 7; matrix products, arithmetic and copies ran while one was open for 17% -> 26% of each run, Pallas kernels for 10% -> 31%
where the time goes in v5:
time: 608 us; the launch traced here: 599 us
  Pallas kernels  312 us (51%)
  matrix products  95.9 us (16%)
  other arithmetic  71.6 us (12%)
  local copies, waits for them, and re-layouts  62 us (10%)
  waiting for transfers between devices  43 us (7%)
  starting transfers between devices  12.4 us (2%)
    pallas_call x1, Pallas kernels, attend(): pl.pallas_call(partial(attend_kernel, heads, scale, chunks, count), out_s...  128 us
    pallas_call x1, Pallas kernels, attend_back(): pl.pallas_call(partial(attend_back_kernel, heads, scale, chunks, count),...  72.9 us
    pallas_call x1, Pallas kernels, gather_first(): pl.pallas_call(partial(gather_kernel, chunks), out_shape=[whole_shape(sha...  59.4 us
    dot_general x9, matrix products, contract(): lax.dot_general(left, right, (((left_dim,), (right_dim,)), ((), ())), pre...  56.9 us
    pallas_call x1, Pallas kernels, scatter_last(): pl.pallas_call(partial(scatter_kernel, chunks, count, lines), out_shape=[...  52.1 us
    unnamed x145, local copies, waits for them, and re-layouts  18.8 us
    dot_general x1, matrix products, image_device(): jnp.dot(grad_rows_two, down_full, preferred_element_type=jnp.float32)  16.8 us
    ppermute x4, waiting for transfers between devices, send_off(): got_x = lax.ppermute(send_x, 'tensor', X_SWAP)  16.3 us
  transfers between devices with their start and end apart: 20, of which 7 were waited for; matrix products, arithmetic and copies ran while one was open for 26% of the time, Pallas kernels for 31%

profile of v5, /device:TPU:0, one launch (start us, length us, event | category | flops | bytes accessed | tf_op | source)
XLA Modules:
  0.0 599.3 jit_solution(6952286144744757346)
XLA Ops:
  2.8 3.0 collective-permute-start.1
  13.1 59.4 %gather_first.1 = (bf16[4,2,144,1792]{3,2,1,0:T(8,128)(2,1)}, f32[8,8,256]{2,1,0:T(8,128)}, f32[4,24,128]{2,1,0:T(8,128)}) custom-call(bf16[144,896]{1,0:T(8,128)(2,1)} %pad.30.refs_0_, f32[8,8,256]{2,1,0:T(8,128)} %pad_convert_fusion.refs_1_, bf16[256,2304]{1,0:T(8,128)(2,1)} %copy.49.refs_2_.refs_9_, f32[1,2304]{1,0:T(1,128)} %bitcast.156), custom_call_target="tpu_custom_call" | custom-call | tf_op jit(solution)/shard_map/gather_first/pallas_call | solution.py:849
  83.2 4.1 fusion.14
  100.6 7.7 %broadcast_add_fusion.refs_0_ = f32[1024,1792]{1,0:T(8,128)} fusion(f32[1792]{0:T(1024)S(1)} %pad_maximum_fusion.12, bf16[1152,1792]{1,0:T(8,128)(2,1)S(1)} %bitcast.167, bf16[512,1152]{1,0:T(8,128)(2,1)S(1)} %get-tuple-element.183, bf16[512,1152]{1,0:T(8,128)(2,1)S(1)} %get-tuple-element.182), kind=kOutput, calls=%fused_computation.19 | convolution fusion | flops 4234412032 | bytes 13835264 | tf_op jit(solution)/shard_map/dot_general | solution.py:1273
  108.3 127.7 %attend.1 = (bf16[1024,768]{1,0:T(8,128)(2,1)}, bf16[8,1024,128]{2,1,0:T(8,128)(2,1)}, bf16[8,1024,128]{2,1,0:T(8,128)(2,1)}, bf16[8,1024,128]{2,1,0:T(8,128)(2,...) custom-call(f32[1024,1792]{1,0:T(8,128)} %broadcast_add_fusion.refs_, ...), custom_call_target="tpu_custom_call" | custom-call | tf_op jit(solution)/shard_map/attend/pallas_call | solution.py:1049
  235.9 4.2 fusion.44
  257.4 3.0 pad_maximum_fusion.2
  262.1 11.1 %multiply_convert_fusion = (bf16[1024,2304]{1,0:T(8,128)(2,1)}, f32[1024,2304]{1,0:T(8,128)}) fusion(f32[2304]{0:T(1024)S(1)} %pad_maximum_fusion.11, bf16[1152,2304]{1,0:T(8,128)(2,1)S(1)} %bitcast.166, bf16[512,1152]{1,0:T(8,128)(2,1)S(1)} %collective-permute-done.3, bf16[512,1152]{1,0:T(8,128)(2,1)S(1)} %add_convert_fusion.2), kind=kOutput, calls=%fused_computation.13 | convolution fusion | flops 5464129536 | bytes 21832704 | tf_op jit(solution)/shard_map/dot_general | solution.py:1288
  273.3 8.6 %convolution_convert_fusion.1 = bf16[1152,2304]{1,0:T(8,128)(2,1)S(1)} fusion(bf16[1024,2304]{1,0:T(8,128)(2,1)} %get-tuple-element.63, bf16[512,1152]{1,0:T(8,128)(2,1)} %collective-permute-done.4, bf16[512,1152]{1,0:T(8,128)(2,1)S(1)} %multiply_convert_fusion.2), kind=kOutput, calls=%fused_computation.5 | convolution fusion | flops 5443190784 | bytes 12386304 | tf_op jit(solution)/shard_map/dot_general | solution.py:44
  283.3 5.6 collective-permute-done.6
  288.9 6.8 %collective-permute-done.5 = bf16[4,80,2304]{2,1,0:T(8,128)(2,1)S(1)} collective-permute-done((bf16[4,80,2304]{2,1,0:T(8,128)(2,1)S(1)}, bf16[4,80,2304]{2,1,0:T(8,128)(2,1)S(1)}, u32[]{:S(2)}, u32[]{:S(2)}) %collective-permute-start.5) | collective-permute-done | bytes 1474592 | tf_op jit(solution)/shard_map/ppermute | solution.py:1282
  301.0 16.8 %convert_reduce_fusion = (f32[2304]{0:T(1024)}, bf16[1024,2304]{1,0:T(8,128)(2,1)}) fusion(f32[1024,2304]{1,0:T(8,128)} %get-tuple-element.206, f32[2304]{0:T(1024)S(1)} %copy-done.47, bf16[1024,1152]{1,0:T(8,128)(2,1)S(1)} %copy-done.16, bf16[1152,2304]{1,0:T(8,128)(2,1)S(1)} %bitcast.144), kind=kOutput, calls=%fused_computation.12 | convolution fusion | flops 5499516928 | bytes 21841920 | tf_op jit(solution)/shard_map/dot_general | solution.py:1313
  317.9 8.9 %convolution_convert_fusion = bf16[1152,2304]{1,0:T(8,128)(2,1)S(1)} fusion(bf16[1024,2304]{1,0:T(8,128)(2,1)} %get-tuple-element.62, bf16[512,1152]{1,0:T(8,128)(2,1)S(1)} %copy-done.59, bf16[512,1152]{1,0:T(8,128)(2,1)S(1)} %copy-done.22), kind=kOutput, calls=%fused_computation.4 | convolution fusion | flops 5443190784 | bytes 12386304 | tf_op jit(solution)/shard_map/dot_general | solution.py:44
  333.5 9.8 %fusion.45 = f32[1024,1152]{1,0:T(8,128)S(1)} fusion(bf16[1024,2304]{1,0:T(8,128)(2,1)} %get-tuple-element.62, bf16[1152,2304]{1,0:T(8,128)(2,1)} %bitcast.163), kind=kOutput, calls=%fused_computation.214 | convolution fusion | flops 5435817984 | bytes 14745600 | tf_op jit(solution)/shard_map/dot_general | solution.py:44
  347.9 9.8 %fusion.46 = f32[1024,1152]{1,0:T(8,128)} fusion(bf16[1024,2304]{1,0:T(8,128)(2,1)} %get-tuple-element.63, bf16[1152,2304]{1,0:T(8,128)(2,1)S(1)} %bitcast.145), kind=kOutput, calls=%fused_computation.215 | convolution fusion | flops 5435817984 | bytes 14745600 | tf_op jit(solution)/shard_map/dot_general | solution.py:44
  360.7 11.3 %collective-permute-done.12 = bf16[4,64,2304]{2,1,0:T(8,128)(2,1)} collective-permute-done((bf16[4,64,2304]{2,1,0:T(8,128)(2,1)S(1)}, bf16[4,64,2304]{2,1,0:T(8,128)(2,1)}, u32[]{:S(2)}, u32[]{:S(2)}) %collective-permute-start.12) | collective-permute-done | bytes 1179680 | tf_op jit(solution)/shard_map/ppermute | solution.py:564
  373.7 4.7 multiply_reduce_fusion
  392.0 3.4 convolution_convert_fusion.4.refs_4_
  395.4 72.9 %attend_back.1 = (bf16[1024,1792]{1,0:T(8,128)(2,1)}, f32[144,1152]{1,0:T(8,128)}, f32[144,1152]{1,0:T(8,128)}) custom-call(bf16[8,1024,128]{2,1,0:T(8,128)(2,1)} %get-tuple-element.65.refs_0_, bf16[8,1024,128]{2,1,0:T(8,128)(2,1)} %get-tuple-element.66.refs_1_, bf16[8,1024,128]{2,1,0:T(8,128)(2,1)} %get-tuple-element.67.refs_2_, ...), custom_call_target="tpu_custom_call" | custom-call | tf_op jit(solution)/shard_map/attend_back/pallas_call | solution.py:1154
  468.3 7.3 %convolution_convert_fusion.2 = bf16[1152,1792]{1,0:T(8,128)(2,1)S(1)} fusion(bf16[1024,1792]{1,0:T(8,128)(2,1)} %get-tuple-element.75, bf16[512,1152]{1,0:T(8,128)(2,1)} %copy-done.20, bf16[512,1152]{1,0:T(8,128)(2,1)} %copy-done.19), kind=kOutput, calls=%fused_computation.14 | convolution fusion | flops 4234641408 | bytes 10158080 | tf_op jit(solution)/shard_map/dot_general | solution.py:44
  478.9 4.9 fusion.47
  491.1 15.7 %collective-permute-done.18 = bf16[4,2,64,896]{3,2,1,0:T(8,128)(2,1)S(1)} collective-permute-done((bf16[4,2,64,896]{3,2,1,0:T(8,128)(2,1)S(1)}, bf16[4,2,64,896]{3,2,1,0:T(8,128)(2,1)S(1)}, u32[]{:S(2)}, u32[]{:S(2)}) %collective-permute-start.18) | collective-permute-done | bytes 917536 | tf_op jit(solution)/shard_map/ppermute | solution.py:565
  516.4 4.9 multiply_add_fusion.2
  533.6 52.1 %scatter_last.1 = (f32[144,384]{1,0:T(8,128)}, f32[144,896]{1,0:T(8,128)}, f32[16,56,128]{2,1,0:T(8,128)}, f32[8,8,256]{2,1,0:T(8,128)}) custom-call(bf16[4,64,384]{2,1,0:T(8,128)(2,1)} %get-tuple-element.176.refs_0_, bf16[4,64,384]{2,1,0:T(8,128)(2,1)} %get-tuple-element.175.refs_1_, bf16[4,80,384]{2,1,0:T(8,128)(2,1)} %get-tuple-element.174.refs_2_, ...), custom_call_target="tpu_custom_call" | custom-call | tf_op jit(solution)/shard_map/scatter_last/pallas_call | solution.py:933
  (324 shorter events, 133.5 us)
Async XLA Ops:
  2.8 91.3 %collective-permute-start.1 = (f32[2048]{0:T(1024)}, f32[2048]{0:T(1024)}, u32[]{:S(2)}, u32[]{:S(2)}) collective-permute-start(f32[2048]{0:T(1024)} %select_maximum_fusion), channel_id=1, source_target_pairs={{0,2},{2,0},{1,3},{3,1},{4,6},{6,4},{5,7},{7,5},{8,10},{10,8},{9,1... | collective-permute-start | bytes 24584 | tf_op jit(solution)/shard_map/ppermute | solution.py:1246
  5.8 89.7 %collective-permute-start = (f32[512,1152]{1,0:T(8,128)}, f32[512,1152]{1,0:T(8,128)}, u32[]{:S(2)}, u32[]{:S(2)}) collective-permute-start(f32[512,1152]{1,0:T(8,128)} %param.15), channel_id=1, source_target_pairs={{0,1},{1,0},{2,3},{3,2},{4,5},{5,4},{6,7},{7,6},{8,9},{9,8},{10,11... | collective-permute-start | bytes 7077896 | tf_op jit(solution)/shard_map/ppermute | solution.py:1213
  76.1 175.1 %collective-permute-start.4 = (bf16[512,1152]{1,0:T(8,128)(2,1)S(1)}, bf16[512,1152]{1,0:T(8,128)(2,1)}, u32[]{:S(2)}, u32[]{:S(2)}) collective-permute-start(bf16[512,1152]{1,0:T(8,128)(2,1)S(1)} %multiply_convert_fusion.2), channel_id=1, source_target_pairs={{0,1},{1,0},{2,3},{3,2},{4,5},{5,4},{6,7},{7,6},{8,9},{9,8},{10,11... | collective-permute-start | bytes 3538952 | tf_op jit(solution)/shard_map/ppermute | solution.py:1213
  243.4 10.0 %collective-permute-start.2 = (bf16[512,1152]{1,0:T(8,128)(2,1)}, bf16[512,1152]{1,0:T(8,128)(2,1)}, u32[]{:S(2)}, u32[]{:S(2)}) collective-permute-start(bf16[512,1152]{1,0:T(8,128)(2,1)} %slice.469), channel_id=1, source_target_pairs={{0,1},{1,0},{2,3},{3,2},{4,5},{5,4},{6,7},{7,6},{8,9},{9,8},{10,11... | collective-permute-start | bytes 3538952 | tf_op jit(solution)/shard_map/ppermute | solution.py:1213
  256.8 5.3 collective-permute-start.3
  260.7 28.2 %collective-permute-start.6 = (bf16[4,2,64,1152]{3,2,1,0:T(8,128)(2,1)S(1)}, bf16[4,2,64,1152]{3,2,1,0:T(8,128)(2,1)S(1)}, u32[]{:S(2)}, u32[]{:S(2)}) collective-permute-start(bf16[4,2,64,1152]{3,2,1,0:T(8,128)(2,1)S(1)} %slice_select_fusion), channel_id=1, source_target_pairs={{0,2},{2,0},{1,3},{3,1},{4,6},{6,4},{5,7},{7,5},{8,10},{10,8},{9,1... | collective-permute-start | bytes 3538952 | tf_op jit(solution)/shard_map/ppermute | solution.py:1283
  261.5 34.2 %collective-permute-start.5 = (bf16[4,80,2304]{2,1,0:T(8,128)(2,1)S(1)}, bf16[4,80,2304]{2,1,0:T(8,128)(2,1)S(1)}, u32[]{:S(2)}, u32[]{:S(2)}) collective-permute-start(bf16[4,80,2304]{2,1,0:T(8,128)(2,1)S(1)} %dynamic-slice_bitcast_fusion), channel_id=1, source_target_pairs={{0,4},{4,0},{8,12},{12,8},{16,20},{20,16},{24,28},{28,24},{1,5},{5... | collective-permute-start | bytes 4423688 | tf_op jit(solution)/shard_map/ppermute | solution.py:1282
  296.0 33.4 %collective-permute-start.8 = (bf16[4,2,64,1152]{3,2,1,0:T(8,128)(2,1)}, bf16[4,2,64,1152]{3,2,1,0:T(8,128)(2,1)}, u32[]{:S(2)}, u32[]{:S(2)}) collective-permute-start(bf16[4,2,64,1152]{3,2,1,0:T(8,128)(2,1)} %broadcast_select_fusion.3), channel_id=1, source_target_pairs={{0,2},{2,0},{1,3},{3,1},{4,6},{6,4},{5,7},{7,5},{8,10},{10,8},{9,1... | collective-permute-start | bytes 3538952 | tf_op jit(solution)/shard_map/ppermute | solution.py:565
  297.5 33.1 %collective-permute-start.7 = (bf16[4,80,2304]{2,1,0:T(8,128)(2,1)S(1)}, bf16[4,80,2304]{2,1,0:T(8,128)(2,1)}, u32[]{:S(2)}, u32[]{:S(2)}) collective-permute-start(bf16[4,80,2304]{2,1,0:T(8,128)(2,1)S(1)} %dynamic-slice_bitcast_fusion.1), channel_id=1, source_target_pairs={{0,4},{4,0},{8,12},{12,8},{16,20},{20,16},{24,28},{28,24},{1,5},{5... | collective-permute-start | bytes 4423688 | tf_op jit(solution)/shard_map/ppermute | solution.py:564
  343.5 4.4 collective-permute-start.9
  343.6 28.5 %collective-permute-start.12 = (bf16[4,64,2304]{2,1,0:T(8,128)(2,1)S(1)}, bf16[4,64,2304]{2,1,0:T(8,128)(2,1)}, u32[]{:S(2)}, u32[]{:S(2)}) collective-permute-start(bf16[4,64,2304]{2,1,0:T(8,128)(2,1)S(1)} %copy-done.18), channel_id=1, source_target_pairs={{0,4},{4,0},{8,12},{12,8},{16,20},{20,16},{24,28},{28,24},{1,5},{5... | collective-permute-start | bytes 3538952 | tf_op jit(solution)/shard_map/ppermute | solution.py:564
  344.2 36.6 %collective-permute-start.13 = (bf16[4,2,80,1152]{3,2,1,0:T(8,128)(2,1)}, bf16[4,2,80,1152]{3,2,1,0:T(8,128)(2,1)}, u32[]{:S(2)}, u32[]{:S(2)}) collective-permute-start(bf16[4,2,80,1152]{3,2,1,0:T(8,128)(2,1)} %broadcast_select_fusion), channel_id=1, source_target_pairs={{0,2},{2,0},{1,3},{3,1},{4,6},{6,4},{5,7},{7,5},{8,10},{10,8},{9,1... | collective-permute-start | bytes 4423688 | tf_op jit(solution)/shard_map/ppermute | solution.py:565
  344.8 28.9 %slice-start.2 = ((s8[4718592]{0:T(1024)(128)(4,1)}), s8[524288]{0:T(1024)(128)(4,1)S(1)}, s32[]{:S(2)}) async-start(s8[4718592]{0:T(1024)(128)(4,1)} %bitcast.142), calls=%async_computation.2 | async-start | bytes 1048576
  347.9 25.8 %slice-start.3 = ((s8[4718592]{0:T(1024)(128)(4,1)}), s8[4194304]{0:T(1024)(128)(4,1)S(1)}, s32[]{:S(2)}) async-start(s8[4718592]{0:T(1024)(128)(4,1)} %bitcast.142), calls=%async_computation.3 | async-start | bytes 8388608
  359.4 14.2 %collective-permute-start.10 = (bf16[512,1152]{1,0:T(8,128)(2,1)S(1)}, bf16[512,1152]{1,0:T(8,128)(2,1)S(1)}, u32[]{:S(2)}, u32[]{:S(2)}) collective-permute-start(bf16[512,1152]{1,0:T(8,128)(2,1)S(1)} %slice.467), channel_id=1, source_target_pairs={{0,1},{1,0},{2,3},{3,2},{4,5},{5,4},{6,7},{7,6},{8,9},{9,8},{10,11... | collective-permute-start | bytes 3538952 | tf_op jit(solution)/shard_map/ppermute | solution.py:1213
  378.6 6.6 %collective-permute-start.11 = (bf16[512,1152]{1,0:T(8,128)(2,1)S(1)}, bf16[512,1152]{1,0:T(8,128)(2,1)S(1)}, u32[]{:S(2)}, u32[]{:S(2)}) collective-permute-start(bf16[512,1152]{1,0:T(8,128)(2,1)S(1)} %multiply_convert_fusion.1), channel_id=1, source_target_pairs={{0,1},{1,0},{2,3},{3,2},{4,5},{5,4},{6,7},{7,6},{8,9},{9,8},{10,11... | collective-permute-start | bytes 3538952 | tf_op jit(solution)/shard_map/ppermute | solution.py:1213
  475.9 12.7 %collective-permute-start.15 = (bf16[4,64,768]{2,1,0:T(8,128)(2,1)}, bf16[4,64,768]{2,1,0:T(8,128)(2,1)S(1)}, u32[]{:S(2)}, u32[]{:S(2)}) collective-permute-start(bf16[4,64,768]{2,1,0:T(8,128)(2,1)} %dynamic-slice_bitcast_fusion.10), channel_id=1, source_target_pairs={{0,4},{4,0},{8,12},{12,8},{16,20},{20,16},{24,28},{28,24},{1,5},{5... | collective-permute-start | bytes 1179656 | tf_op jit(solution)/shard_map/ppermute | solution.py:564
  476.4 13.7 %collective-permute-start.16 = (bf16[4,2,80,384]{3,2,1,0:T(8,128)(2,1)}, bf16[4,2,80,384]{3,2,1,0:T(8,128)(2,1)S(1)}, u32[]{:S(2)}, u32[]{:S(2)}) collective-permute-start(bf16[4,2,80,384]{3,2,1,0:T(8,128)(2,1)} %broadcast_select_fusion.11), channel_id=1, source_target_pairs={{0,2},{2,0},{1,3},{3,1},{4,6},{6,4},{5,7},{7,5},{8,10},{10,8},{9,1... | collective-permute-start | bytes 1474568 | tf_op jit(solution)/shard_map/ppermute | solution.py:565
  483.9 27.5 %copy-start.7 = (f32[1024,1152]{1,0:T(8,128)}, f32[1024,1152]{1,0:T(8,128)S(1)}, u32[]{:S(2)}) copy-start(f32[1024,1152]{1,0:T(8,128)S(1)} %fusion.47) | copy-start | bytes 14155780
  483.9 22.9 %collective-permute-start.18 = (bf16[4,2,64,896]{3,2,1,0:T(8,128)(2,1)S(1)}, bf16[4,2,64,896]{3,2,1,0:T(8,128)(2,1)S(1)}, u32[]{:S(2)}, u32[]{:S(2)}) collective-permute-start(bf16[4,2,64,896]{3,2,1,0:T(8,128)(2,1)S(1)} %broadcast_select_fusion.4), channel_id=1, source_target_pairs={{0,2},{2,0},{1,3},{3,1},{4,6},{6,4},{5,7},{7,5},{8,10},{10,8},{9,1... | collective-permute-start | bytes 2752520 | tf_op jit(solution)/shard_map/ppermute | solution.py:565
  485.4 24.6 %collective-permute-start.17 = (bf16[4,80,1792]{2,1,0:T(8,128)(2,1)S(1)}, bf16[4,80,1792]{2,1,0:T(8,128)(2,1)S(1)}, u32[]{:S(2)}, u32[]{:S(2)}) collective-permute-start(bf16[4,80,1792]{2,1,0:T(8,128)(2,1)S(1)} %dynamic-slice_bitcast_fusion.3), channel_id=1, source_target_pairs={{0,4},{4,0},{8,12},{12,8},{16,20},{20,16},{24,28},{28,24},{1,5},{5... | collective-permute-start | bytes 3440648 | tf_op jit(solution)/shard_map/ppermute | solution.py:564
  486.0 25.4 %collective-permute-start.14 = (bf16[512,1152]{1,0:T(8,128)(2,1)S(1)}, bf16[512,1152]{1,0:T(8,128)(2,1)S(1)}, u32[]{:S(2)}, u32[]{:S(2)}) collective-permute-start(bf16[512,1152]{1,0:T(8,128)(2,1)S(1)} %slice.466), channel_id=1, source_target_pairs={{0,1},{1,0},{2,3},{3,2},{4,5},{5,4},{6,7},{7,6},{8,9},{9,8},{10,11... | collective-permute-start | bytes 3538952 | tf_op jit(solution)/shard_map/ppermute | solution.py:1213
  516.4 4.9 collective-permute-start.19
  533.6 55.7 %copy-start.34 = (f32[2,1152]{1,0:T(2,128)S(1)}, f32[2,1152]{1,0:T(2,128)}, u32[]{:S(2)}) copy-start(f32[2,1152]{1,0:T(2,128)} %param.16) | copy-start | bytes 27652
  (62 other events, 346.6 us)
